TPU v7x, 32 devices: a whole 2x2x4 slice. The times are simulated.
32 devices in a mesh: ep: 8 (over z, y), fsdp: 4 (over x, core).
Axes of the slice: x: 2, y: 2, z: 4, core: 2. Of those that a mesh axis runs over, the one named last changes fastest.
Arguments:
- train_gate: float32 [64, 2048, 1024], P('ep', 'fsdp'), may hold values from -0.1875 to 0.1875
- other_gate: float32 [64, 2048, 1024], P('ep', 'fsdp'), may hold values from -0.125 to 0.125
- train_up: float32 [64, 2048, 1024], P('ep', 'fsdp'), may hold values from -0.1875 to 0.1875
- other_up: float32 [64, 2048, 1024], P('ep', 'fsdp'), may hold values from -0.125 to 0.125
- mix_share: float32 [64], P('ep'), may hold values from 0.2 to 0.8
- router_weight: float32 [2048, 64], P('fsdp', 'ep'), may hold values from -0.125 to 0.125
- router_gain: float32 [2048], P('fsdp'), may hold values from 0.25 to 1.75
Outputs:
- ready_gate: bfloat16 [64, 2048, 1024], P('ep')
- ready_up: bfloat16 [64, 2048, 1024], P('ep')
- scale_gate: float32 [64, 1024], P('ep')
- scale_up: float32 [64, 1024], P('ep')
- serve_router: bfloat16 [2048, 64], replicated
All inputs are finite; a program needn't handle non-finite values. Where the computation divides by a largest or mean magnitude, that divisor is 1e-20 or more.
Results may differ from a plain program's by a relative error of at most 0.001.
Values may be sent and summed in bfloat16 or wider, within the bound.
No kernel may reach another device: no remote copies, remote signals or barrier semaphores. Data moves between devices by JAX's collectives and lax.ppermute only.
A program may use at most 256 MiB of HBM per device.

v0:
```python
import jax
import jax.numpy as jnp
from jax import lax
from jax.sharding import PartitionSpec as P


def per_device(train_gate, other_gate, train_up, other_up, mix_share, router_weight, router_gain):
    latest_gate = (
        mix_share[:, None, None] * train_gate + (1.0 - mix_share[:, None, None]) * other_gate
    )
    latest_up = mix_share[:, None, None] * train_up + (1.0 - mix_share[:, None, None]) * other_up
    scale_gate, scale_up = lax.pmax(
        (jnp.max(jnp.abs(latest_gate), axis=1), jnp.max(jnp.abs(latest_up), axis=1)), "fsdp"
    )
    narrow_gate, narrow_up = (
        (latest_gate / jnp.expand_dims(scale_gate, 1)).astype(jnp.bfloat16),
        (latest_up / jnp.expand_dims(scale_up, 1)).astype(jnp.bfloat16),
    )
    ready_gate, ready_up = (
        lax.all_gather(narrow_gate, "fsdp", axis=1, tiled=True),
        lax.all_gather(narrow_up, "fsdp", axis=1, tiled=True),
    )
    part_router = (router_weight * router_gain[:, None]).astype(jnp.bfloat16)
    row_router = lax.all_gather(part_router, "fsdp", axis=0, tiled=True)
    serve_router = lax.all_gather(row_router, "ep", axis=1, tiled=True)
    return (ready_gate, ready_up, scale_gate, scale_up, serve_router)


def solution(mesh):
    placed = (
        P("ep", "fsdp", None),
        P("ep", "fsdp", None),
        P("ep", "fsdp", None),
        P("ep", "fsdp", None),
        P("ep"),
        P("fsdp", "ep"),
        P("fsdp"),
    )
    return jax.shard_map(
        per_device,
        mesh=mesh,
        in_specs=placed,
        out_specs=(P("ep", None, None), P("ep", None, None), P("ep", None), P("ep", None), P()),
        check_vma=False,
    )
```

profile of v0, /device:TPU:0, one launch (start us, length us, event | category | flops | bytes accessed | tf_op | source)
XLA Modules:
  0.0 555.3 jit_solution(14787650851884378681)
XLA Ops:
  7.2 0.0 all-reduce.3.cloned.1.call-start
  7.2 0.7 broadcast_subtract_fusion
  7.9 0.0 copy-start.3
  7.9 23.2 %abs_reduce_fusion = (f32[8,1024]{1,0:T(8,128)}, f32[8,1024]{1,0:T(8,128)}) fusion(f32[8,512,1024]{2,1,0:T(8,128)} %param.10, f32[8]{0:T(128)S(1)} %broadcast_subtract_fusion, f32[8,512,1024]{2,1,0:T(8,128)} %param.9, f32[8]{0:T(128)} %param.11, f32[8,512,1024]{2,1,0:T(8,128)} %param.8, f32[8,512,1024]{2,1,0:T(8,128)} %param.7), kind=kLoop, calls=%fused_computation.1 | loop fusion | flops 41926656 | bytes 67174464 | tf_op jit(solution)/shard_map/reduce_max | solution.py:13
  31.1 0.0 all-reduce.3.cloned.1.call-update
  31.1 0.0 all-gather.3.cloned.1.call-start
  31.2 34.4 %all-reduce.3.cloned.1.call-done = (f32[8,1024]{1,0:T(8,128)}, f32[8,1024]{1,0:T(8,128)}) async-done(((f32[8,1024]{1,0:T(8,128)}, f32[8,1024]{1,0:T(8,128)}), (f32[8,1024]{1,0:T(8,128)}, f32[8,1024]{1,0:T(8,128)})) %all-reduce.3.cloned.1.call-update) | async-done | bytes 65552 | tf_op jit(solution)/shard_map/pmax | solution.py:12
  65.6 0.0 copy-done.3
  65.6 29.4 %divide_convert_fusion = (bf16[8,512,1024]{2,1,0:T(8,128)(2,1)}, bf16[8,512,1024]{2,1,0:T(8,128)(2,1)}) fusion(f32[8,1024]{1,0:T(8,128)} %get-tuple-element.19, f32[8,512,1024]{2,1,0:T(8,128)} %param.10, f32[8]{0:T(128)S(1)} %broadcast_subtract_fusion, f32[8,512,1024]{2,1,0:T(8,128)} %param.9, f32[8]{0:T(128)S(1)} %copy-done.3, ...), kind=kLoop, calls=%fused_computation | loop fusion | flops 41943040 | bytes 83951680 | tf_op jit(solution)/shard_map/convert_element_type | solution.py:17
  95.0 0.0 copy-start.2
  95.0 0.0 copy-start.4
  95.0 0.0 all-gather.3.cloned.1.call-update
  95.0 0.0 all-gather.5.cloned.1.call-start
  95.0 0.7 all-gather.5.cloned.1.call-update
  95.7 0.0 copy-done.2
  95.7 0.0 copy-done.4
  95.8 5.2 all_gather.14
  101.0 30.9 %all_gather.15 = bf16[2048,64]{0,1:T(8,128)(2,1)S(1)} all-gather(bf16[2048,8]{0,1:T(8,128)(2,1)S(1)} %all_gather.14), channel_id=1, replica_groups=mesh['ep'=8,'fsdp'=4] {'ep'}, dimensions={1}, use_global_device_ids=true | all-gather | bytes 294912 | tf_op jit(solution)/shard_map/all_gather | solution.py:25
  131.8 164.8 %all-gather.3.cloned.1.call-done = bf16[8,2048,1024]{2,1,0:T(8,128)(2,1)} async-done(((bf16[8,512,1024]{2,1,0:T(8,128)(2,1)}), bf16[8,2048,1024]{2,1,0:T(8,128)(2,1)}) %all-gather.3.cloned.1.call-update) | async-done | bytes 33554448 | tf_op jit(solution)/shard_map/all_gather | solution.py:20
  296.7 203.7 %all-gather.5.cloned.1.call-done = bf16[8,2048,1024]{2,1,0:T(8,128)(2,1)} async-done(((bf16[8,512,1024]{2,1,0:T(8,128)(2,1)}), bf16[8,2048,1024]{2,1,0:T(8,128)(2,1)}) %all-gather.5.cloned.1.call-update) | async-done | bytes 33554448 | tf_op jit(solution)/shard_map/all_gather | solution.py:21
  500.4 23.2 %copy.17 = bf16[8,2048,1024]{2,1,0:T(8,128)(2,1)} copy(bf16[8,2048,1024]{2,1,0:T(8,128)(2,1)} %all-gather.3.cloned.1.call-done) | data formatting | bytes 67108864
  523.6 0.0 copy-start.1
  523.6 0.0 copy-start
  523.6 23.2 %copy.18 = bf16[8,2048,1024]{2,1,0:T(8,128)(2,1)} copy(bf16[8,2048,1024]{2,1,0:T(8,128)(2,1)} %all-gather.5.cloned.1.call-done) | data formatting | bytes 67108864
  546.8 0.0 copy-done.1
  546.8 0.6 copy.19
  547.4 0.0 copy-done
  547.5 0.6 copy.20
  548.1 0.7 copy.21
  (1 shorter events, 0.0 us)
Async XLA Ops:
  7.2 58.4 %all-reduce.3.cloned.1.call-start = ((), (), s32[]{:S(2)}) async-start(), calls=%async_computation.2 | async-start | bytes 131072 | tf_op jit(solution)/shard_map/pmax | solution.py:12
  7.9 57.7 %copy-start.3 = (f32[8]{0:T(128)S(1)}, f32[8]{0:T(128)}, u32[]{:S(2)}) copy-start(f32[8]{0:T(128)} %param.11) | copy-start | bytes 100
  31.1 265.5 %all-gather.3.cloned.1.call-start = ((), (), s32[]{:S(2)}) async-start(), calls=%async_computation | async-start | bytes 41943040 | tf_op jit(solution)/shard_map/all_gather | solution.py:20
  95.0 0.8 copy-start.2
  95.0 0.8 copy-start.4
  95.0 405.4 %all-gather.5.cloned.1.call-start = ((), (), s32[]{:S(2)}) async-start(), calls=%async_computation.1 | async-start | bytes 41943040 | tf_op jit(solution)/shard_map/all_gather | solution.py:21
  523.6 23.3 %copy-start.1 = (f32[8,1024]{1,0:T(8,128)S(1)}, f32[8,1024]{1,0:T(8,128)}, u32[]{:S(2)}) copy-start(f32[8,1024]{1,0:T(8,128)} %get-tuple-element.18) | copy-start | bytes 98308
  523.6 23.9 %copy-start = (f32[8,1024]{1,0:T(8,128)S(1)}, f32[8,1024]{1,0:T(8,128)}, u32[]{:S(2)}) copy-start(f32[8,1024]{1,0:T(8,128)} %get-tuple-element.19) | copy-start | bytes 98308
Sparse Core Ops, SparseCore 0:
  31.2 34.2 all-reduce.2
  95.1 201.4 all-gather.2
  298.8 201.4 all-gather.4
where the time goes:
time: 556 us; the launch traced here: 555 us
  waiting for transfers between devices  404 us (73%)
  other arithmetic  53.3 us (10%)
  local copies, waits for them, and re-layouts  48.4 us (9%)
  blocking collectives  36.1 us (6%)
  between operations  13.8 us (2%)
    all_gather x1, waiting for transfers between devices, per_device(): lax.all_gather(narrow_up, 'fsdp', axis=1, tiled=True)  204 us
    all_gather x1, waiting for transfers between devices, per_device(): lax.all_gather(narrow_gate, 'fsdp', axis=1, tiled=True)  165 us
    unnamed x15, local copies, waits for them, and re-layouts  48.4 us
    pmax x1, waiting for transfers between devices, per_device(): lax.pmax((jnp.max(jnp.abs(latest_gate), axis=1), jnp.max(jnp.abs(latest_u...  34.4 us
    all_gather x1, blocking collectives, per_device(): serve_router = lax.all_gather(row_router, 'ep', axis=1, tiled=True)  30.9 us
    convert_element_type x1, other arithmetic, per_device(): (latest_up / jnp.expand_dims(scale_up, 1)).astype(jnp.bfloat16)  29.4 us
    reduce_max x1, other arithmetic, per_device(): jnp.max(jnp.abs(latest_up), axis=1)  23.2 us
  transfers between devices with their start and end apart: 3, of which 3 were waited for; matrix products, arithmetic and copies ran while one was open for 0% of the time, Pallas kernels for 0%

commit v1 on v0

v1 whole, which is shorter than its diff:
```python
import functools

import jax
import jax.numpy as jnp
from jax import lax
from jax.experimental import pallas as pl
from jax.experimental.pallas import tpu as pltpu
from jax.sharding import PartitionSpec as P


ANY = pl.BlockSpec(memory_space=pl.ANY)
SMEM = pl.BlockSpec(memory_space=pltpu.SMEM)
SUB = 8


def rows_per_step(rows, most):
    return max(d for d in range(16, min(rows, most) + 1, 16) if rows % d == 0)


def mixed(share, train, other):
    return share * train + (1.0 - share) * other


def max_kernel(first, steps, mix_ref, train_ref, other_ref, top_ref, held):
    share = mix_ref[first + pl.program_id(0)]
    r = pl.program_id(1)

    def magnitude(i):
        rows = pl.ds(i * SUB, SUB)
        return jnp.abs(mixed(share, train_ref[0, rows], other_ref[0, rows]))

    top = magnitude(0)
    for i in range(1, train_ref.shape[1] // SUB):
        top = jnp.maximum(top, magnitude(i))
    if steps > 1:
        top = jnp.where(r == 0, top, jnp.maximum(top, held[...]))
        held[...] = top

    @pl.when(r == steps - 1)
    def _():
        top_ref[0] = jnp.max(top, axis=0, keepdims=True)


def local_max(mix_share, train, other, first, count):
    _, rows, cols = train.shape
    step = rows_per_step(rows, 128 if count == 1 else 256)
    block = pl.BlockSpec((1, step, cols), lambda e, r: (first + e, r, 0))
    return pl.pallas_call(
        functools.partial(max_kernel, first, rows // step),
        out_shape=jax.ShapeDtypeStruct((count, 1, cols), jnp.float32),
        grid=(count, rows // step),
        in_specs=[SMEM, block, block],
        out_specs=pl.BlockSpec((1, 1, cols), lambda e, r: (e, 0, 0)),
        scratch_shapes=[pltpu.VMEM((SUB, cols), jnp.float32)],
        cost_estimate=pl.CostEstimate(
            flops=5 * count * rows * cols, bytes_accessed=8 * count * rows * cols, transcendentals=0
        ),
        name="local_max",
    )(mix_share, train, other)


def narrow_kernel(first, tops, place_ref, mix_ref, *refs):
    top_refs, (train_ref, other_ref), (send_ref, whole_ref) = refs[:tops], refs[tops : tops + 2], refs[-2:]
    top = top_refs[0][0]
    for ref in top_refs[1:]:
        top = jnp.maximum(top, ref[0])
    scale = jnp.broadcast_to(1.0 / top, (2 * SUB, top.shape[1]))
    share = mix_ref[first + pl.program_id(0)]
    for i in range(train_ref.shape[1] // (2 * SUB)):
        rows = pl.ds(i * 2 * SUB, 2 * SUB)
        part = (mixed(share, train_ref[0, rows], other_ref[0, rows]) * scale).astype(jnp.bfloat16)
        send_ref[0, rows] = part
        whole_ref[0, rows] = part


def narrow(place, mix_share, tops, at, train, other, piece, parts, whole):
    first, count, low, height = piece
    experts, rows, cols = train.shape
    step = rows_per_step(height, 128 if count == 1 else 256)
    block = pl.BlockSpec((1, step, cols), lambda e, r, place: (first + e, low // step + r, 0))
    held = [] if whole is None else [whole]
    return pl.pallas_call(
        functools.partial(narrow_kernel, first, len(tops)),
        out_shape=(
            jax.ShapeDtypeStruct((count, height, cols), jnp.bfloat16),
            jax.ShapeDtypeStruct((experts, parts * rows, cols), jnp.bfloat16),
        ),
        grid_spec=pltpu.PrefetchScalarGridSpec(
            num_scalar_prefetch=1,
            grid=(count, height // step),
            in_specs=[SMEM]
            + [pl.BlockSpec((1, 1, cols), lambda e, r, place: (at + e, 0, 0))] * len(tops)
            + [block, block]
            + [ANY] * len(held),
            out_specs=(
                pl.BlockSpec((1, step, cols), lambda e, r, place: (e, r, 0)),
                pl.BlockSpec(
                    (1, step, cols),
                    lambda e, r, place: (first + e, place[0] * (rows // step) + low // step + r, 0),
                ),
            ),
        ),
        input_output_aliases={4 + len(tops): 1} if held else {},
        cost_estimate=pl.CostEstimate(
            flops=6 * count * height * cols, bytes_accessed=12 * count * height * cols, transcendentals=0
        ),
        name="narrow",
    )(place, mix_share, *tops, train, other, *held)


def put_kernel(sources, place_ref, *refs):
    for k in range(sources):

        @pl.when(pl.program_id(0) == k)
        def _():
            refs[-1][...] = refs[k][...]


def put(place, arrays, slots, piece, rows, whole):
    first, count, low, height = piece
    cols = whole.shape[2]

    def source(k):
        return pl.BlockSpec(
            (1, height, cols),
            lambda s, e, place: (jnp.where(s < k, 0, jnp.where(s > k, count - 1, e)), 0, 0),
        )

    def target(s, e, place):
        slot = place[slots[0]]
        for k in range(1, len(slots)):
            slot = jnp.where(s == k, place[slots[k]], slot)
        return (first + e, slot * (rows // height) + low // height, 0)

    size = len(arrays) * count * height * cols
    return pl.pallas_call(
        functools.partial(put_kernel, len(arrays)),
        out_shape=jax.ShapeDtypeStruct(whole.shape, whole.dtype),
        grid_spec=pltpu.PrefetchScalarGridSpec(
            num_scalar_prefetch=1,
            grid=(len(arrays), count),
            in_specs=[source(k) for k in range(len(arrays))] + [ANY],
            out_specs=pl.BlockSpec((1, height, cols), target),
        ),
        input_output_aliases={1 + len(arrays): 0},
        cost_estimate=pl.CostEstimate(flops=size, bytes_accessed=4 * size, transcendentals=0),
        name="put",
    )(place, *arrays, whole)


def plan(experts, rows):
    half = rows // 2
    split = [(0, half), (half, rows - half)]

    def runs(lo, hi, most):
        return [(e, min(most, hi - e)) for e in range(lo, hi, most)]

    groups = [(0, 0, 1)]
    groups += [(0, e, n) for e, n in runs(1, min(3, experts), 2)]
    groups += [(0, e, n) for e, n in runs(3, experts, experts)]
    groups += [(1, 0, experts)]
    pieces = [(0, (0, 1, low, height)) for low, height in split]
    pieces += [(0, (e, n, 0, rows)) for e, n in runs(1, min(3, experts), 1)]
    pieces += [(0, (e, n, 0, rows)) for e, n in runs(3, experts, 3)]
    tail = max(experts - 2, 0)
    pieces += [(1, (e, n, 0, rows)) for e, n in runs(0, tail, 3)]
    pieces += [(1, (e, n, 0, rows)) for e, n in runs(tail, experts - 1, 1)]
    pieces += [(1, (experts - 1, 1, low, height)) for low, height in split]
    return groups, pieces


def group_of(groups, array, expert):
    return next(g for g, (a, e, n) in enumerate(groups) if a == array and e <= expert < e + n)


def per_device(parts, train_gate, other_gate, train_up, other_up, mix_share, router_weight, router_gain):
    experts, rows, _ = train_gate.shape
    inner = 2 if parts % 2 == 0 else 1
    outer = parts // inner
    me = lax.axis_index("fsdp")
    power = parts & (parts - 1) == 0
    groups, pieces = plan(experts, rows)

    def step(k, l):
        return [(i, (i // inner + k) % outer * inner + (i % inner ^ l)) for i in range(parts)]

    def send(x, k, l):
        return lax.ppermute(x, "fsdp", step(k, l))

    def partner(s):
        return [(i, i ^ s if power else (i + s) % parts) for i in range(parts)]

    steps = [[dict((b, a) for a, b in step(k, l)) for l in range(inner)] for k in range(outer)]
    table = [[steps[k][l][i] for k in range(outer) for l in range(inner)] for i in range(parts)]
    place = jnp.asarray(table, jnp.int32)[me]

    train, other = (train_gate, train_up), (other_gate, other_up)
    tops = []
    for g, (a, first, count) in enumerate(groups):
        top = [local_max(mix_share, train[a], other[a], first, count)]
        for s in range(1, parts):
            top.append(lax.ppermute(top[0], "fsdp", partner(s)))
        tops.append(top)

    whole = [None, None]
    sent = []
    for a, piece in pieces:
        g = group_of(groups, a, piece[0])
        own, whole[a] = narrow(
            place, mix_share, tops[g], piece[0] - groups[g][1], train[a], other[a], piece, parts, whole[a]
        )
        sent.append(own)

    for i, (a, piece) in enumerate(pieces):
        arrays, slots = [], []
        if inner == 2:
            arrays.append(send(sent[i], 0, 1))
            slots.append(1)
        for k in range(1, outer):
            far = send(sent[i], k, 0)
            arrays.append(far)
            slots.append(inner * k)
            if inner == 2:
                arrays.append(send(far, 0, 1))
                slots.append(inner * k + 1)
        if not arrays:
            continue
        cut = len(arrays) - 1 if inner == 2 and i + 1 == len(pieces) else 0
        if cut:
            whole[a] = put(place, arrays[:cut], slots[:cut], piece, rows, whole[a])
        whole[a] = put(place, arrays[cut:], slots[cut:], piece, rows, whole[a])

    scales = [
        jnp.concatenate(
            [functools.reduce(jnp.maximum, top)[:, 0] for top, (b, _, _) in zip(tops, groups) if b == a], axis=0
        )
        for a in range(2)
    ]
    part_router = (router_weight * router_gain[:, None]).astype(jnp.bfloat16)
    wide = lax.all_gather(part_router, "ep", axis=1, tiled=True)
    serve_router = jnp.zeros((parts * rows, wide.shape[1]), wide.dtype)
    serve_router = lax.dynamic_update_slice(serve_router, wide, (me * rows, 0))
    for s in range(1, parts):
        piece = lax.ppermute(wide, "fsdp", partner(s))
        source = jnp.asarray([dict((b, a) for a, b in partner(s))[i] for i in range(parts)], jnp.int32)[me]
        serve_router = lax.dynamic_update_slice(serve_router, piece, (source * rows, 0))
    return whole[0], whole[1], scales[0], scales[1], serve_router


def solution(mesh):
    parts = mesh.shape["fsdp"]
    placed = (
        P("ep", "fsdp", None),
        P("ep", "fsdp", None),
        P("ep", "fsdp", None),
        P("ep", "fsdp", None),
        P("ep"),
        P("fsdp", "ep"),
        P("fsdp"),
    )
    return jax.shard_map(
        functools.partial(per_device, parts),
        mesh=mesh,
        in_specs=placed,
        out_specs=(P("ep", None, None), P("ep", None, None), P("ep", None), P("ep", None), P()),
        check_vma=False,
    )
```

time: 556 us -> 556 us (level)
  Pallas kernels: 0 us -> 168 us
  waiting for transfers between devices: 404 us -> 312 us
  other arithmetic: 53.3 us -> 0.72 us
  local copies, waits for them, and re-layouts: 48.4 us -> 13.5 us
  starting transfers between devices: 0.12 us -> 26.1 us
  between operations: 13.8 us -> 3.08 us
    all_gather x2 -> x0, waiting for transfers between devices: 369 us -> none  [the longest x1 204 us: per_device(): lax.all_gather(narrow_up, 'fsdp', axis=1, tiled=True)]
    ppermute x0 -> x48, waiting for transfers between devices: none -> 312 us  [the longest x33 308 us: send(): return lax.ppermute(x, 'fsdp', step(k, l))]
    pallas_call x0 -> x27, Pallas kernels: none -> 168 us  [the longest x12 71.1 us: put(): pl.pallas_call(functools.partial(put_kernel, len(arrays)), out_shape=jax....]
    unnamed x15 -> x90, local copies, waits for them, and re-layouts: 48.4 us -> 3 us
    pmax x1 -> x0, waiting for transfers between devices: 34.4 us -> none  [per_device(): lax.pmax((jnp.max(jnp.abs(latest_gate), axis=1), jnp.max(jnp.abs(latest_u...]
    convert_element_type x1 -> x0, other arithmetic: 29.4 us -> none  [per_device(): (latest_up / jnp.expand_dims(scale_up, 1)).astype(jnp.bfloat16)]
    ppermute x0 -> x48, starting transfers between devices: none -> 26.1 us  [the longest x33 15.6 us: send(): return lax.ppermute(x, 'fsdp', step(k, l))]
    reduce_max x1 -> x0, other arithmetic: 23.2 us -> none  [per_device(): jnp.max(jnp.abs(latest_up), axis=1)]
  transfers between devices with their start and end apart: 3 -> 48, of which waited for: 3 -> 14; matrix products, arithmetic and copies ran while one was open for 0% -> 2% of each run, Pallas kernels for 0% -> 29%
where the time goes in v1:
time: 556 us; the launch traced here: 554 us
  waiting for transfers between devices  312 us (56%)
  Pallas kernels  168 us (30%)
  blocking collectives  30.9 us (6%)
  starting transfers between devices  26.1 us (5%)
  local copies, waits for them, and re-layouts  13.5 us (2%)
    ppermute x33, waiting for transfers between devices, send(): return lax.ppermute(x, 'fsdp', step(k, l))  308 us
    pallas_call x12, Pallas kernels, put(): pl.pallas_call(functools.partial(put_kernel, len(arrays)), out_shape=jax....  71.1 us
    pallas_call x11, Pallas kernels, narrow(): pl.pallas_call(functools.partial(narrow_kernel, first, len(tops)), out_sh...  61.8 us
    pallas_call x4, Pallas kernels, local_max(): pl.pallas_call(functools.partial(max_kernel, first, rows // step), out_sh...  35.1 us
    all_gather x1, blocking collectives, per_device(): wide = lax.all_gather(part_router, 'ep', axis=1, tiled=True)  30.9 us
    ppermute x33, starting transfers between devices, send(): return lax.ppermute(x, 'fsdp', step(k, l))  15.6 us
  transfers between devices with their start and end apart: 48, of which 14 were waited for; matrix products, arithmetic and copies ran while one was open for 2% of the time, Pallas kernels for 29%

profile of v1, /device:TPU:0, one launch (start us, length us, event | category | flops | bytes accessed | tf_op | source)
XLA Modules:
  0.0 553.8 jit_solution(10516077024899159209)
XLA Ops:
  0.6 3.6 local_max.6.refs_0_
  4.7 2.5 collective-permute-start.7
  7.3 1.3 fusion.place_ref
  9.0 1.4 collective-permute-done.8.refs_3_
  11.0 3.1 narrow.11
  15.3 4.8 local_max.5.refs_0_
  22.8 16.2 %local_max.7.refs_0_ = f32[8,1,1024]{2,1,0:T(1,128)} custom-call(f32[8]{0:T(128)} %mix_ref.29, f32[8,512,1024]{2,1,0:T(8,128)} %refs_4_.21, f32[8,512,1024]{2,1,0:T(8,128)} %refs_5_.21), custom_call_target="tpu_custom_call" | custom-call | flops 20971520 | bytes 33554432 | tf_op jit(solution)/shard_map/local_max/pallas_call | solution.py:48
  39.3 10.5 %local_max.4.refs_0_ = f32[5,1,1024]{2,1,0:T(1,128)} custom-call(f32[8]{0:T(128)} %mix_ref.29, f32[8,512,1024]{2,1,0:T(8,128)} %refs_4_.16, f32[8,512,1024]{2,1,0:T(8,128)} %refs_5_.16), custom_call_target="tpu_custom_call" | custom-call | flops 13107200 | bytes 20971520 | tf_op jit(solution)/shard_map/local_max/pallas_call | solution.py:48
  50.8 1.2 collective-permute-start.1
  53.1 1.7 collective-permute-done.1.refs_2_
  54.9 30.9 %all_gather.3 = bf16[512,64]{0,1:T(8,128)(2,1)S(1)} all-gather(bf16[512,8]{0,1:T(8,128)(2,1)S(1)} %multiply_convert_fusion), channel_id=1, replica_groups=mesh['ep'=8,'fsdp'=4] {'ep'}, dimensions={1}, use_global_device_ids=true | all-gather | bytes 73728 | tf_op jit(solution)/shard_map/all_gather | solution.py:240
  85.9 1.2 collective-permute-start.46
  88.2 3.1 narrow.12
  91.3 9.2 %narrow.17 = (bf16[3,512,1024]{2,1,0:T(8,128)(2,1)}, bf16[8,2048,1024]{2,1,0:T(8,128)(2,1)}) custom-call(s32[4]{0:T(128)} %fusion.place_ref, f32[8]{0:T(128)} %mix_ref.29, f32[8,1,1024]{2,1,0:T(1,128)} %local_max.7.refs_0_, f32[8,1,1024]{2,1,0:T(1,128)} %copy-done.4, f32[8,1,1024]{2,1,0:T(1,128)} %copy-done.6, f32[8,1,1024]{2,1,0:T(1,128)} %copy-done.8, ...), custom_call_target="tpu_custom_call" | custom-call | flops 9437184 | bytes 18874368 | tf_op jit(solution)/shard_map/narrow/pallas_call | solution.py:82
  100.6 9.2 %narrow.18 = (bf16[3,512,1024]{2,1,0:T(8,128)(2,1)}, bf16[8,2048,1024]{2,1,0:T(8,128)(2,1)}) custom-call(s32[4]{0:T(128)} %fusion.place_ref, f32[8]{0:T(128)} %mix_ref.29, f32[8,1,1024]{2,1,0:T(1,128)} %local_max.7.refs_0_, f32[8,1,1024]{2,1,0:T(1,128)} %copy-done.4, f32[8,1,1024]{2,1,0:T(1,128)} %copy-done.6, ...), custom_call_target="tpu_custom_call", output_to_operand_aliasing={{1}: (8, {})} | custom-call | flops 9437184 | bytes 18874368 | tf_op jit(solution)/shard_map/narrow/pallas_call | solution.py:82
  109.8 4.9 narrow.19
  114.8 1.2 collective-permute-start.22
  116.0 3.1 narrow.20
  122.5 4.9 narrow.13
  127.5 1.2 collective-permute-start.19
  128.7 3.1 narrow.21
  133.1 8.0 %collective-permute-done.34.refs_1_ = bf16[1,256,1024]{2,1,0:T(8,128)(2,1)S(1)} collective-permute-done((bf16[1,256,1024]{2,1,0:T(8,128)(2,1)}, bf16[1,256,1024]{2,1,0:T(8,128)(2,1)S(1)}, u32[]{:S(2)}, u32[]{:S(2)}) %collective-permute-start.34) | collective-permute-done | bytes 524320 | tf_op jit(solution)/shard_map/ppermute | solution.py:188
  141.1 4.9 narrow.14
  146.0 9.2 %narrow.15 = (bf16[3,512,1024]{2,1,0:T(8,128)(2,1)}, bf16[8,2048,1024]{2,1,0:T(8,128)(2,1)}) custom-call(s32[4]{0:T(128)} %fusion.place_ref, f32[8]{0:T(128)} %mix_ref.29, f32[5,1,1024]{2,1,0:T(1,128)} %local_max.4.refs_0_, f32[5,1,1024]{2,1,0:T(1,128)} %copy-done.23, f32[5,1,1024]{2,1,0:T(1,128)} %copy-done.25, ...), custom_call_target="tpu_custom_call", output_to_operand_aliasing={{1}: (8, {})} | custom-call | flops 9437184 | bytes 18874368 | tf_op jit(solution)/shard_map/narrow/pallas_call | solution.py:82
  155.3 18.8 %collective-permute-done.30.refs_1_ = bf16[1,256,1024]{2,1,0:T(8,128)(2,1)} collective-permute-done((bf16[1,256,1024]{2,1,0:T(8,128)(2,1)}, bf16[1,256,1024]{2,1,0:T(8,128)(2,1)}, u32[]{:S(2)}, u32[]{:S(2)}) %collective-permute-start.30) | collective-permute-done | bytes 524320 | tf_op jit(solution)/shard_map/ppermute | solution.py:188
  176.3 6.8 %narrow.16 = (bf16[2,512,1024]{2,1,0:T(8,128)(2,1)}, bf16[8,2048,1024]{2,1,0:T(8,128)(2,1)}) custom-call(s32[4]{0:T(128)} %fusion.place_ref, f32[8]{0:T(128)} %mix_ref.29, f32[5,1,1024]{2,1,0:T(1,128)} %local_max.4.refs_0_, f32[5,1,1024]{2,1,0:T(1,128)} %copy-done.23, f32[5,1,1024]{2,1,0:T(1,128)} %copy-done.25, ...), custom_call_target="tpu_custom_call", output_to_operand_aliasing={{1}: (8, {})} | custom-call | flops 6291456 | bytes 12582912 | tf_op jit(solution)/shard_map/narrow/pallas_call | solution.py:82
  183.1 1.2 collective-permute-start.10
  184.3 16.1 %collective-permute-done.16.refs_1_ = bf16[1,512,1024]{2,1,0:T(8,128)(2,1)} collective-permute-done((bf16[1,512,1024]{2,1,0:T(8,128)(2,1)}, bf16[1,512,1024]{2,1,0:T(8,128)(2,1)}, u32[]{:S(2)}, u32[]{:S(2)}) %collective-permute-start.16) | collective-permute-done | bytes 1048608 | tf_op jit(solution)/shard_map/ppermute | solution.py:188
  200.9 21.8 %collective-permute-done.37.refs_1_ = bf16[1,512,1024]{2,1,0:T(8,128)(2,1)S(1)} collective-permute-done((bf16[1,512,1024]{2,1,0:T(8,128)(2,1)}, bf16[1,512,1024]{2,1,0:T(8,128)(2,1)S(1)}, u32[]{:S(2)}, u32[]{:S(2)}) %collective-permute-start.37) | collective-permute-done | bytes 1048608 | tf_op jit(solution)/shard_map/ppermute | solution.py:188
  226.8 41.0 %collective-permute-done.10.refs_1_ = bf16[2,512,1024]{2,1,0:T(8,128)(2,1)} collective-permute-done((bf16[2,512,1024]{2,1,0:T(8,128)(2,1)}, bf16[2,512,1024]{2,1,0:T(8,128)(2,1)}, u32[]{:S(2)}, u32[]{:S(2)}) %collective-permute-start.10) | collective-permute-done | bytes 2097184 | tf_op jit(solution)/shard_map/ppermute | solution.py:188
  269.0 66.1 %collective-permute-done.13.refs_1_ = bf16[3,512,1024]{2,1,0:T(8,128)(2,1)S(1)} collective-permute-done((bf16[3,512,1024]{2,1,0:T(8,128)(2,1)}, bf16[3,512,1024]{2,1,0:T(8,128)(2,1)S(1)}, u32[]{:S(2)}, u32[]{:S(2)}) %collective-permute-start.13) | collective-permute-done | bytes 3145760 | tf_op jit(solution)/shard_map/ppermute | solution.py:188
  335.7 66.9 %collective-permute-done.43.refs_1_ = bf16[3,512,1024]{2,1,0:T(8,128)(2,1)} collective-permute-done((bf16[3,512,1024]{2,1,0:T(8,128)(2,1)}, bf16[3,512,1024]{2,1,0:T(8,128)(2,1)}, u32[]{:S(2)}, u32[]{:S(2)}) %collective-permute-start.43) | collective-permute-done | bytes 3145760 | tf_op jit(solution)/shard_map/ppermute | solution.py:188
  402.6 65.7 %collective-permute-done.40.refs_1_ = bf16[3,512,1024]{2,1,0:T(8,128)(2,1)} collective-permute-done((bf16[3,512,1024]{2,1,0:T(8,128)(2,1)}, bf16[3,512,1024]{2,1,0:T(8,128)(2,1)}, u32[]{:S(2)}, u32[]{:S(2)}) %collective-permute-start.40) | collective-permute-done | bytes 3145760 | tf_op jit(solution)/shard_map/ppermute | solution.py:188
  474.9 2.5 collective-permute-done.11.refs_2_
  479.7 1.5 constant_dynamic-update-slice_fusion.1
  481.2 1.5 constant_dynamic-update-slice_fusion
  482.6 3.7 put.12.refs_3_
  486.3 3.7 put.13.refs_3_
  490.0 4.6 put.14.refs_3_
  494.7 4.6 put.15.refs_3_
  499.3 10.8 %put.16.refs_3_ = bf16[8,2048,1024]{2,1,0:T(8,128)(2,1)} custom-call(s32[4]{0:T(128)} %fusion.place_ref, bf16[3,512,1024]{2,1,0:T(8,128)(2,1)} %collective-permute-done.12.refs_0_, bf16[3,512,1024]{2,1,0:T(8,128)(2,1)} %copy-done, bf16[3,512,1024]{2,1,0:T(8,128)(2,1)} %collective-permute-done.14.refs_2_, ...), custom_call_target="tpu_custom_call", output_to_operand_aliasing={{}: (4, {})} | custom-call | flops 4718592 | bytes 18874368 | tf_op jit(solution)/shard_map/put/pallas_call | solution.py:136
  510.1 8.3 %put.17 = bf16[8,2048,1024]{2,1,0:T(8,128)(2,1)} custom-call(s32[4]{0:T(128)} %fusion.place_ref, bf16[2,512,1024]{2,1,0:T(8,128)(2,1)} %copy-done.1, bf16[2,512,1024]{2,1,0:T(8,128)(2,1)} %collective-permute-done.10.refs_1_, bf16[2,512,1024]{2,1,0:T(8,128)(2,1)} %collective-permute-done.11.refs_2_, ...), custom_call_target="tpu_custom_call", output_to_operand_aliasing={{}: (4, {})} | custom-call | flops 3145728 | bytes 12582912 | tf_op jit(solution)/shard_map/put/pallas_call | solution.py:136
  518.4 10.8 %put.18.refs_3_ = bf16[8,2048,1024]{2,1,0:T(8,128)(2,1)} custom-call(s32[4]{0:T(128)} %fusion.place_ref, bf16[3,512,1024]{2,1,0:T(8,128)(2,1)} %collective-permute-done.42.refs_0_, bf16[3,512,1024]{2,1,0:T(8,128)(2,1)} %collective-permute-done.43.refs_1_, bf16[3,512,1024]{2,1,0:T(8,128)(2,1)} %collective-permute-done.44.refs_2_, ...), custom_call_target="tpu_custom_call", output_to_operand_aliasing={{}: (4, {})} | custom-call | flops 4718592 | bytes 18874368 | tf_op jit(solution)/shard_map/put/pallas_call | solution.py:136
  529.2 10.8 %put.19.refs_3_ = bf16[8,2048,1024]{2,1,0:T(8,128)(2,1)} custom-call(s32[4]{0:T(128)} %fusion.place_ref, bf16[3,512,1024]{2,1,0:T(8,128)(2,1)} %collective-permute-done.39.refs_0_, bf16[3,512,1024]{2,1,0:T(8,128)(2,1)} %collective-permute-done.40.refs_1_, bf16[3,512,1024]{2,1,0:T(8,128)(2,1)} %collective-permute-done.41.refs_2_, ...), custom_call_target="tpu_custom_call", output_to_operand_aliasing={{}: (4, {})} | custom-call | flops 4718592 | bytes 18874368 | tf_op jit(solution)/shard_map/put/pallas_call | solution.py:136
  540.0 4.6 put.20.refs_3_
  544.7 3.7 put.21.refs_2_
  548.4 2.9 put.22.refs_1_
  551.3 2.5 put.23
  (185 shorter events, 28.8 us)
Async XLA Ops:
  4.2 4.3 collective-permute-start.6
  4.7 4.3 collective-permute-start.7
  7.2 3.2 collective-permute-start.8
  14.2 113.3 %collective-permute-start.25 = (bf16[1,256,1024]{2,1,0:T(8,128)(2,1)}, bf16[1,256,1024]{2,1,0:T(8,128)(2,1)S(1)}, u32[]{:S(2)}, u32[]{:S(2)}) collective-permute-start(bf16[1,256,1024]{2,1,0:T(8,128)(2,1)} %get-tuple-element.37), channel_id=1, source_target_pairs={{0,2},{1,3},{2,0},{3,1},{4,6},{5,7},{6,4},{7,5},{8,10},{9,11},{10,... | collective-permute-start | bytes 1572872 | tf_op jit(solution)/shard_map/ppermute | solution.py:188
  20.9 29.0 %collective-permute-start.3 = (f32[2,1,1024]{2,0,1:T(2,128)S(1)}, f32[2,1,1024]{2,0,1:T(2,128)S(1)}, u32[]{:S(2)}, u32[]{:S(2)}) collective-permute-start(f32[2,1,1024]{2,0,1:T(2,128)S(1)} %copy.37), channel_id=1, source_target_pairs={{0,1},{1,0},{2,3},{3,2},{4,5},{5,4},{6,7},{7,6},{8,9},{9,8},{10,11... | collective-permute-start | bytes 24584 | tf_op jit(solution)/shard_map/ppermute | solution.py:202
  20.9 29.8 %collective-permute-start.4 = (f32[2,1,1024]{2,0,1:T(2,128)S(1)}, f32[2,1,1024]{2,0,1:T(2,128)S(1)}, u32[]{:S(2)}, u32[]{:S(2)}) collective-permute-start(f32[2,1,1024]{2,0,1:T(2,128)S(1)} %copy.37), channel_id=1, source_target_pairs={{0,2},{1,3},{2,0},{3,1},{4,6},{5,7},{6,4},{7,5},{8,10},{9,11},{10,... | collective-permute-start | bytes 24584 | tf_op jit(solution)/shard_map/ppermute | solution.py:202
  21.9 28.9 %collective-permute-start.5 = (f32[2,1,1024]{2,0,1:T(2,128)S(1)}, f32[2,1,1024]{2,0,1:T(2,128)S(1)}, u32[]{:S(2)}, u32[]{:S(2)}) collective-permute-start(f32[2,1,1024]{2,0,1:T(2,128)S(1)} %copy.37), channel_id=1, source_target_pairs={{0,3},{1,2},{2,1},{3,0},{4,7},{5,6},{6,5},{7,4},{8,11},{9,10},{10,... | collective-permute-start | bytes 24584 | tf_op jit(solution)/shard_map/ppermute | solution.py:202
  39.0 46.9 %collective-permute-start.27 = (f32[8,1,1024]{2,1,0:T(1,128)}, f32[8,1,1024]{2,1,0:T(1,128)S(1)}, u32[]{:S(2)}, u32[]{:S(2)}) collective-permute-start(f32[8,1,1024]{2,1,0:T(1,128)} %local_max.7.refs_0_), channel_id=1, source_target_pairs={{0,1},{1,0},{2,3},{3,2},{4,5},{5,4},{6,7},{7,6},{8,9},{9,8},{10,11... | collective-permute-start | bytes 98312 | tf_op jit(solution)/shard_map/ppermute | solution.py:202
  49.8 37.3 %collective-permute-start.28 = (f32[8,1,1024]{2,1,0:T(1,128)S(1)}, f32[8,1,1024]{2,1,0:T(1,128)S(1)}, u32[]{:S(2)}, u32[]{:S(2)}) collective-permute-start(f32[8,1,1024]{2,1,0:T(1,128)S(1)} %copy-done.2), channel_id=1, source_target_pairs={{0,2},{1,3},{2,0},{3,1},{4,6},{5,7},{6,4},{7,5},{8,10},{9,11},{10,... | collective-permute-start | bytes 98312 | tf_op jit(solution)/shard_map/ppermute | solution.py:202
  50.8 1.4 collective-permute-start
  50.8 4.1 collective-permute-start.1
  52.2 35.5 %collective-permute-start.29 = (f32[8,1,1024]{2,1,0:T(1,128)S(1)}, f32[8,1,1024]{2,1,0:T(1,128)S(1)}, u32[]{:S(2)}, u32[]{:S(2)}) collective-permute-start(f32[8,1,1024]{2,1,0:T(1,128)S(1)} %copy-done.2), channel_id=1, source_target_pairs={{0,3},{1,2},{2,1},{3,0},{4,7},{5,6},{6,5},{7,4},{8,11},{9,10},{10,... | collective-permute-start | bytes 98312 | tf_op jit(solution)/shard_map/ppermute | solution.py:202
  54.8 30.9 %collective-permute-start.2 = (f32[5,1,1024]{2,1,0:T(1,128)}, f32[5,1,1024]{2,1,0:T(1,128)S(1)}, u32[]{:S(2)}, u32[]{:S(2)}) collective-permute-start(f32[5,1,1024]{2,1,0:T(1,128)} %local_max.4.refs_0_), channel_id=1, source_target_pairs={{0,3},{1,2},{2,1},{3,0},{4,7},{5,6},{6,5},{7,4},{8,11},{9,10},{10,... | collective-permute-start | bytes 61448 | tf_op jit(solution)/shard_map/ppermute | solution.py:202
  85.8 29.0 %collective-permute-start.45 = (bf16[512,64]{0,1:T(8,128)(2,1)S(1)}, bf16[512,64]{0,1:T(8,128)(2,1)S(1)}, u32[]{:S(2)}, u32[]{:S(2)}) collective-permute-start(bf16[512,64]{0,1:T(8,128)(2,1)S(1)} %all_gather.3), channel_id=1, source_target_pairs={{0,1},{1,0},{2,3},{3,2},{4,5},{5,4},{6,7},{7,6},{8,9},{9,8},{10,11... | collective-permute-start | bytes 196616 | tf_op jit(solution)/shard_map/ppermute | solution.py:244
  85.9 33.2 %collective-permute-start.46 = (bf16[512,64]{0,1:T(8,128)(2,1)S(1)}, bf16[512,64]{0,1:T(8,128)(2,1)S(1)}, u32[]{:S(2)}, u32[]{:S(2)}) collective-permute-start(bf16[512,64]{0,1:T(8,128)(2,1)S(1)} %all_gather.3), channel_id=1, source_target_pairs={{0,2},{1,3},{2,0},{3,1},{4,6},{5,7},{6,4},{7,5},{8,10},{9,11},{10,... | collective-permute-start | bytes 196616 | tf_op jit(solution)/shard_map/ppermute | solution.py:244
  87.1 32.1 %collective-permute-start.47 = (bf16[512,64]{0,1:T(8,128)(2,1)S(1)}, bf16[512,64]{0,1:T(8,128)(2,1)S(1)}, u32[]{:S(2)}, u32[]{:S(2)}) collective-permute-start(bf16[512,64]{0,1:T(8,128)(2,1)S(1)} %all_gather.3), channel_id=1, source_target_pairs={{0,3},{1,2},{2,1},{3,0},{4,7},{5,6},{6,5},{7,4},{8,11},{9,10},{10,... | collective-permute-start | bytes 196616 | tf_op jit(solution)/shard_map/ppermute | solution.py:244
  87.7 41.0 %collective-permute-start.24 = (bf16[1,256,1024]{2,1,0:T(8,128)(2,1)S(1)}, bf16[1,256,1024]{2,1,0:T(8,128)(2,1)}, u32[]{:S(2)}, u32[]{:S(2)}) collective-permute-start(bf16[1,256,1024]{2,1,0:T(8,128)(2,1)S(1)} %copy-done.40), channel_id=1, source_target_pairs={{0,1},{1,0},{2,3},{3,2},{4,5},{5,4},{6,7},{7,6},{8,9},{9,8},{10,11... | collective-permute-start | bytes 1572872 | tf_op jit(solution)/shard_map/ppermute | solution.py:188
  114.8 17.1 %collective-permute-start.22 = (bf16[1,256,1024]{2,1,0:T(8,128)(2,1)}, bf16[1,256,1024]{2,1,0:T(8,128)(2,1)}, u32[]{:S(2)}, u32[]{:S(2)}) collective-permute-start(bf16[1,256,1024]{2,1,0:T(8,128)(2,1)} %get-tuple-element.36), channel_id=1, source_target_pairs={{0,2},{1,3},{2,0},{3,1},{4,6},{5,7},{6,4},{7,5},{8,10},{9,11},{10,... | collective-permute-start | bytes 1572872 | tf_op jit(solution)/shard_map/ppermute | solution.py:188
  119.1 13.7 %collective-permute-start.21 = (bf16[1,256,1024]{2,1,0:T(8,128)(2,1)}, bf16[1,256,1024]{2,1,0:T(8,128)(2,1)S(1)}, u32[]{:S(2)}, u32[]{:S(2)}) collective-permute-start(bf16[1,256,1024]{2,1,0:T(8,128)(2,1)} %get-tuple-element.36), channel_id=1, source_target_pairs={{0,1},{1,0},{2,3},{3,2},{4,5},{5,4},{6,7},{7,6},{8,9},{9,8},{10,11... | collective-permute-start | bytes 1572872 | tf_op jit(solution)/shard_map/ppermute | solution.py:188
  119.8 21.2 %collective-permute-start.34 = (bf16[1,256,1024]{2,1,0:T(8,128)(2,1)}, bf16[1,256,1024]{2,1,0:T(8,128)(2,1)S(1)}, u32[]{:S(2)}, u32[]{:S(2)}) collective-permute-start(bf16[1,256,1024]{2,1,0:T(8,128)(2,1)} %get-tuple-element.44), channel_id=1, source_target_pairs={{0,2},{1,3},{2,0},{3,1},{4,6},{5,7},{6,4},{7,5},{8,10},{9,11},{10,... | collective-permute-start | bytes 1572872 | tf_op jit(solution)/shard_map/ppermute | solution.py:188
  127.5 55.6 %collective-permute-start.19 = (bf16[1,512,1024]{2,1,0:T(8,128)(2,1)}, bf16[1,512,1024]{2,1,0:T(8,128)(2,1)}, u32[]{:S(2)}, u32[]{:S(2)}) collective-permute-start(bf16[1,512,1024]{2,1,0:T(8,128)(2,1)} %get-tuple-element.35), channel_id=1, source_target_pairs={{0,2},{1,3},{2,0},{3,1},{4,6},{5,7},{6,4},{7,5},{8,10},{9,11},{10,... | collective-permute-start | bytes 3145736 | tf_op jit(solution)/shard_map/ppermute | solution.py:188
  128.7 55.6 %collective-permute-start.18 = (bf16[1,512,1024]{2,1,0:T(8,128)(2,1)}, bf16[1,512,1024]{2,1,0:T(8,128)(2,1)S(1)}, u32[]{:S(2)}, u32[]{:S(2)}) collective-permute-start(bf16[1,512,1024]{2,1,0:T(8,128)(2,1)} %get-tuple-element.35), channel_id=1, source_target_pairs={{0,1},{1,0},{2,3},{3,2},{4,5},{5,4},{6,7},{7,6},{8,9},{9,8},{10,11... | collective-permute-start | bytes 3145736 | tf_op jit(solution)/shard_map/ppermute | solution.py:188
  131.9 42.2 %collective-permute-start.30 = (bf16[1,256,1024]{2,1,0:T(8,128)(2,1)}, bf16[1,256,1024]{2,1,0:T(8,128)(2,1)}, u32[]{:S(2)}, u32[]{:S(2)}) collective-permute-start(bf16[1,256,1024]{2,1,0:T(8,128)(2,1)} %get-tuple-element.43), channel_id=1, source_target_pairs={{0,2},{1,3},{2,0},{3,1},{4,6},{5,7},{6,4},{7,5},{8,10},{9,11},{10,... | collective-permute-start | bytes 1572872 | tf_op jit(solution)/shard_map/ppermute | solution.py:188
  132.8 42.4 %collective-permute-start.26 = (bf16[1,256,1024]{2,1,0:T(8,128)(2,1)S(1)}, bf16[1,256,1024]{2,1,0:T(8,128)(2,1)}, u32[]{:S(2)}, u32[]{:S(2)}) collective-permute-start(bf16[1,256,1024]{2,1,0:T(8,128)(2,1)S(1)} %collective-permute-done.25.refs_1_), channel_id=1, source_target_pairs={{0,1},{1,0},{2,3},{3,2},{4,5},{5,4},{6,7},{7,6},{8,9},{9,8},{10,11... | collective-permute-start | bytes 1572872 | tf_op jit(solution)/shard_map/ppermute | solution.py:188
  141.1 34.1 %collective-permute-start.23 = (bf16[1,256,1024]{2,1,0:T(8,128)(2,1)}, bf16[1,256,1024]{2,1,0:T(8,128)(2,1)}, u32[]{:S(2)}, u32[]{:S(2)}) collective-permute-start(bf16[1,256,1024]{2,1,0:T(8,128)(2,1)} %collective-permute-done.22.refs_1_), channel_id=1, source_target_pairs={{0,1},{1,0},{2,3},{3,2},{4,5},{5,4},{6,7},{7,6},{8,9},{9,8},{10,11... | collective-permute-start | bytes 1572872 | tf_op jit(solution)/shard_map/ppermute | solution.py:188
  174.1 26.3 %collective-permute-start.16 = (bf16[1,512,1024]{2,1,0:T(8,128)(2,1)}, bf16[1,512,1024]{2,1,0:T(8,128)(2,1)}, u32[]{:S(2)}, u32[]{:S(2)}) collective-permute-start(bf16[1,512,1024]{2,1,0:T(8,128)(2,1)} %get-tuple-element.34), channel_id=1, source_target_pairs={{0,2},{1,3},{2,0},{3,1},{4,6},{5,7},{6,4},{7,5},{8,10},{9,11},{10,... | collective-permute-start | bytes 3145736 | tf_op jit(solution)/shard_map/ppermute | solution.py:188
  175.2 25.2 %collective-permute-start.15 = (bf16[1,512,1024]{2,1,0:T(8,128)(2,1)}, bf16[1,512,1024]{2,1,0:T(8,128)(2,1)S(1)}, u32[]{:S(2)}, u32[]{:S(2)}) collective-permute-start(bf16[1,512,1024]{2,1,0:T(8,128)(2,1)} %get-tuple-element.34), channel_id=1, source_target_pairs={{0,1},{1,0},{2,3},{3,2},{4,5},{5,4},{6,7},{7,6},{8,9},{9,8},{10,11... | collective-permute-start | bytes 3145736 | tf_op jit(solution)/shard_map/ppermute | solution.py:188
  175.2 47.5 %collective-permute-start.37 = (bf16[1,512,1024]{2,1,0:T(8,128)(2,1)}, bf16[1,512,1024]{2,1,0:T(8,128)(2,1)S(1)}, u32[]{:S(2)}, u32[]{:S(2)}) collective-permute-start(bf16[1,512,1024]{2,1,0:T(8,128)(2,1)} %get-tuple-element.45), channel_id=1, source_target_pairs={{0,2},{1,3},{2,0},{3,1},{4,6},{5,7},{6,4},{7,5},{8,10},{9,11},{10,... | collective-permute-start | bytes 3145736 | tf_op jit(solution)/shard_map/ppermute | solution.py:188
  183.1 84.7 %collective-permute-start.10 = (bf16[2,512,1024]{2,1,0:T(8,128)(2,1)}, bf16[2,512,1024]{2,1,0:T(8,128)(2,1)}, u32[]{:S(2)}, u32[]{:S(2)}) collective-permute-start(bf16[2,512,1024]{2,1,0:T(8,128)(2,1)} %get-tuple-element.32), channel_id=1, source_target_pairs={{0,2},{1,3},{2,0},{3,1},{4,6},{5,7},{6,4},{7,5},{8,10},{9,11},{10,... | collective-permute-start | bytes 6291464 | tf_op jit(solution)/shard_map/ppermute | solution.py:188
  184.3 38.5 %collective-permute-start.36 = (bf16[1,512,1024]{2,1,0:T(8,128)(2,1)}, bf16[1,512,1024]{2,1,0:T(8,128)(2,1)S(1)}, u32[]{:S(2)}, u32[]{:S(2)}) collective-permute-start(bf16[1,512,1024]{2,1,0:T(8,128)(2,1)} %get-tuple-element.45), channel_id=1, source_target_pairs={{0,1},{1,0},{2,3},{3,2},{4,5},{5,4},{6,7},{7,6},{8,9},{9,8},{10,11... | collective-permute-start | bytes 3145736 | tf_op jit(solution)/shard_map/ppermute | solution.py:188
  200.4 68.6 %collective-permute-start.9 = (bf16[2,512,1024]{2,1,0:T(8,128)(2,1)}, bf16[2,512,1024]{2,1,0:T(8,128)(2,1)S(1)}, u32[]{:S(2)}, u32[]{:S(2)}) collective-permute-start(bf16[2,512,1024]{2,1,0:T(8,128)(2,1)} %get-tuple-element.32), channel_id=1, source_target_pairs={{0,1},{1,0},{2,3},{3,2},{4,5},{5,4},{6,7},{7,6},{8,9},{9,8},{10,11... | collective-permute-start | bytes 6291464 | tf_op jit(solution)/shard_map/ppermute | solution.py:188
  200.4 24.5 %collective-permute-start.20 = (bf16[1,512,1024]{2,1,0:T(8,128)(2,1)}, bf16[1,512,1024]{2,1,0:T(8,128)(2,1)S(1)}, u32[]{:S(2)}, u32[]{:S(2)}) collective-permute-start(bf16[1,512,1024]{2,1,0:T(8,128)(2,1)} %collective-permute-done.19.refs_1_), channel_id=1, source_target_pairs={{0,1},{1,0},{2,3},{3,2},{4,5},{5,4},{6,7},{7,6},{8,9},{9,8},{10,11... | collective-permute-start | bytes 3145736 | tf_op jit(solution)/shard_map/ppermute | solution.py:188
  222.8 2.9 collective-permute-start.17
  223.8 111.3 %collective-permute-start.13 = (bf16[3,512,1024]{2,1,0:T(8,128)(2,1)}, bf16[3,512,1024]{2,1,0:T(8,128)(2,1)S(1)}, u32[]{:S(2)}, u32[]{:S(2)}) collective-permute-start(bf16[3,512,1024]{2,1,0:T(8,128)(2,1)} %get-tuple-element.33), channel_id=1, source_target_pairs={{0,2},{1,3},{2,0},{3,1},{4,6},{5,7},{6,4},{7,5},{8,10},{9,11},{10,... | collective-permute-start | bytes 9437192 | tf_op jit(solution)/shard_map/ppermute | solution.py:188
  224.9 110.2 %collective-permute-start.12 = (bf16[3,512,1024]{2,1,0:T(8,128)(2,1)}, bf16[3,512,1024]{2,1,0:T(8,128)(2,1)}, u32[]{:S(2)}, u32[]{:S(2)}) collective-permute-start(bf16[3,512,1024]{2,1,0:T(8,128)(2,1)} %get-tuple-element.33), channel_id=1, source_target_pairs={{0,1},{1,0},{2,3},{3,2},{4,5},{5,4},{6,7},{7,6},{8,9},{9,8},{10,11... | collective-permute-start | bytes 9437192 | tf_op jit(solution)/shard_map/ppermute | solution.py:188
  225.6 177.0 %collective-permute-start.43 = (bf16[3,512,1024]{2,1,0:T(8,128)(2,1)}, bf16[3,512,1024]{2,1,0:T(8,128)(2,1)}, u32[]{:S(2)}, u32[]{:S(2)}) collective-permute-start(bf16[3,512,1024]{2,1,0:T(8,128)(2,1)} %get-tuple-element.47), channel_id=1, source_target_pairs={{0,2},{1,3},{2,0},{3,1},{4,6},{5,7},{6,4},{7,5},{8,10},{9,11},{10,... | collective-permute-start | bytes 9437192 | tf_op jit(solution)/shard_map/ppermute | solution.py:188
  267.8 200.6 %collective-permute-start.40 = (bf16[3,512,1024]{2,1,0:T(8,128)(2,1)}, bf16[3,512,1024]{2,1,0:T(8,128)(2,1)}, u32[]{:S(2)}, u32[]{:S(2)}) collective-permute-start(bf16[3,512,1024]{2,1,0:T(8,128)(2,1)} %get-tuple-element.46), channel_id=1, source_target_pairs={{0,2},{1,3},{2,0},{3,1},{4,6},{5,7},{6,4},{7,5},{8,10},{9,11},{10,... | collective-permute-start | bytes 9437192 | tf_op jit(solution)/shard_map/ppermute | solution.py:188
  269.0 199.4 %collective-permute-start.42 = (bf16[3,512,1024]{2,1,0:T(8,128)(2,1)}, bf16[3,512,1024]{2,1,0:T(8,128)(2,1)}, u32[]{:S(2)}, u32[]{:S(2)}) collective-permute-start(bf16[3,512,1024]{2,1,0:T(8,128)(2,1)} %get-tuple-element.47), channel_id=1, source_target_pairs={{0,1},{1,0},{2,3},{3,2},{4,5},{5,4},{6,7},{7,6},{8,9},{9,8},{10,11... | collective-permute-start | bytes 9437192 | tf_op jit(solution)/shard_map/ppermute | solution.py:188
  335.1 138.9 %collective-permute-start.39 = (bf16[3,512,1024]{2,1,0:T(8,128)(2,1)}, bf16[3,512,1024]{2,1,0:T(8,128)(2,1)}, u32[]{:S(2)}, u32[]{:S(2)}) collective-permute-start(bf16[3,512,1024]{2,1,0:T(8,128)(2,1)} %get-tuple-element.46), channel_id=1, source_target_pairs={{0,1},{1,0},{2,3},{3,2},{4,5},{5,4},{6,7},{7,6},{8,9},{9,8},{10,11... | collective-permute-start | bytes 9437192 | tf_op jit(solution)/shard_map/ppermute | solution.py:188
  335.2 142.4 %collective-permute-start.14 = (bf16[3,512,1024]{2,1,0:T(8,128)(2,1)S(1)}, bf16[3,512,1024]{2,1,0:T(8,128)(2,1)}, u32[]{:S(2)}, u32[]{:S(2)}) collective-permute-start(bf16[3,512,1024]{2,1,0:T(8,128)(2,1)S(1)} %collective-permute-done.13.refs_1_), channel_id=1, source_target_pairs={{0,1},{1,0},{2,3},{3,2},{4,5},{5,4},{6,7},{7,6},{8,9},{9,8},{10,11... | collective-permute-start | bytes 9437192 | tf_op jit(solution)/shard_map/ppermute | solution.py:188
  402.6 75.2 %collective-permute-start.44 = (bf16[3,512,1024]{2,1,0:T(8,128)(2,1)}, bf16[3,512,1024]{2,1,0:T(8,128)(2,1)}, u32[]{:S(2)}, u32[]{:S(2)}) collective-permute-start(bf16[3,512,1024]{2,1,0:T(8,128)(2,1)} %collective-permute-done.43.refs_1_), channel_id=1, source_target_pairs={{0,1},{1,0},{2,3},{3,2},{4,5},{5,4},{6,7},{7,6},{8,9},{9,8},{10,11... | collective-permute-start | bytes 9437192 | tf_op jit(solution)/shard_map/ppermute | solution.py:188
  468.4 9.7 %collective-permute-start.41 = (bf16[3,512,1024]{2,1,0:T(8,128)(2,1)}, bf16[3,512,1024]{2,1,0:T(8,128)(2,1)}, u32[]{:S(2)}, u32[]{:S(2)}) collective-permute-start(bf16[3,512,1024]{2,1,0:T(8,128)(2,1)} %collective-permute-done.40.refs_1_), channel_id=1, source_target_pairs={{0,1},{1,0},{2,3},{3,2},{4,5},{5,4},{6,7},{7,6},{8,9},{9,8},{10,11... | collective-permute-start | bytes 9437192 | tf_op jit(solution)/shard_map/ppermute | solution.py:188
  468.4 9.0 %collective-permute-start.11 = (bf16[2,512,1024]{2,1,0:T(8,128)(2,1)}, bf16[2,512,1024]{2,1,0:T(8,128)(2,1)}, u32[]{:S(2)}, u32[]{:S(2)}) collective-permute-start(bf16[2,512,1024]{2,1,0:T(8,128)(2,1)} %collective-permute-done.10.refs_1_), channel_id=1, source_target_pairs={{0,1},{1,0},{2,3},{3,2},{4,5},{5,4},{6,7},{7,6},{8,9},{9,8},{10,11... | collective-permute-start | bytes 6291464 | tf_op jit(solution)/shard_map/ppermute | solution.py:188
  474.0 66.0 %collective-permute-start.38 = (bf16[1,512,1024]{2,1,0:T(8,128)(2,1)}, bf16[1,512,1024]{2,1,0:T(8,128)(2,1)}, u32[]{:S(2)}, u32[]{:S(2)}) collective-permute-start(bf16[1,512,1024]{2,1,0:T(8,128)(2,1)} %copy-done.11), channel_id=1, source_target_pairs={{0,1},{1,0},{2,3},{3,2},{4,5},{5,4},{6,7},{7,6},{8,9},{9,8},{10,11... | collective-permute-start | bytes 3145736 | tf_op jit(solution)/shard_map/ppermute | solution.py:188
  477.4 67.3 %collective-permute-start.33 = (bf16[1,256,1024]{2,1,0:T(8,128)(2,1)}, bf16[1,256,1024]{2,1,0:T(8,128)(2,1)}, u32[]{:S(2)}, u32[]{:S(2)}) collective-permute-start(bf16[1,256,1024]{2,1,0:T(8,128)(2,1)} %get-tuple-element.44), channel_id=1, source_target_pairs={{0,1},{1,0},{2,3},{3,2},{4,5},{5,4},{6,7},{7,6},{8,9},{9,8},{10,11... | collective-permute-start | bytes 1572872 | tf_op jit(solution)/shard_map/ppermute | solution.py:188
  477.5 70.9 %collective-permute-start.32 = (bf16[1,256,1024]{2,1,0:T(8,128)(2,1)}, bf16[1,256,1024]{2,1,0:T(8,128)(2,1)}, u32[]{:S(2)}, u32[]{:S(2)}) collective-permute-start(bf16[1,256,1024]{2,1,0:T(8,128)(2,1)} %get-tuple-element.43), channel_id=1, source_target_pairs={{0,1},{1,0},{2,3},{3,2},{4,5},{5,4},{6,7},{7,6},{8,9},{9,8},{10,11... | collective-permute-start | bytes 1572872 | tf_op jit(solution)/shard_map/ppermute | solution.py:188
  477.9 66.8 %collective-permute-start.35 = (bf16[1,256,1024]{2,1,0:T(8,128)(2,1)}, bf16[1,256,1024]{2,1,0:T(8,128)(2,1)}, u32[]{:S(2)}, u32[]{:S(2)}) collective-permute-start(bf16[1,256,1024]{2,1,0:T(8,128)(2,1)} %copy-done.17), channel_id=1, source_target_pairs={{0,1},{1,0},{2,3},{3,2},{4,5},{5,4},{6,7},{7,6},{8,9},{9,8},{10,11... | collective-permute-start | bytes 1572872 | tf_op jit(solution)/shard_map/ppermute | solution.py:188
  478.0 73.2 %collective-permute-start.31 = (bf16[1,256,1024]{2,1,0:T(8,128)(2,1)}, bf16[1,256,1024]{2,1,0:T(8,128)(2,1)}, u32[]{:S(2)}, u32[]{:S(2)}) collective-permute-start(bf16[1,256,1024]{2,1,0:T(8,128)(2,1)} %collective-permute-done.30.refs_1_), channel_id=1, source_target_pairs={{0,1},{1,0},{2,3},{3,2},{4,5},{5,4},{6,7},{7,6},{8,9},{9,8},{10,11... | collective-permute-start | bytes 1572872 | tf_op jit(solution)/shard_map/ppermute | solution.py:188
  (44 other events, 6051.9 us)

commit v2 on v1

v2 whole, which is shorter than its diff:
```python
import functools

import jax
import jax.numpy as jnp
from jax import lax
from jax.experimental import pallas as pl
from jax.experimental.pallas import tpu as pltpu
from jax.sharding import PartitionSpec as P


ANY = pl.BlockSpec(memory_space=pl.ANY)
HBM = pl.BlockSpec(memory_space=pltpu.HBM)
SMEM = pl.BlockSpec(memory_space=pltpu.SMEM)
SUB = 8
PARAMS = pltpu.CompilerParams(vmem_limit_bytes=48 * 2**20)


def mixed(share, train, other):
    return share * train + (1.0 - share) * other


def fetches(first, low, height, blocks, sources, held, sems):
    step = height // blocks
    return [
        [
            pltpu.make_async_copy(
                ref.at[first, pl.ds(low + j * step, step)], held.at[k, pl.ds(j * step, step)], sems.at[k, j]
            )
            for k, ref in enumerate(sources)
        ]
        for j in range(blocks)
    ]


def first_max_kernel(first, blocks, mix_ref, train_ref, other_ref, top_ref, share_ref, held, sems, mix_sem):
    rows = held.shape[1]
    step = rows // blocks
    copies = fetches(first, 0, rows, blocks, (train_ref, other_ref), held, sems)
    for pair in copies:
        for copy in pair:
            copy.start()
    mix = pltpu.make_async_copy(mix_ref, share_ref, mix_sem)
    mix.start()
    mix.wait()
    share = share_ref[first]
    top = jnp.zeros((SUB, held.shape[2]), jnp.float32)
    for j, pair in enumerate(copies):
        for copy in pair:
            copy.wait()

        def body(i, top):
            at = pl.ds(pl.multiple_of(j * step + i * SUB, SUB), SUB)
            return jnp.maximum(top, jnp.abs(mixed(share, held[0, at], held[1, at])))

        top = lax.fori_loop(0, step // SUB, body, top, unroll=4)
    top_ref[...] = jnp.max(top, axis=0, keepdims=True)


def first_max(mix_share, train, other, first):
    _, rows, cols = train.shape
    blocks = 4
    return pl.pallas_call(
        functools.partial(first_max_kernel, first, blocks),
        out_shape=jax.ShapeDtypeStruct((1, cols), jnp.float32),
        in_specs=[HBM, HBM, HBM],
        scratch_shapes=[
            pltpu.SMEM(mix_share.shape, jnp.float32),
            pltpu.VMEM((2, rows, cols), jnp.float32),
            pltpu.SemaphoreType.DMA((2, blocks)),
            pltpu.SemaphoreType.DMA,
        ],
        compiler_params=PARAMS,
        cost_estimate=pl.CostEstimate(flops=5 * rows * cols, bytes_accessed=8 * rows * cols, transcendentals=0),
        name="first_max",
    )(mix_share, train, other)


def max_kernel(first, mix_ref, train_ref, other_ref, top_ref):
    e = pl.program_id(0)
    share = mix_ref[first + e]

    def body(i, top):
        at = pl.ds(pl.multiple_of(i * SUB, SUB), SUB)
        return jnp.maximum(top, jnp.abs(mixed(share, train_ref[0, at], other_ref[0, at])))

    rows, cols = train_ref.shape[1:]
    top = lax.fori_loop(0, rows // SUB, body, jnp.zeros((SUB, cols), jnp.float32), unroll=4)
    top_ref[pl.ds(e, 1)] = jnp.max(top, axis=0, keepdims=True)


def local_max(mix_share, train, other, first, count):
    _, rows, cols = train.shape
    block = pl.BlockSpec((1, rows, cols), lambda e: (first + e, 0, 0))
    return pl.pallas_call(
        functools.partial(max_kernel, first),
        out_shape=jax.ShapeDtypeStruct((count, cols), jnp.float32),
        grid=(count,),
        in_specs=[SMEM, block, block],
        out_specs=pl.BlockSpec((count, cols), lambda e: (0, 0)),
        compiler_params=PARAMS,
        cost_estimate=pl.CostEstimate(
            flops=5 * count * rows * cols, bytes_accessed=8 * count * rows * cols, transcendentals=0
        ),
        name="local_max",
    )(mix_share, train, other)


def top_of(refs, at):
    top = refs[0][pl.ds(at, 1)]
    for ref in refs[1:]:
        top = jnp.maximum(top, ref[pl.ds(at, 1)])
    return top


def first_narrow_kernel(tops, piece, blocks, mix_ref, *refs):
    first, _, low, height = piece
    top_refs, (train_ref, other_ref, send_ref, share_ref, held, sems, mix_sem) = refs[:tops], refs[tops:]
    step = height // blocks
    copies = fetches(first, low, height, blocks, (train_ref, other_ref), held, sems)
    b = pl.program_id(0)
    mix = pltpu.make_async_copy(mix_ref, share_ref, mix_sem)

    @pl.when(b == 0)
    def _():
        for pair in copies:
            for copy in pair:
                copy.start()
        mix.start()
        mix.wait()

    for j, pair in enumerate(copies):

        @pl.when(b == j)
        def _():
            for copy in pair:
                copy.wait()

    share = share_ref[first]
    scale = jnp.broadcast_to(1.0 / top_of(top_refs, 0), (2 * SUB, held.shape[2]))

    def body(i, carry):
        at = pl.ds(pl.multiple_of(b * step + i * 2 * SUB, 2 * SUB), 2 * SUB)
        part = mixed(share, held[0, at], held[1, at]) * scale
        send_ref[0, pl.ds(pl.multiple_of(i * 2 * SUB, 2 * SUB), 2 * SUB)] = part.astype(jnp.bfloat16)
        return carry

    lax.fori_loop(0, step // (2 * SUB), body, 0, unroll=2)


def first_narrow(mix_share, tops, train, other, piece):
    cols = train.shape[2]
    height = piece[3]
    blocks = 2
    return pl.pallas_call(
        functools.partial(first_narrow_kernel, len(tops), piece, blocks),
        out_shape=jax.ShapeDtypeStruct((1, height, cols), jnp.bfloat16),
        grid=(blocks,),
        in_specs=[HBM] + [pl.BlockSpec((1, cols), lambda b: (0, 0))] * len(tops) + [HBM, HBM],
        out_specs=pl.BlockSpec((1, height // blocks, cols), lambda b: (0, b, 0)),
        scratch_shapes=[
            pltpu.SMEM(mix_share.shape, jnp.float32),
            pltpu.VMEM((2, height, cols), jnp.float32),
            pltpu.SemaphoreType.DMA((2, blocks)),
            pltpu.SemaphoreType.DMA,
        ],
        compiler_params=PARAMS,
        cost_estimate=pl.CostEstimate(flops=6 * height * cols, bytes_accessed=10 * height * cols, transcendentals=0),
        name="first_narrow",
    )(mix_share, *tops, train, other)


def narrow_kernel(first, at, tops, place_ref, mix_ref, *refs):
    top_refs, (train_ref, other_ref), (send_ref, whole_ref) = refs[:tops], refs[tops : tops + 2], refs[-2:]
    e = pl.program_id(0)
    height, cols = train_ref.shape[1:]
    scale = jnp.broadcast_to(1.0 / top_of(top_refs, at + e), (2 * SUB, cols))
    share = mix_ref[first + e]

    def body(i, carry):
        rows = pl.ds(pl.multiple_of(i * 2 * SUB, 2 * SUB), 2 * SUB)
        part = (mixed(share, train_ref[0, rows], other_ref[0, rows]) * scale).astype(jnp.bfloat16)
        send_ref[0, rows] = part
        whole_ref[0, rows] = part
        return carry

    lax.fori_loop(0, height // (2 * SUB), body, 0, unroll=2)


def narrow(place, mix_share, tops, at, train, other, piece, parts, whole):
    first, count, low, height = piece
    experts, rows, cols = train.shape
    step = max(d for d in (height, height // 2) if d <= 256 or d == height // 2)
    step = step if low % step == 0 and rows % step == 0 else rows // 4
    block = pl.BlockSpec((1, step, cols), lambda e, r, place: (first + e, low // step + r, 0))
    held = [] if whole is None else [whole]
    return pl.pallas_call(
        functools.partial(narrow_kernel, first, at, len(tops)),
        out_shape=(
            jax.ShapeDtypeStruct((count, height, cols), jnp.bfloat16),
            jax.ShapeDtypeStruct((experts, parts * rows, cols), jnp.bfloat16),
        ),
        grid_spec=pltpu.PrefetchScalarGridSpec(
            num_scalar_prefetch=1,
            grid=(count, height // step),
            in_specs=[SMEM]
            + [pl.BlockSpec(top.shape, lambda e, r, place: (0, 0)) for top in tops]
            + [block, block]
            + [ANY] * len(held),
            out_specs=(
                pl.BlockSpec((1, step, cols), lambda e, r, place: (e, r, 0)),
                pl.BlockSpec(
                    (1, step, cols),
                    lambda e, r, place: (first + e, place[0] * (rows // step) + low // step + r, 0),
                ),
            ),
        ),
        input_output_aliases={4 + len(tops): 1} if held else {},
        compiler_params=PARAMS,
        cost_estimate=pl.CostEstimate(
            flops=6 * count * height * cols, bytes_accessed=12 * count * height * cols, transcendentals=0
        ),
        name="narrow",
    )(place, mix_share, *tops, train, other, *held)


def put_kernel(slots, piece, rows, place_ref, *refs):
    first, count, low, height = piece
    whole_ref, held, in_sems, out_sems = refs[-4:]
    items = [(s, e) for s in range(len(slots)) for e in range(count)]
    reads, writes = [], []
    for i, (s, e) in enumerate(items):
        reads.append(pltpu.make_async_copy(refs[s].at[e], held.at[i], in_sems.at[i]))
        start = pl.multiple_of(place_ref[slots[s]] * rows + low, 2 * SUB)
        target = whole_ref.at[first + e, pl.ds(start, height)]
        writes.append(pltpu.make_async_copy(held.at[i], target, out_sems.at[i]))
    for read in reads:
        read.start()
    for read, write in zip(reads, writes):
        read.wait()
        write.start()
    for write in writes:
        write.wait()


def put(place, arrays, slots, piece, rows, whole):
    _, count, _, height = piece
    cols = whole.shape[2]
    n = len(arrays) * count
    return pl.pallas_call(
        functools.partial(put_kernel, tuple(slots), piece, rows),
        out_shape=jax.ShapeDtypeStruct(whole.shape, whole.dtype),
        in_specs=[SMEM] + [ANY] * (len(arrays) + 1),
        out_specs=ANY,
        scratch_shapes=[
            pltpu.VMEM((n, height, cols), jnp.bfloat16),
            pltpu.SemaphoreType.DMA((n,)),
            pltpu.SemaphoreType.DMA((n,)),
        ],
        input_output_aliases={1 + len(arrays): 0},
        compiler_params=PARAMS,
        cost_estimate=pl.CostEstimate(flops=n * height * cols, bytes_accessed=4 * n * height * cols, transcendentals=0),
        name="put",
    )(place, *arrays, whole)


def scales_kernel(groups, parts, *refs):
    for g, (a, first, count) in enumerate(groups):
        tops = refs[g * parts : (g + 1) * parts]
        top = tops[0][...]
        for ref in tops[1:]:
            top = jnp.maximum(top, ref[...])
        refs[len(groups) * parts + a][pl.ds(first, count)] = top


def all_scales(tops, groups, experts, cols):
    flat = [top for group in tops for top in group]
    shape = jax.ShapeDtypeStruct((experts, cols), jnp.float32)
    return pl.pallas_call(
        functools.partial(scales_kernel, groups, len(tops[0])),
        out_shape=(shape, shape),
        compiler_params=PARAMS,
        cost_estimate=pl.CostEstimate(flops=8 * experts * cols, bytes_accessed=64 * experts * cols, transcendentals=0),
        name="scales",
    )(*flat)


def keep_kernel(x_ref, y_ref):
    y_ref[...] = x_ref[...]


def keep(x):
    return pl.pallas_call(
        keep_kernel,
        out_shape=jax.ShapeDtypeStruct(x.shape, x.dtype),
        compiler_params=PARAMS,
        cost_estimate=pl.CostEstimate(flops=x.size, bytes_accessed=4 * x.size, transcendentals=0),
        name="keep",
    )(x)


def plan(experts, rows):
    def runs(lo, hi, most):
        return [(e, min(most, hi - e)) for e in range(lo, hi, most)]

    def split(cut):
        return [(0, cut), (cut, rows - cut)]

    groups = [(0, 0, 1)]
    groups += [(0, e, n) for e, n in runs(1, min(3, experts), 2)]
    groups += [(0, e, n) for e, n in runs(3, experts, experts)]
    groups += [(1, 0, experts)]
    pieces = [(0, (0, 1, low, height)) for low, height in split(rows // 2)]
    pieces += [(0, (e, n, 0, rows)) for e, n in runs(1, min(3, experts), 1)]
    pieces += [(0, (e, n, 0, rows)) for e, n in runs(3, experts, 3)]
    tail = max(experts - 2, 0)
    pieces += [(1, (e, n, 0, rows)) for e, n in runs(0, tail, 3)]
    pieces += [(1, (e, n, 0, rows)) for e, n in runs(tail, experts - 1, 1)]
    pieces += [(1, (experts - 1, 1, low, height)) for low, height in split(rows - rows // 4)]
    return groups, pieces


def group_of(groups, array, expert):
    return next(g for g, (a, e, n) in enumerate(groups) if a == array and e <= expert < e + n)


def per_device(parts, train_gate, other_gate, train_up, other_up, mix_share, router_weight, router_gain):
    experts, rows, cols = train_gate.shape
    inner = 2 if parts % 2 == 0 else 1
    outer = parts // inner
    me = lax.axis_index("fsdp")
    groups, pieces = plan(experts, rows)

    def step(k, l):
        return [(i, (i // inner + k) % outer * inner + (i % inner ^ l)) for i in range(parts)]

    def spread(x):
        got = [x]
        if inner == 2:
            got.append(lax.ppermute(x, "fsdp", step(0, 1)))
        for k in range(1, outer):
            got.append(lax.ppermute(x, "fsdp", step(k, 0)))
            if inner == 2:
                got.append(lax.ppermute(got[-1], "fsdp", step(0, 1)))
        return got

    steps = [[dict((b, a) for a, b in step(k, l)) for l in range(inner)] for k in range(outer)]
    table = [[steps[k][l][i] for k in range(outer) for l in range(inner)] for i in range(parts)]
    place = jnp.asarray(table, jnp.int32)[me]

    train, other = (train_gate, train_up), (other_gate, other_up)
    tops = []
    for g, (a, first, count) in enumerate(groups):
        if g == 0:
            top = first_max(mix_share, train[a], other[a], first)
        else:
            top = local_max(mix_share, train[a], other[a], first, count)
        if g > 0:
            tops.append(spread(top))
            continue
        direct = [top]
        for s in range(1, parts):
            direct.append(lax.ppermute(top, "fsdp", step(s // inner, s % inner)))
        tops.append(direct)

    whole = [None, None]
    got = []
    for i, (a, piece) in enumerate(pieces):
        g = group_of(groups, a, piece[0])
        if i == 0:
            own = first_narrow(mix_share, tops[g], train[a], other[a], piece)
        else:
            own, whole[a] = narrow(
                place, mix_share, tops[g], piece[0] - groups[g][1], train[a], other[a], piece, parts, whole[a]
            )
        got.append(spread(own))

    for i, (a, piece) in enumerate(pieces):
        slots = list(range(0 if i == 0 else 1, parts))
        cut = len(slots) - 1 if i + 1 == len(pieces) else 0
        for some in (slots[:cut], slots[cut:]):
            if some:
                whole[a] = put(place, [got[i][j] for j in some], some, piece, rows, whole[a])

    scales = all_scales(tops, groups, experts, cols)
    part_router = (router_weight * router_gain[:, None]).astype(jnp.bfloat16)
    row_router = jnp.zeros((parts * rows, part_router.shape[1]), jnp.bfloat16)
    for j, x in enumerate(spread(part_router)):
        row_router = lax.dynamic_update_slice(row_router, x, (place[j] * rows, 0))
    wide_router = lax.all_gather(row_router, "ep", axis=1, tiled=True)
    serve_router = keep(wide_router.T).T
    return whole[0], whole[1], scales[0], scales[1], serve_router


def solution(mesh):
    parts = mesh.shape["fsdp"]
    placed = (
        P("ep", "fsdp", None),
        P("ep", "fsdp", None),
        P("ep", "fsdp", None),
        P("ep", "fsdp", None),
        P("ep"),
        P("fsdp", "ep"),
        P("fsdp"),
    )
    return jax.shard_map(
        functools.partial(per_device, parts),
        mesh=mesh,
        in_specs=placed,
        out_specs=(P("ep", None, None), P("ep", None, None), P("ep", None), P("ep", None), P()),
        check_vma=False,
    )
```

time: 556 us -> 526 us (0.946)
  Pallas kernels: 168 us -> 132 us
  local copies, waits for them, and re-layouts: 13.5 us -> 26.3 us
    pallas_call x27 -> x29, Pallas kernels: 168 us -> 132 us  [the longest x10 53.5 us: narrow(): pl.pallas_call(functools.partial(narrow_kernel, first, at, len(tops)), ou...]
    unnamed x90 -> x96, local copies, waits for them, and re-layouts: 3 us -> 25 us
  transfers between devices with their start and end apart: 48 -> 48, of which waited for: 14 -> 13; matrix products, arithmetic and copies ran while one was open for 2% -> 0% of each run, Pallas kernels for 29% -> 22%
where the time goes in v2:
time: 526 us; the launch traced here: 525 us
  waiting for transfers between devices  309 us (59%)
  Pallas kernels  132 us (25%)
  blocking collectives  31.1 us (6%)
  local copies, waits for them, and re-layouts  26.3 us (5%)
  starting transfers between devices  24 us (5%)
    ppermute x15, waiting for transfers between devices, spread(): got.append(lax.ppermute(x, 'fsdp', step(k, 0)))  303 us
    pallas_call x10, Pallas kernels, narrow(): pl.pallas_call(functools.partial(narrow_kernel, first, at, len(tops)), ou...  53.5 us
    pallas_call x12, Pallas kernels, put(): pl.pallas_call(functools.partial(put_kernel, tuple(slots), piece, rows),...  47.9 us
    all_gather x1, blocking collectives, per_device(): wide_router = lax.all_gather(row_router, 'ep', axis=1, tiled=True)  31.1 us
    pallas_call x3, Pallas kernels, local_max(): pl.pallas_call(functools.partial(max_kernel, first), out_shape=jax.ShapeD...  25 us
    unnamed x96, local copies, waits for them, and re-layouts  25 us
    ppermute x15, starting transfers between devices, spread(): got.append(lax.ppermute(x, 'fsdp', step(k, 0)))  17.1 us
  transfers between devices with their start and end apart: 48, of which 13 were waited for; matrix products, arithmetic and copies ran while one was open for 0% of the time, Pallas kernels for 22%

profile of v2, /device:TPU:0, one launch (start us, length us, event | category | flops | bytes accessed | tf_op | source)
XLA Modules:
  0.0 525.4 jit_solution(8602163501551345965)
XLA Ops:
  1.3 12.7 %local_max.5.refs_0_.refs_12_ = f32[8,1024]{1,0:T(8,128)S(1)} custom-call(f32[8]{0:T(128)S(1)} %copy-done.36, f32[8,512,1024]{2,1,0:T(8,128)} %refs_4_.21, f32[8,512,1024]{2,1,0:T(8,128)} %refs_5_.21), custom_call_target="tpu_custom_call" | custom-call | flops 20971520 | bytes 33554432 | tf_op jit(solution)/shard_map/local_max/pallas_call | solution.py:94
  13.9 3.0 collective-permute-start.28
  17.0 2.3 first_max.1.refs_0_
  20.0 1.4 collective-permute-start.8
  22.0 3.9 local_max.4.refs_0_.refs_4_
  26.9 1.7 first_narrow.1.refs_0_
  28.6 1.7 collective-permute-start.25
  32.1 8.3 %narrow.15 = (bf16[3,512,1024]{2,1,0:T(8,128)(2,1)S(1)}, bf16[8,2048,1024]{2,1,0:T(8,128)(2,1)}) custom-call(s32[4]{0:T(128)S(1)} %get-tuple-element.52.place_ref, f32[8]{0:T(128)S(1)} %copy-done.37, f32[8,1024]{1,0:T(8,128)S(1)} %local_max.5.refs_0_.refs_12_, f32[8,1024]{1,0:T(8,128)S(1)} %collective-permute-done.27.refs_1_.refs_13_, ...), custom_call_target="tpu_custom_call" | custom-call | flops 9437184 | bytes 18874368 | tf_op jit(solution)/shard_map/narrow/pallas_call | solution.py:196
  40.4 1.6 copy-done.40
  42.0 8.3 %narrow.16 = (bf16[3,512,1024]{2,1,0:T(8,128)(2,1)S(1)}, bf16[8,2048,1024]{2,1,0:T(8,128)(2,1)}) custom-call(s32[4]{0:T(128)S(1)} %get-tuple-element.52.place_ref, f32[8]{0:T(128)S(1)} %copy-done.37, f32[8,1024]{1,0:T(8,128)S(1)} %local_max.5.refs_0_.refs_12_, ...), custom_call_target="tpu_custom_call", output_to_operand_aliasing={{1}: (8, {})} | custom-call | flops 9437184 | bytes 18874368 | tf_op jit(solution)/shard_map/narrow/pallas_call | solution.py:196
  50.4 1.6 copy-done.38
  52.0 3.8 narrow.17
  55.8 4.2 narrow.18
  59.9 2.6 narrow.19
  63.0 1.7 collective-permute-start.46
  64.7 8.4 %local_max.3.refs_0_.refs_8_ = f32[5,1024]{1,0:T(8,128)S(1)} custom-call(f32[8]{0:T(128)S(1)} %copy-done.37, f32[8,512,1024]{2,1,0:T(8,128)} %refs_4_.16, f32[8,512,1024]{2,1,0:T(8,128)} %refs_5_.16), custom_call_target="tpu_custom_call" | custom-call | flops 13107200 | bytes 20971520 | tf_op jit(solution)/shard_map/local_max/pallas_call | solution.py:94
  77.2 3.1 narrow.10
  82.3 3.8 narrow.11
  88.2 6.9 %collective-permute-done.22.refs_1_ = bf16[1,256,1024]{2,1,0:T(8,128)(2,1)S(1)} collective-permute-done((bf16[1,256,1024]{2,1,0:T(8,128)(2,1)S(1)}, bf16[1,256,1024]{2,1,0:T(8,128)(2,1)S(1)}, u32[]{:S(2)}, u32[]{:S(2)}) %collective-permute-start.22) | collective-permute-done | bytes 524320 | tf_op jit(solution)/shard_map/ppermute | solution.py:341
  95.6 3.9 narrow.12
  99.6 12.5 %collective-permute-done.34.refs_1_ = bf16[1,384,1024]{2,1,0:T(8,128)(2,1)} collective-permute-done((bf16[1,384,1024]{2,1,0:T(8,128)(2,1)S(1)}, bf16[1,384,1024]{2,1,0:T(8,128)(2,1)}, u32[]{:S(2)}, u32[]{:S(2)}) %collective-permute-start.34) | collective-permute-done | bytes 786464 | tf_op jit(solution)/shard_map/ppermute | solution.py:341
  113.8 9.2 %narrow.13 = (bf16[3,512,1024]{2,1,0:T(8,128)(2,1)}, bf16[8,2048,1024]{2,1,0:T(8,128)(2,1)}) custom-call(s32[4]{0:T(128)S(1)} %get-tuple-element.52.place_ref, f32[8]{0:T(128)S(1)} %copy-done.37, f32[5,1024]{1,0:T(8,128)S(1)} %local_max.3.refs_0_.refs_8_, f32[5,1024]{1,0:T(8,128)S(1)} %collective-permute-done.refs_1_.refs_9_, ...), custom_call_target="tpu_custom_call", output_to_operand_aliasing={{1}: (8, {})} | custom-call | flops 9437184 | bytes 18874368 | tf_op jit(solution)/shard_map/narrow/pallas_call | solution.py:196
  124.1 6.3 %narrow.14 = (bf16[2,512,1024]{2,1,0:T(8,128)(2,1)S(1)}, bf16[8,2048,1024]{2,1,0:T(8,128)(2,1)}) custom-call(s32[4]{0:T(128)S(1)} %get-tuple-element.52.place_ref, f32[8]{0:T(128)S(1)} %copy-done.37, f32[5,1024]{1,0:T(8,128)S(1)} %local_max.3.refs_0_.refs_8_, f32[5,1024]{1,0:T(8,128)S(1)} %collective-permute-done.refs_1_.refs_9_, ...), custom_call_target="tpu_custom_call", output_to_operand_aliasing={{1}: (8, {})} | custom-call | flops 6291456 | bytes 12582912 | tf_op jit(solution)/shard_map/narrow/pallas_call | solution.py:196
  130.5 3.9 collective-permute-done.19.refs_1_
  136.4 20.5 %collective-permute-done.16.refs_1_ = bf16[1,512,1024]{2,1,0:T(8,128)(2,1)S(1)} collective-permute-done((bf16[1,512,1024]{2,1,0:T(8,128)(2,1)}, bf16[1,512,1024]{2,1,0:T(8,128)(2,1)S(1)}, u32[]{:S(2)}, u32[]{:S(2)}) %collective-permute-start.16) | collective-permute-done | bytes 1048608 | tf_op jit(solution)/shard_map/ppermute | solution.py:341
  159.3 20.1 %collective-permute-done.37.refs_1_ = bf16[1,512,1024]{2,1,0:T(8,128)(2,1)} collective-permute-done((bf16[1,512,1024]{2,1,0:T(8,128)(2,1)S(1)}, bf16[1,512,1024]{2,1,0:T(8,128)(2,1)}, u32[]{:S(2)}, u32[]{:S(2)}) %collective-permute-start.37) | collective-permute-done | bytes 1048608 | tf_op jit(solution)/shard_map/ppermute | solution.py:341
  185.7 38.6 %collective-permute-done.10.refs_1_ = bf16[2,512,1024]{2,1,0:T(8,128)(2,1)S(1)} collective-permute-done((bf16[2,512,1024]{2,1,0:T(8,128)(2,1)S(1)}, bf16[2,512,1024]{2,1,0:T(8,128)(2,1)S(1)}, u32[]{:S(2)}, u32[]{:S(2)}) %collective-permute-start.10) | collective-permute-done | bytes 2097184 | tf_op jit(solution)/shard_map/ppermute | solution.py:341
  226.6 65.1 %collective-permute-done.13.refs_1_ = bf16[3,512,1024]{2,1,0:T(8,128)(2,1)S(1)} collective-permute-done((bf16[3,512,1024]{2,1,0:T(8,128)(2,1)}, bf16[3,512,1024]{2,1,0:T(8,128)(2,1)S(1)}, u32[]{:S(2)}, u32[]{:S(2)}) %collective-permute-start.13) | collective-permute-done | bytes 3145760 | tf_op jit(solution)/shard_map/ppermute | solution.py:341
  292.2 67.0 %collective-permute-done.43.refs_1_ = bf16[3,512,1024]{2,1,0:T(8,128)(2,1)} collective-permute-done((bf16[3,512,1024]{2,1,0:T(8,128)(2,1)}, bf16[3,512,1024]{2,1,0:T(8,128)(2,1)}, u32[]{:S(2)}, u32[]{:S(2)}) %collective-permute-start.43) | collective-permute-done | bytes 3145760 | tf_op jit(solution)/shard_map/ppermute | solution.py:341
  359.2 66.9 %collective-permute-done.40.refs_1_ = bf16[3,512,1024]{2,1,0:T(8,128)(2,1)} collective-permute-done((bf16[3,512,1024]{2,1,0:T(8,128)(2,1)S(1)}, bf16[3,512,1024]{2,1,0:T(8,128)(2,1)}, u32[]{:S(2)}, u32[]{:S(2)}) %collective-permute-start.40) | collective-permute-done | bytes 3145760 | tf_op jit(solution)/shard_map/ppermute | solution.py:341
  426.2 1.7 copy-done
  428.4 1.4 copy-done.6
  429.7 1.6 copy-done.2
  431.3 3.7 collective-permute-done.11.refs_2_
  435.2 1.8 copy-done.44
  440.0 31.1 %all_gather.3 = bf16[2048,64]{0,1:T(8,128)(2,1)S(1)} all-gather(bf16[2048,8]{0,1:T(8,128)(2,1)S(1)} %constant_dynamic-update-slice_fusion), channel_id=1, replica_groups=mesh['ep'=8,'fsdp'=4] {'ep'}, dimensions={1}, use_global_device_ids=true | all-gather | bytes 294912 | tf_op jit(solution)/shard_map/all_gather | solution.py:389
  476.6 2.1 put.12.refs_3_
  478.8 1.8 put.13.refs_3_
  481.2 2.5 put.14.refs_3_
  483.7 2.5 put.15.refs_3_
  486.2 7.8 %put.16.refs_3_ = bf16[8,2048,1024]{2,1,0:T(8,128)(2,1)} custom-call(s32[4]{0:T(128)S(1)} %get-tuple-element.52.place_ref, bf16[3,512,1024]{2,1,0:T(8,128)(2,1)S(1)} %collective-permute-done.12.refs_0_, bf16[3,512,1024]{2,1,0:T(8,128)(2,1)} %copy-done.43, bf16[3,512,1024]{2,1,0:T(8,128)(2,1)} %copy-done.44, ...), custom_call_target="tpu_custom_call", output_to_operand_aliasing={{}: (4, {})} | custom-call | flops 4718592 | bytes 18874368 | tf_op jit(solution)/shard_map/put/pallas_call | solution.py:249
  494.0 5.1 put.17
  499.1 7.6 %put.18.refs_3_ = bf16[8,2048,1024]{2,1,0:T(8,128)(2,1)} custom-call(s32[4]{0:T(128)S(1)} %get-tuple-element.52.place_ref, bf16[3,512,1024]{2,1,0:T(8,128)(2,1)S(1)} %copy-done.1, bf16[3,512,1024]{2,1,0:T(8,128)(2,1)} %collective-permute-done.43.refs_1_, bf16[3,512,1024]{2,1,0:T(8,128)(2,1)} %collective-permute-done.44.refs_2_, ...), custom_call_target="tpu_custom_call", output_to_operand_aliasing={{}: (4, {})} | custom-call | flops 4718592 | bytes 18874368 | tf_op jit(solution)/shard_map/put/pallas_call | solution.py:249
  506.7 7.3 %put.19.refs_3_ = bf16[8,2048,1024]{2,1,0:T(8,128)(2,1)} custom-call(s32[4]{0:T(128)S(1)} %get-tuple-element.52.place_ref, bf16[3,512,1024]{2,1,0:T(8,128)(2,1)S(1)} %copy-done.3, bf16[3,512,1024]{2,1,0:T(8,128)(2,1)} %collective-permute-done.40.refs_1_, bf16[3,512,1024]{2,1,0:T(8,128)(2,1)} %collective-permute-done.41.refs_2_, ...), custom_call_target="tpu_custom_call", output_to_operand_aliasing={{}: (4, {})} | custom-call | flops 4718592 | bytes 18874368 | tf_op jit(solution)/shard_map/put/pallas_call | solution.py:249
  514.1 3.6 put.20.refs_3_
  517.7 3.1 put.21.refs_2_
  520.8 2.3 put.22.refs_1_
  523.2 2.2 put.23
  (181 shorter events, 37.4 us)
Async XLA Ops:
  13.9 16.3 %collective-permute-start.28 = (f32[8,1024]{1,0:T(8,128)S(1)}, f32[8,1024]{1,0:T(8,128)S(1)}, u32[]{:S(2)}, u32[]{:S(2)}) collective-permute-start(f32[8,1024]{1,0:T(8,128)S(1)} %local_max.5.refs_0_.refs_12_), channel_id=1, source_target_pairs={{0,2},{1,3},{2,0},{3,1},{4,6},{5,7},{6,4},{7,5},{8,10},{9,11},{10,... | collective-permute-start | bytes 98312 | tf_op jit(solution)/shard_map/ppermute | solution.py:341
  17.0 14.6 %collective-permute-start.27 = (f32[8,1024]{1,0:T(8,128)S(1)}, f32[8,1024]{1,0:T(8,128)S(1)}, u32[]{:S(2)}, u32[]{:S(2)}) collective-permute-start(f32[8,1024]{1,0:T(8,128)S(1)} %local_max.5.refs_0_.refs_12_), channel_id=1, source_target_pairs={{0,1},{1,0},{2,3},{3,2},{4,5},{5,4},{6,7},{7,6},{8,9},{9,8},{10,11... | collective-permute-start | bytes 98312 | tf_op jit(solution)/shard_map/ppermute | solution.py:339
  19.3 6.6 %collective-permute-start.6 = (f32[1,1024]{1,0:T(1,128)S(1)}, f32[1,1024]{1,0:T(1,128)S(1)}, u32[]{:S(2)}, u32[]{:S(2)}) collective-permute-start(f32[1,1024]{1,0:T(1,128)S(1)} %first_max.1.refs_0_), channel_id=1, source_target_pairs={{0,1},{1,0},{2,3},{3,2},{4,5},{5,4},{6,7},{7,6},{8,9},{9,8},{10,11... | collective-permute-start | bytes 12296 | tf_op jit(solution)/shard_map/ppermute | solution.py:362
  19.9 6.7 %collective-permute-start.7 = (f32[1,1024]{1,0:T(1,128)S(1)}, f32[1,1024]{1,0:T(1,128)S(1)}, u32[]{:S(2)}, u32[]{:S(2)}) collective-permute-start(f32[1,1024]{1,0:T(1,128)S(1)} %first_max.1.refs_0_), channel_id=1, source_target_pairs={{0,2},{1,3},{2,0},{3,1},{4,6},{5,7},{6,4},{7,5},{8,10},{9,11},{10,... | collective-permute-start | bytes 12296 | tf_op jit(solution)/shard_map/ppermute | solution.py:362
  20.0 6.9 %collective-permute-start.8 = (f32[1,1024]{1,0:T(1,128)S(1)}, f32[1,1024]{1,0:T(1,128)S(1)}, u32[]{:S(2)}, u32[]{:S(2)}) collective-permute-start(f32[1,1024]{1,0:T(1,128)S(1)} %first_max.1.refs_0_), channel_id=1, source_target_pairs={{0,3},{1,2},{2,1},{3,0},{4,7},{5,6},{6,5},{7,4},{8,11},{9,10},{10,... | collective-permute-start | bytes 12296 | tf_op jit(solution)/shard_map/ppermute | solution.py:362
  26.0 36.9 %collective-permute-start.4 = (f32[2,1024]{1,0:T(2,128)S(1)}, f32[2,1024]{1,0:T(2,128)S(1)}, u32[]{:S(2)}, u32[]{:S(2)}) collective-permute-start(f32[2,1024]{1,0:T(2,128)S(1)} %local_max.4.refs_0_.refs_4_), channel_id=1, source_target_pairs={{0,2},{1,3},{2,0},{3,1},{4,6},{5,7},{6,4},{7,5},{8,10},{9,11},{10,... | collective-permute-start | bytes 24584 | tf_op jit(solution)/shard_map/ppermute | solution.py:341
  26.7 36.4 %collective-permute-start.3 = (f32[2,1024]{1,0:T(2,128)S(1)}, f32[2,1024]{1,0:T(2,128)S(1)}, u32[]{:S(2)}, u32[]{:S(2)}) collective-permute-start(f32[2,1024]{1,0:T(2,128)S(1)} %local_max.4.refs_0_.refs_4_), channel_id=1, source_target_pairs={{0,1},{1,0},{2,3},{3,2},{4,5},{5,4},{6,7},{7,6},{8,9},{9,8},{10,11... | collective-permute-start | bytes 24584 | tf_op jit(solution)/shard_map/ppermute | solution.py:339
  28.6 57.5 %collective-permute-start.25 = (bf16[1,256,1024]{2,1,0:T(8,128)(2,1)S(1)}, bf16[1,256,1024]{2,1,0:T(8,128)(2,1)S(1)}, u32[]{:S(2)}, u32[]{:S(2)}) collective-permute-start(bf16[1,256,1024]{2,1,0:T(8,128)(2,1)S(1)} %first_narrow.1.refs_0_), channel_id=1, source_target_pairs={{0,2},{1,3},{2,0},{3,1},{4,6},{5,7},{6,4},{7,5},{8,10},{9,11},{10,... | collective-permute-start | bytes 1572872 | tf_op jit(solution)/shard_map/ppermute | solution.py:341
  30.3 1.8 collective-permute-start.29
  31.5 55.6 %collective-permute-start.24 = (bf16[1,256,1024]{2,1,0:T(8,128)(2,1)S(1)}, bf16[1,256,1024]{2,1,0:T(8,128)(2,1)S(1)}, u32[]{:S(2)}, u32[]{:S(2)}) collective-permute-start(bf16[1,256,1024]{2,1,0:T(8,128)(2,1)S(1)} %first_narrow.1.refs_0_), channel_id=1, source_target_pairs={{0,1},{1,0},{2,3},{3,2},{4,5},{5,4},{6,7},{7,6},{8,9},{9,8},{10,11... | collective-permute-start | bytes 1572872 | tf_op jit(solution)/shard_map/ppermute | solution.py:339
  62.5 19.8 %collective-permute-start.30 = (bf16[1,128,1024]{2,1,0:T(8,128)(2,1)S(1)}, bf16[1,128,1024]{2,1,0:T(8,128)(2,1)}, u32[]{:S(2)}, u32[]{:S(2)}) collective-permute-start(bf16[1,128,1024]{2,1,0:T(8,128)(2,1)S(1)} %get-tuple-element.41), channel_id=1, source_target_pairs={{0,2},{1,3},{2,0},{3,1},{4,6},{5,7},{6,4},{7,5},{8,10},{9,11},{10,... | collective-permute-start | bytes 786440 | tf_op jit(solution)/shard_map/ppermute | solution.py:341
  62.9 10.2 %collective-permute-start.45 = (bf16[512,8]{0,1:T(8,128)(2,1)S(1)}, bf16[512,8]{0,1:T(8,128)(2,1)S(1)}, u32[]{:S(2)}, u32[]{:S(2)}) collective-permute-start(bf16[512,8]{0,1:T(8,128)(2,1)S(1)} %get-tuple-element.50), channel_id=1, source_target_pairs={{0,1},{1,0},{2,3},{3,2},{4,5},{5,4},{6,7},{7,6},{8,9},{9,8},{10,11... | collective-permute-start | bytes 24584 | tf_op jit(solution)/shard_map/ppermute | solution.py:339
  63.0 10.6 %collective-permute-start.46 = (bf16[512,8]{0,1:T(8,128)(2,1)S(1)}, bf16[512,8]{0,1:T(8,128)(2,1)S(1)}, u32[]{:S(2)}, u32[]{:S(2)}) collective-permute-start(bf16[512,8]{0,1:T(8,128)(2,1)S(1)} %get-tuple-element.50), channel_id=1, source_target_pairs={{0,2},{1,3},{2,0},{3,1},{4,6},{5,7},{6,4},{7,5},{8,10},{9,11},{10,... | collective-permute-start | bytes 24584 | tf_op jit(solution)/shard_map/ppermute | solution.py:341
  73.2 4.0 collective-permute-start.1
  73.6 1.2 collective-permute-start.5
  74.8 1.2 collective-permute-start.47
  76.0 4.3 collective-permute-start
  77.2 4.1 collective-permute-start.2
  80.3 14.8 %collective-permute-start.22 = (bf16[1,256,1024]{2,1,0:T(8,128)(2,1)S(1)}, bf16[1,256,1024]{2,1,0:T(8,128)(2,1)S(1)}, u32[]{:S(2)}, u32[]{:S(2)}) collective-permute-start(bf16[1,256,1024]{2,1,0:T(8,128)(2,1)S(1)} %get-tuple-element.35), channel_id=1, source_target_pairs={{0,2},{1,3},{2,0},{3,1},{4,6},{5,7},{6,4},{7,5},{8,10},{9,11},{10,... | collective-permute-start | bytes 1572872 | tf_op jit(solution)/shard_map/ppermute | solution.py:341
  81.2 30.8 %collective-permute-start.34 = (bf16[1,384,1024]{2,1,0:T(8,128)(2,1)S(1)}, bf16[1,384,1024]{2,1,0:T(8,128)(2,1)}, u32[]{:S(2)}, u32[]{:S(2)}) collective-permute-start(bf16[1,384,1024]{2,1,0:T(8,128)(2,1)S(1)} %get-tuple-element.42), channel_id=1, source_target_pairs={{0,2},{1,3},{2,0},{3,1},{4,6},{5,7},{6,4},{7,5},{8,10},{9,11},{10,... | collective-permute-start | bytes 2359304 | tf_op jit(solution)/shard_map/ppermute | solution.py:341
  82.3 12.8 %collective-permute-start.21 = (bf16[1,256,1024]{2,1,0:T(8,128)(2,1)S(1)}, bf16[1,256,1024]{2,1,0:T(8,128)(2,1)S(1)}, u32[]{:S(2)}, u32[]{:S(2)}) collective-permute-start(bf16[1,256,1024]{2,1,0:T(8,128)(2,1)S(1)} %get-tuple-element.35), channel_id=1, source_target_pairs={{0,1},{1,0},{2,3},{3,2},{4,5},{5,4},{6,7},{7,6},{8,9},{9,8},{10,11... | collective-permute-start | bytes 1572872 | tf_op jit(solution)/shard_map/ppermute | solution.py:339
  86.1 48.3 %collective-permute-start.19 = (bf16[1,512,1024]{2,1,0:T(8,128)(2,1)S(1)}, bf16[1,512,1024]{2,1,0:T(8,128)(2,1)S(1)}, u32[]{:S(2)}, u32[]{:S(2)}) collective-permute-start(bf16[1,512,1024]{2,1,0:T(8,128)(2,1)S(1)} %get-tuple-element.34), channel_id=1, source_target_pairs={{0,2},{1,3},{2,0},{3,1},{4,6},{5,7},{6,4},{7,5},{8,10},{9,11},{10,... | collective-permute-start | bytes 3145736 | tf_op jit(solution)/shard_map/ppermute | solution.py:341
  87.9 25.1 %collective-permute-start.26 = (bf16[1,256,1024]{2,1,0:T(8,128)(2,1)S(1)}, bf16[1,256,1024]{2,1,0:T(8,128)(2,1)S(1)}, u32[]{:S(2)}, u32[]{:S(2)}) collective-permute-start(bf16[1,256,1024]{2,1,0:T(8,128)(2,1)S(1)} %collective-permute-done.25.refs_2_), channel_id=1, source_target_pairs={{0,1},{1,0},{2,3},{3,2},{4,5},{5,4},{6,7},{7,6},{8,9},{9,8},{10,11... | collective-permute-start | bytes 1572872 | tf_op jit(solution)/shard_map/ppermute | solution.py:343
  95.1 40.3 %collective-permute-start.18 = (bf16[1,512,1024]{2,1,0:T(8,128)(2,1)S(1)}, bf16[1,512,1024]{2,1,0:T(8,128)(2,1)S(1)}, u32[]{:S(2)}, u32[]{:S(2)}) collective-permute-start(bf16[1,512,1024]{2,1,0:T(8,128)(2,1)S(1)} %get-tuple-element.34), channel_id=1, source_target_pairs={{0,1},{1,0},{2,3},{3,2},{4,5},{5,4},{6,7},{7,6},{8,9},{9,8},{10,11... | collective-permute-start | bytes 3145736 | tf_op jit(solution)/shard_map/ppermute | solution.py:339
  95.1 27.9 %collective-permute-start.23 = (bf16[1,256,1024]{2,1,0:T(8,128)(2,1)S(1)}, bf16[1,256,1024]{2,1,0:T(8,128)(2,1)S(1)}, u32[]{:S(2)}, u32[]{:S(2)}) collective-permute-start(bf16[1,256,1024]{2,1,0:T(8,128)(2,1)S(1)} %collective-permute-done.22.refs_1_), channel_id=1, source_target_pairs={{0,1},{1,0},{2,3},{3,2},{4,5},{5,4},{6,7},{7,6},{8,9},{9,8},{10,11... | collective-permute-start | bytes 1572872 | tf_op jit(solution)/shard_map/ppermute | solution.py:343
  112.0 44.8 %collective-permute-start.16 = (bf16[1,512,1024]{2,1,0:T(8,128)(2,1)}, bf16[1,512,1024]{2,1,0:T(8,128)(2,1)S(1)}, u32[]{:S(2)}, u32[]{:S(2)}) collective-permute-start(bf16[1,512,1024]{2,1,0:T(8,128)(2,1)} %get-tuple-element.33), channel_id=1, source_target_pairs={{0,2},{1,3},{2,0},{3,1},{4,6},{5,7},{6,4},{7,5},{8,10},{9,11},{10,... | collective-permute-start | bytes 3145736 | tf_op jit(solution)/shard_map/ppermute | solution.py:341
  113.8 43.1 %collective-permute-start.15 = (bf16[1,512,1024]{2,1,0:T(8,128)(2,1)}, bf16[1,512,1024]{2,1,0:T(8,128)(2,1)S(1)}, u32[]{:S(2)}, u32[]{:S(2)}) collective-permute-start(bf16[1,512,1024]{2,1,0:T(8,128)(2,1)} %get-tuple-element.33), channel_id=1, source_target_pairs={{0,1},{1,0},{2,3},{3,2},{4,5},{5,4},{6,7},{7,6},{8,9},{9,8},{10,11... | collective-permute-start | bytes 3145736 | tf_op jit(solution)/shard_map/ppermute | solution.py:339
  123.0 56.4 %collective-permute-start.37 = (bf16[1,512,1024]{2,1,0:T(8,128)(2,1)S(1)}, bf16[1,512,1024]{2,1,0:T(8,128)(2,1)}, u32[]{:S(2)}, u32[]{:S(2)}) collective-permute-start(bf16[1,512,1024]{2,1,0:T(8,128)(2,1)S(1)} %get-tuple-element.43), channel_id=1, source_target_pairs={{0,2},{1,3},{2,0},{3,1},{4,6},{5,7},{6,4},{7,5},{8,10},{9,11},{10,... | collective-permute-start | bytes 3145736 | tf_op jit(solution)/shard_map/ppermute | solution.py:341
  134.4 89.9 %collective-permute-start.10 = (bf16[2,512,1024]{2,1,0:T(8,128)(2,1)S(1)}, bf16[2,512,1024]{2,1,0:T(8,128)(2,1)S(1)}, u32[]{:S(2)}, u32[]{:S(2)}) collective-permute-start(bf16[2,512,1024]{2,1,0:T(8,128)(2,1)S(1)} %get-tuple-element.31), channel_id=1, source_target_pairs={{0,2},{1,3},{2,0},{3,1},{4,6},{5,7},{6,4},{7,5},{8,10},{9,11},{10,... | collective-permute-start | bytes 6291464 | tf_op jit(solution)/shard_map/ppermute | solution.py:341
  136.4 44.1 %collective-permute-start.36 = (bf16[1,512,1024]{2,1,0:T(8,128)(2,1)S(1)}, bf16[1,512,1024]{2,1,0:T(8,128)(2,1)S(1)}, u32[]{:S(2)}, u32[]{:S(2)}) collective-permute-start(bf16[1,512,1024]{2,1,0:T(8,128)(2,1)S(1)} %get-tuple-element.43), channel_id=1, source_target_pairs={{0,1},{1,0},{2,3},{3,2},{4,5},{5,4},{6,7},{7,6},{8,9},{9,8},{10,11... | collective-permute-start | bytes 3145736 | tf_op jit(solution)/shard_map/ppermute | solution.py:339
  156.9 68.4 %collective-permute-start.9 = (bf16[2,512,1024]{2,1,0:T(8,128)(2,1)S(1)}, bf16[2,512,1024]{2,1,0:T(8,128)(2,1)S(1)}, u32[]{:S(2)}, u32[]{:S(2)}) collective-permute-start(bf16[2,512,1024]{2,1,0:T(8,128)(2,1)S(1)} %get-tuple-element.31), channel_id=1, source_target_pairs={{0,1},{1,0},{2,3},{3,2},{4,5},{5,4},{6,7},{7,6},{8,9},{9,8},{10,11... | collective-permute-start | bytes 6291464 | tf_op jit(solution)/shard_map/ppermute | solution.py:339
  157.8 24.5 %collective-permute-start.20 = (bf16[1,512,1024]{2,1,0:T(8,128)(2,1)S(1)}, bf16[1,512,1024]{2,1,0:T(8,128)(2,1)S(1)}, u32[]{:S(2)}, u32[]{:S(2)}) collective-permute-start(bf16[1,512,1024]{2,1,0:T(8,128)(2,1)S(1)} %collective-permute-done.19.refs_1_), channel_id=1, source_target_pairs={{0,1},{1,0},{2,3},{3,2},{4,5},{5,4},{6,7},{7,6},{8,9},{9,8},{10,11... | collective-permute-start | bytes 3145736 | tf_op jit(solution)/shard_map/ppermute | solution.py:343
  179.4 4.2 collective-permute-start.17
  181.4 110.3 %collective-permute-start.13 = (bf16[3,512,1024]{2,1,0:T(8,128)(2,1)}, bf16[3,512,1024]{2,1,0:T(8,128)(2,1)S(1)}, u32[]{:S(2)}, u32[]{:S(2)}) collective-permute-start(bf16[3,512,1024]{2,1,0:T(8,128)(2,1)} %get-tuple-element.32), channel_id=1, source_target_pairs={{0,2},{1,3},{2,0},{3,1},{4,6},{5,7},{6,4},{7,5},{8,10},{9,11},{10,... | collective-permute-start | bytes 9437192 | tf_op jit(solution)/shard_map/ppermute | solution.py:341
  183.4 108.3 %collective-permute-start.12 = (bf16[3,512,1024]{2,1,0:T(8,128)(2,1)}, bf16[3,512,1024]{2,1,0:T(8,128)(2,1)S(1)}, u32[]{:S(2)}, u32[]{:S(2)}) collective-permute-start(bf16[3,512,1024]{2,1,0:T(8,128)(2,1)} %get-tuple-element.32), channel_id=1, source_target_pairs={{0,1},{1,0},{2,3},{3,2},{4,5},{5,4},{6,7},{7,6},{8,9},{9,8},{10,11... | collective-permute-start | bytes 9437192 | tf_op jit(solution)/shard_map/ppermute | solution.py:339
  184.6 174.6 %collective-permute-start.43 = (bf16[3,512,1024]{2,1,0:T(8,128)(2,1)}, bf16[3,512,1024]{2,1,0:T(8,128)(2,1)}, u32[]{:S(2)}, u32[]{:S(2)}) collective-permute-start(bf16[3,512,1024]{2,1,0:T(8,128)(2,1)} %copy-done.40), channel_id=1, source_target_pairs={{0,2},{1,3},{2,0},{3,1},{4,6},{5,7},{6,4},{7,5},{8,10},{9,11},{10,... | collective-permute-start | bytes 9437192 | tf_op jit(solution)/shard_map/ppermute | solution.py:341
  224.3 201.9 %collective-permute-start.40 = (bf16[3,512,1024]{2,1,0:T(8,128)(2,1)S(1)}, bf16[3,512,1024]{2,1,0:T(8,128)(2,1)}, u32[]{:S(2)}, u32[]{:S(2)}) collective-permute-start(bf16[3,512,1024]{2,1,0:T(8,128)(2,1)S(1)} %copy-done.39), channel_id=1, source_target_pairs={{0,2},{1,3},{2,0},{3,1},{4,6},{5,7},{6,4},{7,5},{8,10},{9,11},{10,... | collective-permute-start | bytes 9437192 | tf_op jit(solution)/shard_map/ppermute | solution.py:341
  226.6 199.6 %collective-permute-start.42 = (bf16[3,512,1024]{2,1,0:T(8,128)(2,1)}, bf16[3,512,1024]{2,1,0:T(8,128)(2,1)S(1)}, u32[]{:S(2)}, u32[]{:S(2)}) collective-permute-start(bf16[3,512,1024]{2,1,0:T(8,128)(2,1)} %copy-done.40), channel_id=1, source_target_pairs={{0,1},{1,0},{2,3},{3,2},{4,5},{5,4},{6,7},{7,6},{8,9},{9,8},{10,11... | collective-permute-start | bytes 9437192 | tf_op jit(solution)/shard_map/ppermute | solution.py:339
  291.7 138.0 %collective-permute-start.39 = (bf16[3,512,1024]{2,1,0:T(8,128)(2,1)S(1)}, bf16[3,512,1024]{2,1,0:T(8,128)(2,1)S(1)}, u32[]{:S(2)}, u32[]{:S(2)}) collective-permute-start(bf16[3,512,1024]{2,1,0:T(8,128)(2,1)S(1)} %copy-done.39), channel_id=1, source_target_pairs={{0,1},{1,0},{2,3},{3,2},{4,5},{5,4},{6,7},{7,6},{8,9},{9,8},{10,11... | collective-permute-start | bytes 9437192 | tf_op jit(solution)/shard_map/ppermute | solution.py:339
  291.7 143.5 %collective-permute-start.14 = (bf16[3,512,1024]{2,1,0:T(8,128)(2,1)S(1)}, bf16[3,512,1024]{2,1,0:T(8,128)(2,1)S(1)}, u32[]{:S(2)}, u32[]{:S(2)}) collective-permute-start(bf16[3,512,1024]{2,1,0:T(8,128)(2,1)S(1)} %collective-permute-done.13.refs_1_), channel_id=1, source_target_pairs={{0,1},{1,0},{2,3},{3,2},{4,5},{5,4},{6,7},{7,6},{8,9},{9,8},{10,11... | collective-permute-start | bytes 9437192 | tf_op jit(solution)/shard_map/ppermute | solution.py:343
  359.2 80.2 %collective-permute-start.44 = (bf16[3,512,1024]{2,1,0:T(8,128)(2,1)}, bf16[3,512,1024]{2,1,0:T(8,128)(2,1)}, u32[]{:S(2)}, u32[]{:S(2)}) collective-permute-start(bf16[3,512,1024]{2,1,0:T(8,128)(2,1)} %collective-permute-done.43.refs_1_), channel_id=1, source_target_pairs={{0,1},{1,0},{2,3},{3,2},{4,5},{5,4},{6,7},{7,6},{8,9},{9,8},{10,11... | collective-permute-start | bytes 9437192 | tf_op jit(solution)/shard_map/ppermute | solution.py:343
  426.1 13.4 %collective-permute-start.41 = (bf16[3,512,1024]{2,1,0:T(8,128)(2,1)}, bf16[3,512,1024]{2,1,0:T(8,128)(2,1)}, u32[]{:S(2)}, u32[]{:S(2)}) collective-permute-start(bf16[3,512,1024]{2,1,0:T(8,128)(2,1)} %collective-permute-done.40.refs_1_), channel_id=1, source_target_pairs={{0,1},{1,0},{2,3},{3,2},{4,5},{5,4},{6,7},{7,6},{8,9},{9,8},{10,11... | collective-permute-start | bytes 9437192 | tf_op jit(solution)/shard_map/ppermute | solution.py:343
  427.8 7.2 %collective-permute-start.11 = (bf16[2,512,1024]{2,1,0:T(8,128)(2,1)S(1)}, bf16[2,512,1024]{2,1,0:T(8,128)(2,1)S(1)}, u32[]{:S(2)}, u32[]{:S(2)}) collective-permute-start(bf16[2,512,1024]{2,1,0:T(8,128)(2,1)S(1)} %collective-permute-done.10.refs_1_), channel_id=1, source_target_pairs={{0,1},{1,0},{2,3},{3,2},{4,5},{5,4},{6,7},{7,6},{8,9},{9,8},{10,11... | collective-permute-start | bytes 6291464 | tf_op jit(solution)/shard_map/ppermute | solution.py:343
  431.3 82.7 %collective-permute-start.38 = (bf16[1,512,1024]{2,1,0:T(8,128)(2,1)}, bf16[1,512,1024]{2,1,0:T(8,128)(2,1)}, u32[]{:S(2)}, u32[]{:S(2)}) collective-permute-start(bf16[1,512,1024]{2,1,0:T(8,128)(2,1)} %collective-permute-done.37.refs_1_), channel_id=1, source_target_pairs={{0,1},{1,0},{2,3},{3,2},{4,5},{5,4},{6,7},{7,6},{8,9},{9,8},{10,11... | collective-permute-start | bytes 3145736 | tf_op jit(solution)/shard_map/ppermute | solution.py:343
  435.0 82.6 %collective-permute-start.33 = (bf16[1,384,1024]{2,1,0:T(8,128)(2,1)}, bf16[1,384,1024]{2,1,0:T(8,128)(2,1)}, u32[]{:S(2)}, u32[]{:S(2)}) collective-permute-start(bf16[1,384,1024]{2,1,0:T(8,128)(2,1)} %copy-done.41), channel_id=1, source_target_pairs={{0,1},{1,0},{2,3},{3,2},{4,5},{5,4},{6,7},{7,6},{8,9},{9,8},{10,11... | collective-permute-start | bytes 2359304 | tf_op jit(solution)/shard_map/ppermute | solution.py:339
  437.0 80.7 %collective-permute-start.35 = (bf16[1,384,1024]{2,1,0:T(8,128)(2,1)}, bf16[1,384,1024]{2,1,0:T(8,128)(2,1)}, u32[]{:S(2)}, u32[]{:S(2)}) collective-permute-start(bf16[1,384,1024]{2,1,0:T(8,128)(2,1)} %collective-permute-done.34.refs_1_), channel_id=1, source_target_pairs={{0,1},{1,0},{2,3},{3,2},{4,5},{5,4},{6,7},{7,6},{8,9},{9,8},{10,11... | collective-permute-start | bytes 2359304 | tf_op jit(solution)/shard_map/ppermute | solution.py:343
  439.4 81.4 %collective-permute-start.32 = (bf16[1,128,1024]{2,1,0:T(8,128)(2,1)}, bf16[1,128,1024]{2,1,0:T(8,128)(2,1)}, u32[]{:S(2)}, u32[]{:S(2)}) collective-permute-start(bf16[1,128,1024]{2,1,0:T(8,128)(2,1)} %copy-done.42), channel_id=1, source_target_pairs={{0,1},{1,0},{2,3},{3,2},{4,5},{5,4},{6,7},{7,6},{8,9},{9,8},{10,11... | collective-permute-start | bytes 786440 | tf_op jit(solution)/shard_map/ppermute | solution.py:339
  439.6 83.6 %collective-permute-start.31 = (bf16[1,128,1024]{2,1,0:T(8,128)(2,1)}, bf16[1,128,1024]{2,1,0:T(8,128)(2,1)}, u32[]{:S(2)}, u32[]{:S(2)}) collective-permute-start(bf16[1,128,1024]{2,1,0:T(8,128)(2,1)} %collective-permute-done.30.refs_1_), channel_id=1, source_target_pairs={{0,1},{1,0},{2,3},{3,2},{4,5},{5,4},{6,7},{7,6},{8,9},{9,8},{10,11... | collective-permute-start | bytes 786440 | tf_op jit(solution)/shard_map/ppermute | solution.py:343
  (48 other events, 457.5 us)

commit v3 on v2

--- a/solution.py
+++ b/solution.py
@@ -1,4 +1,5 @@
 import functools
+import math
 
 import jax
 import jax.numpy as jnp
@@ -32,7 +33,7 @@
     ]
 
 
-def first_max_kernel(first, blocks, mix_ref, train_ref, other_ref, top_ref, share_ref, held, sems, mix_sem):
+def first_max_kernel(first, blocks, mix_ref, train_ref, other_ref, top_ref, early_ref, share_ref, held, early, sems, mix_sem, early_sem):
     rows = held.shape[1]
     step = rows // blocks
     copies = fetches(first, 0, rows, blocks, (train_ref, other_ref), held, sems)
@@ -44,6 +45,7 @@
     mix.wait()
     share = share_ref[first]
     top = jnp.zeros((SUB, held.shape[2]), jnp.float32)
+    leave = pltpu.make_async_copy(early, early_ref, early_sem)
     for j, pair in enumerate(copies):
         for copy in pair:
             copy.wait()
@@ -52,21 +54,37 @@
             at = pl.ds(pl.multiple_of(j * step + i * SUB, SUB), SUB)
             return jnp.maximum(top, jnp.abs(mixed(share, held[0, at], held[1, at])))
 
+        def mix_rows(i, carry):
+            at = pl.ds(pl.multiple_of(i * SUB, SUB), SUB)
+            early[at] = mixed(share, held[0, at], held[1, at])
+            return carry
+
+        if j == 0:
+            lax.fori_loop(0, early.shape[0] // SUB, mix_rows, 0, unroll=2)
         top = lax.fori_loop(0, step // SUB, body, top, unroll=4)
+        if j == 1:
+            leave.start()
     top_ref[...] = jnp.max(top, axis=0, keepdims=True)
-
-
-def first_max(mix_share, train, other, first):
+    leave.wait()
+
+
+def first_max(mix_share, train, other, first, early):
     _, rows, cols = train.shape
     blocks = 4
     return pl.pallas_call(
         functools.partial(first_max_kernel, first, blocks),
-        out_shape=jax.ShapeDtypeStruct((1, cols), jnp.float32),
+        out_shape=(
+            jax.ShapeDtypeStruct((1, cols), jnp.float32),
+            jax.ShapeDtypeStruct((early, cols), jnp.float32),
+        ),
         in_specs=[HBM, HBM, HBM],
+        out_specs=(pl.BlockSpec(memory_space=pltpu.VMEM), ANY),
         scratch_shapes=[
             pltpu.SMEM(mix_share.shape, jnp.float32),
             pltpu.VMEM((2, rows, cols), jnp.float32),
+            pltpu.VMEM((early, cols), jnp.float32),
             pltpu.SemaphoreType.DMA((2, blocks)),
+            pltpu.SemaphoreType.DMA,
             pltpu.SemaphoreType.DMA,
         ],
         compiler_params=PARAMS,
@@ -189,8 +207,8 @@
 def narrow(place, mix_share, tops, at, train, other, piece, parts, whole):
     first, count, low, height = piece
     experts, rows, cols = train.shape
-    step = max(d for d in (height, height // 2) if d <= 256 or d == height // 2)
-    step = step if low % step == 0 and rows % step == 0 else rows // 4
+    common = math.gcd(height, low, rows)
+    step = max(d for d in range(16, min(common, 256) + 1, 16) if common % d == 0)
     block = pl.BlockSpec((1, step, cols), lambda e, r, place: (first + e, low // step + r, 0))
     held = [] if whole is None else [whole]
     return pl.pallas_call(
@@ -221,6 +239,44 @@
         ),
         name="narrow",
     )(place, mix_share, *tops, train, other, *held)
+
+
+def finish_kernel(parts, place_ref, *refs):
+    tops, rows, whole_ref = refs[:parts], refs[parts : 2 * parts], refs[-1]
+    scale = jnp.broadcast_to(1.0 / top_of(tops, 0), (2 * SUB, whole_ref.shape[2]))
+    for j in range(parts):
+
+        @pl.when(pl.program_id(0) == j)
+        def _():
+            def body(i, carry):
+                at = pl.ds(pl.multiple_of(i * 2 * SUB, 2 * SUB), 2 * SUB)
+                whole_ref[0, at] = (rows[j][at] * scale).astype(jnp.bfloat16)
+                return carry
+
+            lax.fori_loop(0, whole_ref.shape[1] // (2 * SUB), body, 0)
+
+
+def finish(place, tops, mixed_rows, expert, rows, whole):
+    early, cols = mixed_rows[0].shape
+    parts = len(mixed_rows)
+    return pl.pallas_call(
+        functools.partial(finish_kernel, parts),
+        out_shape=jax.ShapeDtypeStruct(whole.shape, whole.dtype),
+        grid_spec=pltpu.PrefetchScalarGridSpec(
+            num_scalar_prefetch=1,
+            grid=(parts,),
+            in_specs=[pl.BlockSpec((1, cols), lambda j, place: (0, 0))] * parts
+            + [pl.BlockSpec((early, cols), lambda j, place: (0, 0))] * parts
+            + [ANY],
+            out_specs=pl.BlockSpec((1, early, cols), lambda j, place: (expert, place[j] * (rows // early), 0)),
+        ),
+        input_output_aliases={1 + 2 * parts: 0},
+        compiler_params=PARAMS,
+        cost_estimate=pl.CostEstimate(
+            flops=2 * parts * early * cols, bytes_accessed=6 * parts * early * cols, transcendentals=0
+        ),
+        name="finish",
+    )(place, *tops, *mixed_rows, whole)
 
 
 def put_kernel(slots, piece, rows, place_ref, *refs):
@@ -302,25 +358,29 @@
     def runs(lo, hi, most):
         return [(e, min(most, hi - e)) for e in range(lo, hi, most)]
 
-    def split(cut):
-        return [(0, cut), (cut, rows - cut)]
-
     groups = [(0, 0, 1)]
     groups += [(0, e, n) for e, n in runs(1, min(3, experts), 2)]
     groups += [(0, e, n) for e, n in runs(3, experts, experts)]
     groups += [(1, 0, experts)]
-    pieces = [(0, (0, 1, low, height)) for low, height in split(rows // 2)]
+    early = rows // 8
+    cut = rows // 2 + early
+    pieces = [(0, (0, 1, early, cut - early)), (0, (0, 1, cut, rows - cut))]
     pieces += [(0, (e, n, 0, rows)) for e, n in runs(1, min(3, experts), 1)]
     pieces += [(0, (e, n, 0, rows)) for e, n in runs(3, experts, 3)]
     tail = max(experts - 2, 0)
     pieces += [(1, (e, n, 0, rows)) for e, n in runs(0, tail, 3)]
     pieces += [(1, (e, n, 0, rows)) for e, n in runs(tail, experts - 1, 1)]
-    pieces += [(1, (experts - 1, 1, low, height)) for low, height in split(rows - rows // 4)]
-    return groups, pieces
+    cut = rows - rows // 4
+    pieces += [(1, (experts - 1, 1, 0, cut)), (1, (experts - 1, 1, cut, rows - cut))]
+    return groups, pieces, early
 
 
 def group_of(groups, array, expert):
     return next(g for g, (a, e, n) in enumerate(groups) if a == array and e <= expert < e + n)
+
+
+def last_puts(count, parts):
+    return range(count - 2, count) if parts % 2 == 0 and parts > 2 else ()
 
 
 def per_device(parts, train_gate, other_gate, train_up, other_up, mix_share, router_weight, router_gain):
@@ -328,7 +388,7 @@
     inner = 2 if parts % 2 == 0 else 1
     outer = parts // inner
     me = lax.axis_index("fsdp")
-    groups, pieces = plan(experts, rows)
+    groups, pieces, early = plan(experts, rows)
 
     def step(k, l):
         return [(i, (i // inner + k) % outer * inner + (i % inner ^ l)) for i in range(parts)]
@@ -351,16 +411,10 @@
     tops = []
     for g, (a, first, count) in enumerate(groups):
         if g == 0:
-            top = first_max(mix_share, train[a], other[a], first)
+            top, ahead = first_max(mix_share, train[a], other[a], first, early)
         else:
             top = local_max(mix_share, train[a], other[a], first, count)
-        if g > 0:
-            tops.append(spread(top))
-            continue
-        direct = [top]
-        for s in range(1, parts):
-            direct.append(lax.ppermute(top, "fsdp", step(s // inner, s % inner)))
-        tops.append(direct)
+        tops.append(spread(top))
 
     whole = [None, None]
     got = []
@@ -374,12 +428,25 @@
             )
         got.append(spread(own))
 
-    for i, (a, piece) in enumerate(pieces):
-        slots = list(range(0 if i == 0 else 1, parts))
-        cut = len(slots) - 1 if i + 1 == len(pieces) else 0
-        for some in (slots[:cut], slots[cut:]):
-            if some:
-                whole[a] = put(place, [got[i][j] for j in some], some, piece, rows, whole[a])
+    whole[0] = finish(place, tops[0], spread(ahead), groups[0][1], rows, whole[0])
+
+    def place_rows(i, slots):
+        a, piece = pieces[i]
+        whole[a] = put(place, [got[i][j] for j in slots], slots, piece, rows, whole[a])
+
+    early_puts = last_puts(len(pieces), parts)
+    for i in early_puts:
+        place_rows(i, [1])
+    for i in range(len(pieces)):
+        slots = list(range(0 if i == 0 else 2 if i in early_puts else 1, parts))
+        if i + 1 == len(pieces) and len(slots) > 1:
+            a, (expert, _, low, _) = pieces[i]
+            for j in slots:
+                whole[a] = lax.dynamic_update_slice(
+                    whole[a], got[i][j], (expert, place[j] * rows + low, 0)
+                )
+        elif slots:
+            place_rows(i, slots)
 
     scales = all_scales(tops, groups, experts, cols)
     part_router = (router_weight * router_gain[:, None]).astype(jnp.bfloat16)

time: 526 us -> 538 us (1.023)
  waiting for transfers between devices: 309 us -> 322 us
    ppermute x15 -> x17, waiting for transfers between devices: 303 us -> 314 us  [spread(): got.append(lax.ppermute(x, 'fsdp', step(k, 0)))]
    unnamed x96 -> x116, local copies, waits for them, and re-layouts: 25 us -> 21.8 us
    ppermute x15 -> x17, starting transfers between devices: 17.1 us -> 16.8 us  [spread(): got.append(lax.ppermute(x, 'fsdp', step(k, 0)))]
  transfers between devices with their start and end apart: 48 -> 51, of which waited for: 13 -> 15; matrix products, arithmetic and copies ran while one was open for 0% -> 0% of each run, Pallas kernels for 22% -> 22%
where the time goes in v3:
time: 538 us; the launch traced here: 537 us
  waiting for transfers between devices  322 us (60%)
  Pallas kernels  132 us (25%)
  blocking collectives  31.2 us (6%)
  local copies, waits for them, and re-layouts  25.5 us (5%)
  starting transfers between devices  22.3 us (4%)
    ppermute x17, waiting for transfers between devices, spread(): got.append(lax.ppermute(x, 'fsdp', step(k, 0)))  314 us
    pallas_call x10, Pallas kernels, narrow(): pl.pallas_call(functools.partial(narrow_kernel, first, at, len(tops)), ou...  53.8 us
    pallas_call x12, Pallas kernels, put(): pl.pallas_call(functools.partial(put_kernel, tuple(slots), piece, rows),...  46.1 us
    all_gather x1, blocking collectives, per_device(): wide_router = lax.all_gather(row_router, 'ep', axis=1, tiled=True)  31.2 us
    pallas_call x3, Pallas kernels, local_max(): pl.pallas_call(functools.partial(max_kernel, first), out_shape=jax.ShapeD...  25 us
    unnamed x116, local copies, waits for them, and re-layouts  21.8 us
    ppermute x17, starting transfers between devices, spread(): got.append(lax.ppermute(x, 'fsdp', step(k, 0)))  16.8 us
  transfers between devices with their start and end apart: 51, of which 15 were waited for; matrix products, arithmetic and copies ran while one was open for 0% of the time, Pallas kernels for 22%

profile of v3, /device:TPU:0, one launch (start us, length us, event | category | flops | bytes accessed | tf_op | source)
XLA Modules:
  0.0 536.9 jit_solution(15474726600861873816)
XLA Ops:
  1.3 12.6 %local_max.5.refs_0_.refs_12_ = f32[8,1024]{1,0:T(8,128)S(1)} custom-call(f32[8]{0:T(128)S(1)} %copy-done.46, f32[8,512,1024]{2,1,0:T(8,128)} %refs_4_.21, f32[8,512,1024]{2,1,0:T(8,128)} %refs_5_.21), custom_call_target="tpu_custom_call" | custom-call | flops 20971520 | bytes 33554432 | tf_op jit(solution)/shard_map/local_max/pallas_call | solution.py:112
  14.0 3.0 collective-permute-start.31
  17.0 2.3 first_max.1
  20.0 3.9 local_max.4.refs_0_.refs_4_
  24.0 1.7 collective-permute-start.4
  28.7 3.5 narrow.10
  32.5 1.7 collective-permute-start.22
  34.1 8.3 %narrow.15 = (bf16[3,512,1024]{2,1,0:T(8,128)(2,1)S(1)}, bf16[8,2048,1024]{2,1,0:T(8,128)(2,1)}) custom-call(s32[4]{0:T(128)S(1)} %get-tuple-element.56.place_ref, f32[8]{0:T(128)S(1)} %copy-done.47, f32[8,1024]{1,0:T(8,128)S(1)} %local_max.5.refs_0_.refs_12_, f32[8,1024]{1,0:T(8,128)S(1)} %collective-permute-done.30.refs_1_.refs_13_, ...), custom_call_target="tpu_custom_call" | custom-call | flops 9437184 | bytes 18874368 | tf_op jit(solution)/shard_map/narrow/pallas_call | solution.py:214
  44.1 8.3 %narrow.16 = (bf16[3,512,1024]{2,1,0:T(8,128)(2,1)S(1)}, bf16[8,2048,1024]{2,1,0:T(8,128)(2,1)}) custom-call(s32[4]{0:T(128)S(1)} %get-tuple-element.56.place_ref, f32[8]{0:T(128)S(1)} %copy-done.47, f32[8,1024]{1,0:T(8,128)S(1)} %local_max.5.refs_0_.refs_12_, ...), custom_call_target="tpu_custom_call", output_to_operand_aliasing={{1}: (8, {})} | custom-call | flops 9437184 | bytes 18874368 | tf_op jit(solution)/shard_map/narrow/pallas_call | solution.py:214
  52.4 3.8 narrow.17
  57.1 4.2 narrow.18
  61.3 2.6 narrow.19
  65.8 3.3 collective-permute-done.49
  70.4 8.4 %local_max.3.refs_0_.refs_8_ = f32[5,1024]{1,0:T(8,128)S(1)} custom-call(f32[8]{0:T(128)S(1)} %copy-done.47, f32[8,512,1024]{2,1,0:T(8,128)} %refs_4_.16, f32[8,512,1024]{2,1,0:T(8,128)} %refs_5_.16), custom_call_target="tpu_custom_call" | custom-call | flops 13107200 | bytes 20971520 | tf_op jit(solution)/shard_map/local_max/pallas_call | solution.py:112
  79.2 3.6 collective-permute-done.1.refs_2_.refs_10_
  85.6 1.7 first_narrow.1.refs_0_
  87.3 1.7 collective-permute-start.25
  90.2 4.1 collective-permute-done.46
  95.1 3.9 narrow.11
  99.5 6.1 %collective-permute-done.25.refs_2_ = bf16[1,256,1024]{2,1,0:T(8,128)(2,1)S(1)} collective-permute-done((bf16[1,256,1024]{2,1,0:T(8,128)(2,1)S(1)}, bf16[1,256,1024]{2,1,0:T(8,128)(2,1)S(1)}, u32[]{:S(2)}, u32[]{:S(2)}) %collective-permute-start.25) | collective-permute-done | bytes 524320 | tf_op jit(solution)/shard_map/ppermute | solution.py:401
  106.1 3.9 narrow.12
  110.8 1.7 collective-permute-start.16
  113.3 31.7 %collective-permute-done.33.refs_0_ = bf16[1,384,1024]{2,1,0:T(8,128)(2,1)} collective-permute-done((bf16[1,384,1024]{2,1,0:T(8,128)(2,1)S(1)}, bf16[1,384,1024]{2,1,0:T(8,128)(2,1)}, u32[]{:S(2)}, u32[]{:S(2)}) %collective-permute-start.33) | collective-permute-done | bytes 786464 | tf_op jit(solution)/shard_map/ppermute | solution.py:401
  145.1 9.2 %narrow.13 = (bf16[3,512,1024]{2,1,0:T(8,128)(2,1)}, bf16[8,2048,1024]{2,1,0:T(8,128)(2,1)}) custom-call(s32[4]{0:T(128)S(1)} %get-tuple-element.56.place_ref, f32[8]{0:T(128)S(1)} %copy-done.47, f32[5,1024]{1,0:T(8,128)S(1)} %local_max.3.refs_0_.refs_8_, f32[5,1024]{1,0:T(8,128)S(1)} %collective-permute-done.refs_1_.refs_9_, ...), custom_call_target="tpu_custom_call", output_to_operand_aliasing={{1}: (8, {})} | custom-call | flops 9437184 | bytes 18874368 | tf_op jit(solution)/shard_map/narrow/pallas_call | solution.py:214
  154.3 6.0 %narrow.14 = (bf16[2,512,1024]{2,1,0:T(8,128)(2,1)S(1)}, bf16[8,2048,1024]{2,1,0:T(8,128)(2,1)}) custom-call(s32[4]{0:T(128)S(1)} %get-tuple-element.56.place_ref, f32[8]{0:T(128)S(1)} %copy-done.47, f32[5,1024]{1,0:T(8,128)S(1)} %local_max.3.refs_0_.refs_8_, f32[5,1024]{1,0:T(8,128)S(1)} %collective-permute-done.refs_1_.refs_9_, ...), custom_call_target="tpu_custom_call", output_to_operand_aliasing={{1}: (8, {})} | custom-call | flops 6291456 | bytes 12582912 | tf_op jit(solution)/shard_map/narrow/pallas_call | solution.py:214
  161.5 1.7 collective-permute-start.36
  164.2 3.2 collective-permute-done.16.refs_1_
  170.9 63.2 %collective-permute-done.36.refs_1_ = bf16[1,512,1024]{2,1,0:T(8,128)(2,1)} collective-permute-done((bf16[1,512,1024]{2,1,0:T(8,128)(2,1)S(1)}, bf16[1,512,1024]{2,1,0:T(8,128)(2,1)}, u32[]{:S(2)}, u32[]{:S(2)}) %collective-permute-start.36) | collective-permute-done | bytes 1048608 | tf_op jit(solution)/shard_map/ppermute | solution.py:401
  236.5 1.7 collective-permute-start.42
  239.8 65.5 %collective-permute-done.13.refs_1_ = bf16[3,512,1024]{2,1,0:T(8,128)(2,1)S(1)} collective-permute-done((bf16[3,512,1024]{2,1,0:T(8,128)(2,1)}, bf16[3,512,1024]{2,1,0:T(8,128)(2,1)S(1)}, u32[]{:S(2)}, u32[]{:S(2)}) %collective-permute-start.13) | collective-permute-done | bytes 3145760 | tf_op jit(solution)/shard_map/ppermute | solution.py:401
  305.8 67.0 %collective-permute-done.42.refs_1_ = bf16[3,512,1024]{2,1,0:T(8,128)(2,1)} collective-permute-done((bf16[3,512,1024]{2,1,0:T(8,128)(2,1)}, bf16[3,512,1024]{2,1,0:T(8,128)(2,1)}, u32[]{:S(2)}, u32[]{:S(2)}) %collective-permute-start.42) | collective-permute-done | bytes 3145760 | tf_op jit(solution)/shard_map/ppermute | solution.py:401
  372.8 65.7 %collective-permute-done.39.refs_1_ = bf16[3,512,1024]{2,1,0:T(8,128)(2,1)} collective-permute-done((bf16[3,512,1024]{2,1,0:T(8,128)(2,1)S(1)}, bf16[3,512,1024]{2,1,0:T(8,128)(2,1)}, u32[]{:S(2)}, u32[]{:S(2)}) %collective-permute-start.39) | collective-permute-done | bytes 3145760 | tf_op jit(solution)/shard_map/ppermute | solution.py:401
  438.6 1.7 copy-done.2
  443.7 3.7 collective-permute-done.11.refs_2_
  447.6 1.8 copy-done.52
  452.0 31.2 %all_gather.3 = bf16[2048,64]{0,1:T(8,128)(2,1)S(1)} all-gather(bf16[2048,8]{0,1:T(8,128)(2,1)S(1)} %constant_dynamic-update-slice_fusion), channel_id=1, replica_groups=mesh['ep'=8,'fsdp'=4] {'ep'}, dimensions={1}, use_global_device_ids=true | all-gather | bytes 294912 | tf_op jit(solution)/shard_map/all_gather | solution.py:456
  487.2 2.1 finish.1.refs_4_
  490.9 2.1 put.12.refs_3_
  493.0 2.2 put.13.refs_3_
  495.3 2.5 put.14.refs_3_
  497.8 2.5 put.15.refs_3_
  500.3 7.8 %put.16.refs_3_ = bf16[8,2048,1024]{2,1,0:T(8,128)(2,1)} custom-call(s32[4]{0:T(128)S(1)} %get-tuple-element.56.place_ref, bf16[3,512,1024]{2,1,0:T(8,128)(2,1)S(1)} %collective-permute-done.12.refs_0_, bf16[3,512,1024]{2,1,0:T(8,128)(2,1)} %copy-done.51, bf16[3,512,1024]{2,1,0:T(8,128)(2,1)} %copy-done.52, ...), custom_call_target="tpu_custom_call", output_to_operand_aliasing={{}: (4, {})} | custom-call | flops 4718592 | bytes 18874368 | tf_op jit(solution)/shard_map/put/pallas_call | solution.py:305
  508.1 5.1 put.17
  513.2 7.6 %put.20.refs_3_ = bf16[8,2048,1024]{2,1,0:T(8,128)(2,1)} custom-call(s32[4]{0:T(128)S(1)} %get-tuple-element.56.place_ref, bf16[3,512,1024]{2,1,0:T(8,128)(2,1)S(1)} %copy-done.3, bf16[3,512,1024]{2,1,0:T(8,128)(2,1)} %collective-permute-done.42.refs_1_, bf16[3,512,1024]{2,1,0:T(8,128)(2,1)} %collective-permute-done.43.refs_2_, ...), custom_call_target="tpu_custom_call", output_to_operand_aliasing={{}: (4, {})} | custom-call | flops 4718592 | bytes 18874368 | tf_op jit(solution)/shard_map/put/pallas_call | solution.py:305
  520.8 7.3 %put.21.refs_3_ = bf16[8,2048,1024]{2,1,0:T(8,128)(2,1)} custom-call(s32[4]{0:T(128)S(1)} %get-tuple-element.56.place_ref, bf16[3,512,1024]{2,1,0:T(8,128)(2,1)S(1)} %copy-done.1, bf16[3,512,1024]{2,1,0:T(8,128)(2,1)} %collective-permute-done.39.refs_1_, bf16[3,512,1024]{2,1,0:T(8,128)(2,1)} %collective-permute-done.40.refs_2_, ...), custom_call_target="tpu_custom_call", output_to_operand_aliasing={{}: (4, {})} | custom-call | flops 4718592 | bytes 18874368 | tf_op jit(solution)/shard_map/put/pallas_call | solution.py:305
  528.2 3.5 put.22.refs_2_
  531.7 2.8 put.23
  535.3 1.7 constant_dynamic-update-slice_fusion.4
  (210 shorter events, 38.1 us)
Async XLA Ops:
  14.0 12.4 %collective-permute-start.31 = (f32[8,1024]{1,0:T(8,128)S(1)}, f32[8,1024]{1,0:T(8,128)S(1)}, u32[]{:S(2)}, u32[]{:S(2)}) collective-permute-start(f32[8,1024]{1,0:T(8,128)S(1)} %local_max.5.refs_0_.refs_12_), channel_id=1, source_target_pairs={{0,2},{1,3},{2,0},{3,1},{4,6},{5,7},{6,4},{7,5},{8,10},{9,11},{10,... | collective-permute-start | bytes 98312 | tf_op jit(solution)/shard_map/ppermute | solution.py:401
  17.0 15.3 %collective-permute-start.30 = (f32[8,1024]{1,0:T(8,128)S(1)}, f32[8,1024]{1,0:T(8,128)S(1)}, u32[]{:S(2)}, u32[]{:S(2)}) collective-permute-start(f32[8,1024]{1,0:T(8,128)S(1)} %local_max.5.refs_0_.refs_12_), channel_id=1, source_target_pairs={{0,1},{1,0},{2,3},{3,2},{4,5},{5,4},{6,7},{7,6},{8,9},{9,8},{10,11... | collective-permute-start | bytes 98312 | tf_op jit(solution)/shard_map/ppermute | solution.py:399
  19.4 7.0 %collective-permute-start.7 = (f32[1,1024]{1,0:T(1,128)S(1)}, f32[1,1024]{1,0:T(1,128)S(1)}, u32[]{:S(2)}, u32[]{:S(2)}) collective-permute-start(f32[1,1024]{1,0:T(1,128)S(1)} %get-tuple-element.29.refs_0_), channel_id=1, source_target_pairs={{0,2},{1,3},{2,0},{3,1},{4,6},{5,7},{6,4},{7,5},{8,10},{9,11},{10,... | collective-permute-start | bytes 12296 | tf_op jit(solution)/shard_map/ppermute | solution.py:401
  19.5 8.7 %collective-permute-start.6 = (f32[1,1024]{1,0:T(1,128)S(1)}, f32[1,1024]{1,0:T(1,128)S(1)}, u32[]{:S(2)}, u32[]{:S(2)}) collective-permute-start(f32[1,1024]{1,0:T(1,128)S(1)} %get-tuple-element.29.refs_0_), channel_id=1, source_target_pairs={{0,1},{1,0},{2,3},{3,2},{4,5},{5,4},{6,7},{7,6},{8,9},{9,8},{10,11... | collective-permute-start | bytes 12296 | tf_op jit(solution)/shard_map/ppermute | solution.py:399
  24.0 39.9 %collective-permute-start.4 = (f32[2,1024]{1,0:T(2,128)S(1)}, f32[2,1024]{1,0:T(2,128)S(1)}, u32[]{:S(2)}, u32[]{:S(2)}) collective-permute-start(f32[2,1024]{1,0:T(2,128)S(1)} %local_max.4.refs_0_.refs_4_), channel_id=1, source_target_pairs={{0,2},{1,3},{2,0},{3,1},{4,6},{5,7},{6,4},{7,5},{8,10},{9,11},{10,... | collective-permute-start | bytes 24584 | tf_op jit(solution)/shard_map/ppermute | solution.py:401
  26.4 1.9 collective-permute-start.8
  26.4 6.1 %collective-permute-start.32 = (f32[8,1024]{1,0:T(8,128)S(1)}, f32[8,1024]{1,0:T(8,128)S(1)}, u32[]{:S(2)}, u32[]{:S(2)}) collective-permute-start(f32[8,1024]{1,0:T(8,128)S(1)} %collective-permute-done.31.refs_2_.refs_14_), channel_id=1, source_target_pairs={{0,1},{1,0},{2,3},{3,2},{4,5},{5,4},{6,7},{7,6},{8,9},{9,8},{10,11... | collective-permute-start | bytes 98312 | tf_op jit(solution)/shard_map/ppermute | solution.py:403
  28.2 35.8 %collective-permute-start.3 = (f32[2,1024]{1,0:T(2,128)S(1)}, f32[2,1024]{1,0:T(2,128)S(1)}, u32[]{:S(2)}, u32[]{:S(2)}) collective-permute-start(f32[2,1024]{1,0:T(2,128)S(1)} %local_max.4.refs_0_.refs_4_), channel_id=1, source_target_pairs={{0,1},{1,0},{2,3},{3,2},{4,5},{5,4},{6,7},{7,6},{8,9},{9,8},{10,11... | collective-permute-start | bytes 24584 | tf_op jit(solution)/shard_map/ppermute | solution.py:399
  28.3 58.9 %collective-permute-start.28 = (f32[64,1024]{1,0:T(8,128)S(1)}, f32[64,1024]{1,0:T(8,128)S(1)}, u32[]{:S(2)}, u32[]{:S(2)}) collective-permute-start(f32[64,1024]{1,0:T(8,128)S(1)} %get-tuple-element.39.refs_4_), channel_id=1, source_target_pairs={{0,2},{1,3},{2,0},{3,1},{4,6},{5,7},{6,4},{7,5},{8,10},{9,11},{10,... | collective-permute-start | bytes 786440 | tf_op jit(solution)/shard_map/ppermute | solution.py:401
  32.3 56.8 %collective-permute-start.27 = (f32[64,1024]{1,0:T(8,128)S(1)}, f32[64,1024]{1,0:T(8,128)S(1)}, u32[]{:S(2)}, u32[]{:S(2)}) collective-permute-start(f32[64,1024]{1,0:T(8,128)S(1)} %get-tuple-element.39.refs_4_), channel_id=1, source_target_pairs={{0,1},{1,0},{2,3},{3,2},{4,5},{5,4},{6,7},{7,6},{8,9},{9,8},{10,11... | collective-permute-start | bytes 786440 | tf_op jit(solution)/shard_map/ppermute | solution.py:399
  32.5 61.9 %collective-permute-start.22 = (bf16[1,192,1024]{2,1,0:T(8,128)(2,1)S(1)}, bf16[1,192,1024]{2,1,0:T(8,128)(2,1)S(1)}, u32[]{:S(2)}, u32[]{:S(2)}) collective-permute-start(bf16[1,192,1024]{2,1,0:T(8,128)(2,1)S(1)} %get-tuple-element.38), channel_id=1, source_target_pairs={{0,2},{1,3},{2,0},{3,1},{4,6},{5,7},{6,4},{7,5},{8,10},{9,11},{10,... | collective-permute-start | bytes 1179656 | tf_op jit(solution)/shard_map/ppermute | solution.py:401
  63.8 25.2 %collective-permute-start.44 = (bf16[1,128,1024]{2,1,0:T(8,128)(2,1)S(1)}, bf16[1,128,1024]{2,1,0:T(8,128)(2,1)S(1)}, u32[]{:S(2)}, u32[]{:S(2)}) collective-permute-start(bf16[1,128,1024]{2,1,0:T(8,128)(2,1)S(1)} %get-tuple-element.49), channel_id=1, source_target_pairs={{0,1},{1,0},{2,3},{3,2},{4,5},{5,4},{6,7},{7,6},{8,9},{9,8},{10,11... | collective-permute-start | bytes 786440 | tf_op jit(solution)/shard_map/ppermute | solution.py:399
  64.0 1.4 collective-permute-start.48
  65.4 3.7 collective-permute-start.49
  70.2 8.6 %collective-permute-start.50 = (bf16[512,8]{0,1:T(8,128)(2,1)S(1)}, bf16[512,8]{0,1:T(8,128)(2,1)S(1)}, u32[]{:S(2)}, u32[]{:S(2)}) collective-permute-start(bf16[512,8]{0,1:T(8,128)(2,1)S(1)} %collective-permute-done.49), channel_id=1, source_target_pairs={{0,1},{1,0},{2,3},{3,2},{4,5},{5,4},{6,7},{7,6},{8,9},{9,8},{10,11... | collective-permute-start | bytes 24584 | tf_op jit(solution)/shard_map/ppermute | solution.py:403
  78.8 4.0 collective-permute-start.1
  85.2 9.2 %collective-permute-start.46 = (bf16[1,128,1024]{2,1,0:T(8,128)(2,1)S(1)}, bf16[1,128,1024]{2,1,0:T(8,128)(2,1)S(1)}, u32[]{:S(2)}, u32[]{:S(2)}) collective-permute-start(bf16[1,128,1024]{2,1,0:T(8,128)(2,1)S(1)} %get-tuple-element.49), channel_id=1, source_target_pairs={{0,2},{1,3},{2,0},{3,1},{4,6},{5,7},{6,4},{7,5},{8,10},{9,11},{10,... | collective-permute-start | bytes 786440 | tf_op jit(solution)/shard_map/ppermute | solution.py:401
  87.3 18.3 %collective-permute-start.25 = (bf16[1,256,1024]{2,1,0:T(8,128)(2,1)S(1)}, bf16[1,256,1024]{2,1,0:T(8,128)(2,1)S(1)}, u32[]{:S(2)}, u32[]{:S(2)}) collective-permute-start(bf16[1,256,1024]{2,1,0:T(8,128)(2,1)S(1)} %first_narrow.1.refs_0_), channel_id=1, source_target_pairs={{0,2},{1,3},{2,0},{3,1},{4,6},{5,7},{6,4},{7,5},{8,10},{9,11},{10,... | collective-permute-start | bytes 1572872 | tf_op jit(solution)/shard_map/ppermute | solution.py:401
  89.0 5.9 %collective-permute-start.21 = (bf16[1,192,1024]{2,1,0:T(8,128)(2,1)S(1)}, bf16[1,192,1024]{2,1,0:T(8,128)(2,1)S(1)}, u32[]{:S(2)}, u32[]{:S(2)}) collective-permute-start(bf16[1,192,1024]{2,1,0:T(8,128)(2,1)S(1)} %get-tuple-element.38), channel_id=1, source_target_pairs={{0,1},{1,0},{2,3},{3,2},{4,5},{5,4},{6,7},{7,6},{8,9},{9,8},{10,11... | collective-permute-start | bytes 1179656 | tf_op jit(solution)/shard_map/ppermute | solution.py:399
  89.8 15.8 %collective-permute-start.24 = (bf16[1,256,1024]{2,1,0:T(8,128)(2,1)S(1)}, bf16[1,256,1024]{2,1,0:T(8,128)(2,1)S(1)}, u32[]{:S(2)}, u32[]{:S(2)}) collective-permute-start(bf16[1,256,1024]{2,1,0:T(8,128)(2,1)S(1)} %first_narrow.1.refs_0_), channel_id=1, source_target_pairs={{0,1},{1,0},{2,3},{3,2},{4,5},{5,4},{6,7},{7,6},{8,9},{9,8},{10,11... | collective-permute-start | bytes 1572872 | tf_op jit(solution)/shard_map/ppermute | solution.py:399
  94.4 18.1 %collective-permute-start.45 = (bf16[1,384,1024]{2,1,0:T(8,128)(2,1)S(1)}, bf16[1,384,1024]{2,1,0:T(8,128)(2,1)S(1)}, u32[]{:S(2)}, u32[]{:S(2)}) collective-permute-start(bf16[1,384,1024]{2,1,0:T(8,128)(2,1)S(1)} %get-tuple-element.44), channel_id=1, source_target_pairs={{0,1},{1,0},{2,3},{3,2},{4,5},{5,4},{6,7},{7,6},{8,9},{9,8},{10,11... | collective-permute-start | bytes 2359304 | tf_op jit(solution)/shard_map/ppermute | solution.py:399
  94.4 4.7 collective-permute-start.29
  95.1 14.9 %collective-permute-start.23 = (bf16[1,192,1024]{2,1,0:T(8,128)(2,1)S(1)}, bf16[1,192,1024]{2,1,0:T(8,128)(2,1)S(1)}, u32[]{:S(2)}, u32[]{:S(2)}) collective-permute-start(bf16[1,192,1024]{2,1,0:T(8,128)(2,1)S(1)} %collective-permute-done.22.refs_1_), channel_id=1, source_target_pairs={{0,1},{1,0},{2,3},{3,2},{4,5},{5,4},{6,7},{7,6},{8,9},{9,8},{10,11... | collective-permute-start | bytes 1179656 | tf_op jit(solution)/shard_map/ppermute | solution.py:403
  99.1 62.4 %collective-permute-start.19 = (bf16[1,512,1024]{2,1,0:T(8,128)(2,1)}, bf16[1,512,1024]{2,1,0:T(8,128)(2,1)S(1)}, u32[]{:S(2)}, u32[]{:S(2)}) collective-permute-start(bf16[1,512,1024]{2,1,0:T(8,128)(2,1)} %get-tuple-element.37), channel_id=1, source_target_pairs={{0,2},{1,3},{2,0},{3,1},{4,6},{5,7},{6,4},{7,5},{8,10},{9,11},{10,... | collective-permute-start | bytes 3145736 | tf_op jit(solution)/shard_map/ppermute | solution.py:401
  105.6 57.5 %collective-permute-start.18 = (bf16[1,512,1024]{2,1,0:T(8,128)(2,1)}, bf16[1,512,1024]{2,1,0:T(8,128)(2,1)S(1)}, u32[]{:S(2)}, u32[]{:S(2)}) collective-permute-start(bf16[1,512,1024]{2,1,0:T(8,128)(2,1)} %get-tuple-element.37), channel_id=1, source_target_pairs={{0,1},{1,0},{2,3},{3,2},{4,5},{5,4},{6,7},{7,6},{8,9},{9,8},{10,11... | collective-permute-start | bytes 3145736 | tf_op jit(solution)/shard_map/ppermute | solution.py:399
  105.6 39.4 %collective-permute-start.33 = (bf16[1,384,1024]{2,1,0:T(8,128)(2,1)S(1)}, bf16[1,384,1024]{2,1,0:T(8,128)(2,1)}, u32[]{:S(2)}, u32[]{:S(2)}) collective-permute-start(bf16[1,384,1024]{2,1,0:T(8,128)(2,1)S(1)} %get-tuple-element.44), channel_id=1, source_target_pairs={{0,2},{1,3},{2,0},{3,1},{4,6},{5,7},{6,4},{7,5},{8,10},{9,11},{10,... | collective-permute-start | bytes 2359304 | tf_op jit(solution)/shard_map/ppermute | solution.py:401
  110.8 56.6 %collective-permute-start.16 = (bf16[1,512,1024]{2,1,0:T(8,128)(2,1)}, bf16[1,512,1024]{2,1,0:T(8,128)(2,1)S(1)}, u32[]{:S(2)}, u32[]{:S(2)}) collective-permute-start(bf16[1,512,1024]{2,1,0:T(8,128)(2,1)} %get-tuple-element.36), channel_id=1, source_target_pairs={{0,2},{1,3},{2,0},{3,1},{4,6},{5,7},{6,4},{7,5},{8,10},{9,11},{10,... | collective-permute-start | bytes 3145736 | tf_op jit(solution)/shard_map/ppermute | solution.py:401
  113.3 47.0 %collective-permute-start.26 = (bf16[1,256,1024]{2,1,0:T(8,128)(2,1)S(1)}, bf16[1,256,1024]{2,1,0:T(8,128)(2,1)S(1)}, u32[]{:S(2)}, u32[]{:S(2)}) collective-permute-start(bf16[1,256,1024]{2,1,0:T(8,128)(2,1)S(1)} %collective-permute-done.25.refs_2_), channel_id=1, source_target_pairs={{0,1},{1,0},{2,3},{3,2},{4,5},{5,4},{6,7},{7,6},{8,9},{9,8},{10,11... | collective-permute-start | bytes 1572872 | tf_op jit(solution)/shard_map/ppermute | solution.py:403
  145.1 23.3 %collective-permute-start.15 = (bf16[1,512,1024]{2,1,0:T(8,128)(2,1)}, bf16[1,512,1024]{2,1,0:T(8,128)(2,1)S(1)}, u32[]{:S(2)}, u32[]{:S(2)}) collective-permute-start(bf16[1,512,1024]{2,1,0:T(8,128)(2,1)} %get-tuple-element.36), channel_id=1, source_target_pairs={{0,1},{1,0},{2,3},{3,2},{4,5},{5,4},{6,7},{7,6},{8,9},{9,8},{10,11... | collective-permute-start | bytes 3145736 | tf_op jit(solution)/shard_map/ppermute | solution.py:399
  161.1 77.0 %collective-permute-start.10 = (bf16[2,512,1024]{2,1,0:T(8,128)(2,1)S(1)}, bf16[2,512,1024]{2,1,0:T(8,128)(2,1)S(1)}, u32[]{:S(2)}, u32[]{:S(2)}) collective-permute-start(bf16[2,512,1024]{2,1,0:T(8,128)(2,1)S(1)} %get-tuple-element.34), channel_id=1, source_target_pairs={{0,2},{1,3},{2,0},{3,1},{4,6},{5,7},{6,4},{7,5},{8,10},{9,11},{10,... | collective-permute-start | bytes 6291464 | tf_op jit(solution)/shard_map/ppermute | solution.py:401
  161.5 72.6 %collective-permute-start.36 = (bf16[1,512,1024]{2,1,0:T(8,128)(2,1)S(1)}, bf16[1,512,1024]{2,1,0:T(8,128)(2,1)}, u32[]{:S(2)}, u32[]{:S(2)}) collective-permute-start(bf16[1,512,1024]{2,1,0:T(8,128)(2,1)S(1)} %copy-done.50), channel_id=1, source_target_pairs={{0,2},{1,3},{2,0},{3,1},{4,6},{5,7},{6,4},{7,5},{8,10},{9,11},{10,... | collective-permute-start | bytes 3145736 | tf_op jit(solution)/shard_map/ppermute | solution.py:401
  164.2 74.3 %collective-permute-start.9 = (bf16[2,512,1024]{2,1,0:T(8,128)(2,1)S(1)}, bf16[2,512,1024]{2,1,0:T(8,128)(2,1)S(1)}, u32[]{:S(2)}, u32[]{:S(2)}) collective-permute-start(bf16[2,512,1024]{2,1,0:T(8,128)(2,1)S(1)} %get-tuple-element.34), channel_id=1, source_target_pairs={{0,1},{1,0},{2,3},{3,2},{4,5},{5,4},{6,7},{7,6},{8,9},{9,8},{10,11... | collective-permute-start | bytes 6291464 | tf_op jit(solution)/shard_map/ppermute | solution.py:399
  167.4 67.1 %collective-permute-start.20 = (bf16[1,512,1024]{2,1,0:T(8,128)(2,1)S(1)}, bf16[1,512,1024]{2,1,0:T(8,128)(2,1)S(1)}, u32[]{:S(2)}, u32[]{:S(2)}) collective-permute-start(bf16[1,512,1024]{2,1,0:T(8,128)(2,1)S(1)} %collective-permute-done.19.refs_1_), channel_id=1, source_target_pairs={{0,1},{1,0},{2,3},{3,2},{4,5},{5,4},{6,7},{7,6},{8,9},{9,8},{10,11... | collective-permute-start | bytes 3145736 | tf_op jit(solution)/shard_map/ppermute | solution.py:403
  169.4 66.2 %collective-permute-start.17 = (bf16[1,512,1024]{2,1,0:T(8,128)(2,1)S(1)}, bf16[1,512,1024]{2,1,0:T(8,128)(2,1)S(1)}, u32[]{:S(2)}, u32[]{:S(2)}) collective-permute-start(bf16[1,512,1024]{2,1,0:T(8,128)(2,1)S(1)} %collective-permute-done.16.refs_1_), channel_id=1, source_target_pairs={{0,1},{1,0},{2,3},{3,2},{4,5},{5,4},{6,7},{7,6},{8,9},{9,8},{10,11... | collective-permute-start | bytes 3145736 | tf_op jit(solution)/shard_map/ppermute | solution.py:403
  234.1 71.2 %collective-permute-start.13 = (bf16[3,512,1024]{2,1,0:T(8,128)(2,1)}, bf16[3,512,1024]{2,1,0:T(8,128)(2,1)S(1)}, u32[]{:S(2)}, u32[]{:S(2)}) collective-permute-start(bf16[3,512,1024]{2,1,0:T(8,128)(2,1)} %get-tuple-element.35), channel_id=1, source_target_pairs={{0,2},{1,3},{2,0},{3,1},{4,6},{5,7},{6,4},{7,5},{8,10},{9,11},{10,... | collective-permute-start | bytes 9437192 | tf_op jit(solution)/shard_map/ppermute | solution.py:401
  235.5 69.8 %collective-permute-start.12 = (bf16[3,512,1024]{2,1,0:T(8,128)(2,1)}, bf16[3,512,1024]{2,1,0:T(8,128)(2,1)S(1)}, u32[]{:S(2)}, u32[]{:S(2)}) collective-permute-start(bf16[3,512,1024]{2,1,0:T(8,128)(2,1)} %get-tuple-element.35), channel_id=1, source_target_pairs={{0,1},{1,0},{2,3},{3,2},{4,5},{5,4},{6,7},{7,6},{8,9},{9,8},{10,11... | collective-permute-start | bytes 9437192 | tf_op jit(solution)/shard_map/ppermute | solution.py:399
  236.5 136.3 %collective-permute-start.42 = (bf16[3,512,1024]{2,1,0:T(8,128)(2,1)}, bf16[3,512,1024]{2,1,0:T(8,128)(2,1)}, u32[]{:S(2)}, u32[]{:S(2)}) collective-permute-start(bf16[3,512,1024]{2,1,0:T(8,128)(2,1)} %copy-done.48), channel_id=1, source_target_pairs={{0,2},{1,3},{2,0},{3,1},{4,6},{5,7},{6,4},{7,5},{8,10},{9,11},{10,... | collective-permute-start | bytes 9437192 | tf_op jit(solution)/shard_map/ppermute | solution.py:401
  238.2 200.4 %collective-permute-start.39 = (bf16[3,512,1024]{2,1,0:T(8,128)(2,1)S(1)}, bf16[3,512,1024]{2,1,0:T(8,128)(2,1)}, u32[]{:S(2)}, u32[]{:S(2)}) collective-permute-start(bf16[3,512,1024]{2,1,0:T(8,128)(2,1)S(1)} %get-tuple-element.46), channel_id=1, source_target_pairs={{0,2},{1,3},{2,0},{3,1},{4,6},{5,7},{6,4},{7,5},{8,10},{9,11},{10,... | collective-permute-start | bytes 9437192 | tf_op jit(solution)/shard_map/ppermute | solution.py:401
  239.8 198.8 %collective-permute-start.41 = (bf16[3,512,1024]{2,1,0:T(8,128)(2,1)}, bf16[3,512,1024]{2,1,0:T(8,128)(2,1)S(1)}, u32[]{:S(2)}, u32[]{:S(2)}) collective-permute-start(bf16[3,512,1024]{2,1,0:T(8,128)(2,1)} %copy-done.48), channel_id=1, source_target_pairs={{0,1},{1,0},{2,3},{3,2},{4,5},{5,4},{6,7},{7,6},{8,9},{9,8},{10,11... | collective-permute-start | bytes 9437192 | tf_op jit(solution)/shard_map/ppermute | solution.py:399
  305.3 136.8 %collective-permute-start.38 = (bf16[3,512,1024]{2,1,0:T(8,128)(2,1)S(1)}, bf16[3,512,1024]{2,1,0:T(8,128)(2,1)S(1)}, u32[]{:S(2)}, u32[]{:S(2)}) collective-permute-start(bf16[3,512,1024]{2,1,0:T(8,128)(2,1)S(1)} %get-tuple-element.46), channel_id=1, source_target_pairs={{0,1},{1,0},{2,3},{3,2},{4,5},{5,4},{6,7},{7,6},{8,9},{9,8},{10,11... | collective-permute-start | bytes 9437192 | tf_op jit(solution)/shard_map/ppermute | solution.py:399
  305.3 142.3 %collective-permute-start.14 = (bf16[3,512,1024]{2,1,0:T(8,128)(2,1)S(1)}, bf16[3,512,1024]{2,1,0:T(8,128)(2,1)S(1)}, u32[]{:S(2)}, u32[]{:S(2)}) collective-permute-start(bf16[3,512,1024]{2,1,0:T(8,128)(2,1)S(1)} %collective-permute-done.13.refs_1_), channel_id=1, source_target_pairs={{0,1},{1,0},{2,3},{3,2},{4,5},{5,4},{6,7},{7,6},{8,9},{9,8},{10,11... | collective-permute-start | bytes 9437192 | tf_op jit(solution)/shard_map/ppermute | solution.py:403
  372.8 79.1 %collective-permute-start.43 = (bf16[3,512,1024]{2,1,0:T(8,128)(2,1)}, bf16[3,512,1024]{2,1,0:T(8,128)(2,1)}, u32[]{:S(2)}, u32[]{:S(2)}) collective-permute-start(bf16[3,512,1024]{2,1,0:T(8,128)(2,1)} %collective-permute-done.42.refs_1_), channel_id=1, source_target_pairs={{0,1},{1,0},{2,3},{3,2},{4,5},{5,4},{6,7},{7,6},{8,9},{9,8},{10,11... | collective-permute-start | bytes 9437192 | tf_op jit(solution)/shard_map/ppermute | solution.py:403
  438.6 82.2 %collective-permute-start.40 = (bf16[3,512,1024]{2,1,0:T(8,128)(2,1)}, bf16[3,512,1024]{2,1,0:T(8,128)(2,1)}, u32[]{:S(2)}, u32[]{:S(2)}) collective-permute-start(bf16[3,512,1024]{2,1,0:T(8,128)(2,1)} %collective-permute-done.39.refs_1_), channel_id=1, source_target_pairs={{0,1},{1,0},{2,3},{3,2},{4,5},{5,4},{6,7},{7,6},{8,9},{9,8},{10,11... | collective-permute-start | bytes 9437192 | tf_op jit(solution)/shard_map/ppermute | solution.py:403
  440.2 7.2 %collective-permute-start.11 = (bf16[2,512,1024]{2,1,0:T(8,128)(2,1)S(1)}, bf16[2,512,1024]{2,1,0:T(8,128)(2,1)S(1)}, u32[]{:S(2)}, u32[]{:S(2)}) collective-permute-start(bf16[2,512,1024]{2,1,0:T(8,128)(2,1)S(1)} %collective-permute-done.10.refs_1_), channel_id=1, source_target_pairs={{0,1},{1,0},{2,3},{3,2},{4,5},{5,4},{6,7},{7,6},{8,9},{9,8},{10,11... | collective-permute-start | bytes 6291464 | tf_op jit(solution)/shard_map/ppermute | solution.py:403
  443.7 84.4 %collective-permute-start.35 = (bf16[1,512,1024]{2,1,0:T(8,128)(2,1)}, bf16[1,512,1024]{2,1,0:T(8,128)(2,1)}, u32[]{:S(2)}, u32[]{:S(2)}) collective-permute-start(bf16[1,512,1024]{2,1,0:T(8,128)(2,1)} %copy-done.49), channel_id=1, source_target_pairs={{0,1},{1,0},{2,3},{3,2},{4,5},{5,4},{6,7},{7,6},{8,9},{9,8},{10,11... | collective-permute-start | bytes 3145736 | tf_op jit(solution)/shard_map/ppermute | solution.py:399
  447.5 80.7 %collective-permute-start.37 = (bf16[1,512,1024]{2,1,0:T(8,128)(2,1)}, bf16[1,512,1024]{2,1,0:T(8,128)(2,1)}, u32[]{:S(2)}, u32[]{:S(2)}) collective-permute-start(bf16[1,512,1024]{2,1,0:T(8,128)(2,1)} %collective-permute-done.36.refs_1_), channel_id=1, source_target_pairs={{0,1},{1,0},{2,3},{3,2},{4,5},{5,4},{6,7},{7,6},{8,9},{9,8},{10,11... | collective-permute-start | bytes 3145736 | tf_op jit(solution)/shard_map/ppermute | solution.py:403
  449.4 82.3 %collective-permute-start.34 = (bf16[1,384,1024]{2,1,0:T(8,128)(2,1)}, bf16[1,384,1024]{2,1,0:T(8,128)(2,1)}, u32[]{:S(2)}, u32[]{:S(2)}) collective-permute-start(bf16[1,384,1024]{2,1,0:T(8,128)(2,1)} %collective-permute-done.33.refs_0_), channel_id=1, source_target_pairs={{0,1},{1,0},{2,3},{3,2},{4,5},{5,4},{6,7},{7,6},{8,9},{9,8},{10,11... | collective-permute-start | bytes 2359304 | tf_op jit(solution)/shard_map/ppermute | solution.py:403
  451.9 83.4 %collective-permute-start.47 = (bf16[1,128,1024]{2,1,0:T(8,128)(2,1)}, bf16[1,128,1024]{2,1,0:T(8,128)(2,1)}, u32[]{:S(2)}, u32[]{:S(2)}) collective-permute-start(bf16[1,128,1024]{2,1,0:T(8,128)(2,1)} %copy-done.54), channel_id=1, source_target_pairs={{0,1},{1,0},{2,3},{3,2},{4,5},{5,4},{6,7},{7,6},{8,9},{9,8},{10,11... | collective-permute-start | bytes 786440 | tf_op jit(solution)/shard_map/ppermute | solution.py:403
  (61 other events, 340.2 us)

commit v4 on v3

--- a/solution.py
+++ b/solution.py
@@ -20,23 +20,20 @@
     return share * train + (1.0 - share) * other
 
 
-def fetches(first, low, height, blocks, sources, held, sems):
-    step = height // blocks
-    return [
+def first_max_kernel(
+    first, mix_ref, train_ref, other_ref, top_ref, kept_ref, early_ref, share_ref, held, early, sems, mix_sem, early_sem
+):
+    rows, step = held.shape[1], early.shape[0]
+    blocks, kept = rows // step, kept_ref.shape[0] // step
+    copies = [
         [
             pltpu.make_async_copy(
-                ref.at[first, pl.ds(low + j * step, step)], held.at[k, pl.ds(j * step, step)], sems.at[k, j]
+                ref.at[first, pl.ds(j * step, step)], held.at[k, pl.ds(j * step, step)], sems.at[k, j]
             )
-            for k, ref in enumerate(sources)
+            for k, ref in enumerate((train_ref, other_ref))
         ]
         for j in range(blocks)
     ]
-
-
-def first_max_kernel(first, blocks, mix_ref, train_ref, other_ref, top_ref, early_ref, share_ref, held, early, sems, mix_sem, early_sem):
-    rows = held.shape[1]
-    step = rows // blocks
-    copies = fetches(first, 0, rows, blocks, (train_ref, other_ref), held, sems)
     for pair in copies:
         for copy in pair:
             copy.start()
@@ -52,38 +49,36 @@
 
         def body(i, top):
             at = pl.ds(pl.multiple_of(j * step + i * SUB, SUB), SUB)
-            return jnp.maximum(top, jnp.abs(mixed(share, held[0, at], held[1, at])))
-
-        def mix_rows(i, carry):
-            at = pl.ds(pl.multiple_of(i * SUB, SUB), SUB)
-            early[at] = mixed(share, held[0, at], held[1, at])
-            return carry
-
-        if j == 0:
-            lax.fori_loop(0, early.shape[0] // SUB, mix_rows, 0, unroll=2)
+            row = mixed(share, held[0, at], held[1, at])
+            if j == 0:
+                early[pl.ds(pl.multiple_of(i * SUB, SUB), SUB)] = row
+            elif j <= kept:
+                kept_ref[pl.ds(pl.multiple_of((j - 1) * step + i * SUB, SUB), SUB)] = row
+            return jnp.maximum(top, jnp.abs(row))
+
         top = lax.fori_loop(0, step // SUB, body, top, unroll=4)
-        if j == 1:
+        if j == min(2, blocks - 1):
             leave.start()
     top_ref[...] = jnp.max(top, axis=0, keepdims=True)
     leave.wait()
 
 
-def first_max(mix_share, train, other, first, early):
+def first_max(mix_share, train, other, first, early, kept):
     _, rows, cols = train.shape
-    blocks = 4
-    return pl.pallas_call(
-        functools.partial(first_max_kernel, first, blocks),
+    return pl.pallas_call(
+        functools.partial(first_max_kernel, first),
         out_shape=(
             jax.ShapeDtypeStruct((1, cols), jnp.float32),
+            jax.ShapeDtypeStruct((kept, cols), jnp.float32),
             jax.ShapeDtypeStruct((early, cols), jnp.float32),
         ),
         in_specs=[HBM, HBM, HBM],
-        out_specs=(pl.BlockSpec(memory_space=pltpu.VMEM), ANY),
+        out_specs=(pl.BlockSpec(memory_space=pltpu.VMEM), pl.BlockSpec(memory_space=pltpu.VMEM), ANY),
         scratch_shapes=[
             pltpu.SMEM(mix_share.shape, jnp.float32),
             pltpu.VMEM((2, rows, cols), jnp.float32),
             pltpu.VMEM((early, cols), jnp.float32),
-            pltpu.SemaphoreType.DMA((2, blocks)),
+            pltpu.SemaphoreType.DMA((2, rows // early)),
             pltpu.SemaphoreType.DMA,
             pltpu.SemaphoreType.DMA,
         ],
@@ -130,61 +125,27 @@
     return top
 
 
-def first_narrow_kernel(tops, piece, blocks, mix_ref, *refs):
-    first, _, low, height = piece
-    top_refs, (train_ref, other_ref, send_ref, share_ref, held, sems, mix_sem) = refs[:tops], refs[tops:]
-    step = height // blocks
-    copies = fetches(first, low, height, blocks, (train_ref, other_ref), held, sems)
-    b = pl.program_id(0)
-    mix = pltpu.make_async_copy(mix_ref, share_ref, mix_sem)
-
-    @pl.when(b == 0)
-    def _():
-        for pair in copies:
-            for copy in pair:
-                copy.start()
-        mix.start()
-        mix.wait()
-
-    for j, pair in enumerate(copies):
-
-        @pl.when(b == j)
-        def _():
-            for copy in pair:
-                copy.wait()
-
-    share = share_ref[first]
-    scale = jnp.broadcast_to(1.0 / top_of(top_refs, 0), (2 * SUB, held.shape[2]))
+def first_narrow_kernel(kept_ref, *refs):
+    tops, send_ref = refs[:-1], refs[-1]
+    scale = jnp.broadcast_to(1.0 / top_of(tops, 0), (2 * SUB, kept_ref.shape[1]))
 
     def body(i, carry):
-        at = pl.ds(pl.multiple_of(b * step + i * 2 * SUB, 2 * SUB), 2 * SUB)
-        part = mixed(share, held[0, at], held[1, at]) * scale
-        send_ref[0, pl.ds(pl.multiple_of(i * 2 * SUB, 2 * SUB), 2 * SUB)] = part.astype(jnp.bfloat16)
+        at = pl.ds(pl.multiple_of(i * 2 * SUB, 2 * SUB), 2 * SUB)
+        send_ref[0, at] = (kept_ref[at] * scale).astype(jnp.bfloat16)
         return carry
 
-    lax.fori_loop(0, step // (2 * SUB), body, 0, unroll=2)
-
-
-def first_narrow(mix_share, tops, train, other, piece):
-    cols = train.shape[2]
-    height = piece[3]
-    blocks = 2
-    return pl.pallas_call(
-        functools.partial(first_narrow_kernel, len(tops), piece, blocks),
+    lax.fori_loop(0, kept_ref.shape[0] // (2 * SUB), body, 0, unroll=2)
+
+
+def first_narrow(kept, tops):
+    height, cols = kept.shape
+    return pl.pallas_call(
+        first_narrow_kernel,
         out_shape=jax.ShapeDtypeStruct((1, height, cols), jnp.bfloat16),
-        grid=(blocks,),
-        in_specs=[HBM] + [pl.BlockSpec((1, cols), lambda b: (0, 0))] * len(tops) + [HBM, HBM],
-        out_specs=pl.BlockSpec((1, height // blocks, cols), lambda b: (0, b, 0)),
-        scratch_shapes=[
-            pltpu.SMEM(mix_share.shape, jnp.float32),
-            pltpu.VMEM((2, height, cols), jnp.float32),
-            pltpu.SemaphoreType.DMA((2, blocks)),
-            pltpu.SemaphoreType.DMA,
-        ],
-        compiler_params=PARAMS,
-        cost_estimate=pl.CostEstimate(flops=6 * height * cols, bytes_accessed=10 * height * cols, transcendentals=0),
+        compiler_params=PARAMS,
+        cost_estimate=pl.CostEstimate(flops=2 * height * cols, bytes_accessed=6 * height * cols, transcendentals=0),
         name="first_narrow",
-    )(mix_share, *tops, train, other)
+    )(kept, *tops)
 
 
 def narrow_kernel(first, at, tops, place_ref, mix_ref, *refs):
@@ -370,7 +331,7 @@
     tail = max(experts - 2, 0)
     pieces += [(1, (e, n, 0, rows)) for e, n in runs(0, tail, 3)]
     pieces += [(1, (e, n, 0, rows)) for e, n in runs(tail, experts - 1, 1)]
-    cut = rows - rows // 4
+    cut = rows - rows * 3 // 16 // 16 * 16
     pieces += [(1, (experts - 1, 1, 0, cut)), (1, (experts - 1, 1, cut, rows - cut))]
     return groups, pieces, early
 
@@ -411,7 +372,8 @@
     tops = []
     for g, (a, first, count) in enumerate(groups):
         if g == 0:
-            top, ahead = first_max(mix_share, train[a], other[a], first, early)
+            share = pltpu.with_memory_space_constraint(mix_share, pltpu.HBM) if experts > 1 else mix_share
+            top, kept, ahead = first_max(share, train[a], other[a], first, early, pieces[0][1][3])
         else:
             top = local_max(mix_share, train[a], other[a], first, count)
         tops.append(spread(top))
@@ -421,7 +383,7 @@
     for i, (a, piece) in enumerate(pieces):
         g = group_of(groups, a, piece[0])
         if i == 0:
-            own = first_narrow(mix_share, tops[g], train[a], other[a], piece)
+            own = first_narrow(kept, tops[g])
         else:
             own, whole[a] = narrow(
                 place, mix_share, tops[g], piece[0] - groups[g][1], train[a], other[a], piece, parts, whole[a]
@@ -439,7 +401,7 @@
         place_rows(i, [1])
     for i in range(len(pieces)):
         slots = list(range(0 if i == 0 else 2 if i in early_puts else 1, parts))
-        if i + 1 == len(pieces) and len(slots) > 1:
+        if i in early_puts:
             a, (expert, _, low, _) = pieces[i]
             for j in slots:
                 whole[a] = lax.dynamic_update_slice(

time: 538 us -> 538 us (level)
  waiting for transfers between devices: 322 us -> 316 us
    pallas_call x10, Pallas kernels: 53.8 us -> 60.1 us  [narrow(): pl.pallas_call(functools.partial(narrow_kernel, first, at, len(tops)), ou...]
    pallas_call x12 -> x11, Pallas kernels: 46.1 us -> 43.6 us  [put(): pl.pallas_call(functools.partial(put_kernel, tuple(slots), piece, rows),...]
    unnamed x116 -> x114, local copies, waits for them, and re-layouts: 21.8 us -> 19.6 us
  transfers between devices with their start and end apart: 51 -> 51, of which waited for: 15 -> 12; matrix products, arithmetic and copies ran while one was open for 0% -> 1% of each run, Pallas kernels for 22% -> 23%
where the time goes in v4:
time: 538 us; the launch traced here: 537 us
  waiting for transfers between devices  316 us (59%)
  Pallas kernels  135 us (25%)
  blocking collectives  31.1 us (6%)
  local copies, waits for them, and re-layouts  26.6 us (5%)
  starting transfers between devices  24.5 us (5%)
    ppermute x17, waiting for transfers between devices, spread(): got.append(lax.ppermute(x, 'fsdp', step(k, 0)))  308 us
    pallas_call x10, Pallas kernels, narrow(): pl.pallas_call(functools.partial(narrow_kernel, first, at, len(tops)), ou...  60.1 us
    pallas_call x11, Pallas kernels, put(): pl.pallas_call(functools.partial(put_kernel, tuple(slots), piece, rows),...  43.6 us
    all_gather x1, blocking collectives, per_device(): wide_router = lax.all_gather(row_router, 'ep', axis=1, tiled=True)  31.1 us
    pallas_call x3, Pallas kernels, local_max(): pl.pallas_call(functools.partial(max_kernel, first), out_shape=jax.ShapeD...  25 us
    unnamed x114, local copies, waits for them, and re-layouts  19.6 us
    ppermute x17, starting transfers between devices, spread(): got.append(lax.ppermute(x, 'fsdp', step(k, 0)))  18.1 us
  transfers between devices with their start and end apart: 51, of which 12 were waited for; matrix products, arithmetic and copies ran while one was open for 1% of the time, Pallas kernels for 23%

profile of v4, /device:TPU:0, one launch (start us, length us, event | category | flops | bytes accessed | tf_op | source)
XLA Modules:
  0.0 537.3 jit_solution(13502810833685050038)
XLA Ops:
  1.3 12.7 %local_max.5.refs_0_.refs_12_ = f32[8,1024]{1,0:T(8,128)S(1)} custom-call(f32[8]{0:T(128)S(1)} %copy-done.44, f32[8,512,1024]{2,1,0:T(8,128)} %refs_4_.19, f32[8,512,1024]{2,1,0:T(8,128)} %refs_5_.19), custom_call_target="tpu_custom_call" | custom-call | flops 20971520 | bytes 33554432 | tf_op jit(solution)/shard_map/local_max/pallas_call | solution.py:107
  14.0 3.0 collective-permute-start.31
  17.0 2.4 first_max.1
  20.0 3.9 local_max.4.refs_0_.refs_4_
  24.0 1.7 collective-permute-start.4
  28.4 3.5 narrow.10
  32.3 8.3 %narrow.15 = (bf16[3,512,1024]{2,1,0:T(8,128)(2,1)S(1)}, bf16[8,2048,1024]{2,1,0:T(8,128)(2,1)}) custom-call(s32[4]{0:T(128)S(1)} %get-tuple-element.58.place_ref, f32[8]{0:T(128)S(1)} %copy-done.45, f32[8,1024]{1,0:T(8,128)S(1)} %local_max.5.refs_0_.refs_12_, f32[8,1024]{1,0:T(8,128)S(1)} %collective-permute-done.30.refs_1_.refs_13_, ...), custom_call_target="tpu_custom_call" | custom-call | flops 9437184 | bytes 18874368 | tf_op jit(solution)/shard_map/narrow/pallas_call | solution.py:175
  40.6 9.2 %narrow.16 = (bf16[3,512,1024]{2,1,0:T(8,128)(2,1)}, bf16[8,2048,1024]{2,1,0:T(8,128)(2,1)}) custom-call(s32[4]{0:T(128)S(1)} %get-tuple-element.58.place_ref, f32[8]{0:T(128)S(1)} %copy-done.45, f32[8,1024]{1,0:T(8,128)S(1)} %local_max.5.refs_0_.refs_12_, f32[8,1024]{1,0:T(8,128)S(1)} %collective-permute-done.30.refs_1_.refs_13_, ...), custom_call_target="tpu_custom_call", output_to_operand_aliasing={{1}: (8, {})} | custom-call | flops 9437184 | bytes 18874368 | tf_op jit(solution)/shard_map/narrow/pallas_call | solution.py:175
  49.8 3.8 narrow.17
  54.6 8.8 %narrow.18 = (bf16[1,416,1024]{2,1,0:T(8,128)(2,1)S(1)}, bf16[8,2048,1024]{2,1,0:T(8,128)(2,1)}) custom-call(s32[4]{0:T(128)S(1)} %get-tuple-element.58.place_ref, f32[8]{0:T(128)S(1)} %copy-done.45, f32[8,1024]{1,0:T(8,128)S(1)} %local_max.5.refs_0_.refs_12_, ...), custom_call_target="tpu_custom_call", output_to_operand_aliasing={{1}: (8, {})} | custom-call | flops 2555904 | bytes 5111808 | tf_op jit(solution)/shard_map/narrow/pallas_call | solution.py:175
  63.4 3.3 narrow.19
  66.9 1.7 collective-permute-start.46
  69.1 8.4 %local_max.3.refs_0_.refs_8_ = f32[5,1024]{1,0:T(8,128)S(1)} custom-call(f32[8]{0:T(128)S(1)} %copy-done.45, f32[8,512,1024]{2,1,0:T(8,128)} %refs_4_.14, f32[8,512,1024]{2,1,0:T(8,128)} %refs_5_.14), custom_call_target="tpu_custom_call" | custom-call | flops 13107200 | bytes 20971520 | tf_op jit(solution)/shard_map/local_max/pallas_call | solution.py:107
  77.5 1.7 collective-permute-start.1
  84.3 1.4 collective-permute-start.25
  85.9 6.0 %collective-permute-done.28.refs_6_ = f32[64,1024]{1,0:T(8,128)S(1)} collective-permute-done((f32[64,1024]{1,0:T(8,128)S(1)}, f32[64,1024]{1,0:T(8,128)S(1)}, u32[]{:S(2)}, u32[]{:S(2)}) %collective-permute-start.28) | collective-permute-done | bytes 262176 | tf_op jit(solution)/shard_map/ppermute | solution.py:362
  93.7 3.9 narrow.11
  98.2 5.1 collective-permute-done.25.refs_2_
  103.7 3.9 narrow.12
  108.4 1.7 collective-permute-start.16
  111.0 9.2 %narrow.13 = (bf16[3,512,1024]{2,1,0:T(8,128)(2,1)}, bf16[8,2048,1024]{2,1,0:T(8,128)(2,1)}) custom-call(s32[4]{0:T(128)S(1)} %get-tuple-element.58.place_ref, f32[8]{0:T(128)S(1)} %copy-done.45, f32[5,1024]{1,0:T(8,128)S(1)} %local_max.3.refs_0_.refs_8_, f32[5,1024]{1,0:T(8,128)S(1)} %collective-permute-done.refs_1_.refs_9_, ...), custom_call_target="tpu_custom_call", output_to_operand_aliasing={{1}: (8, {})} | custom-call | flops 9437184 | bytes 18874368 | tf_op jit(solution)/shard_map/narrow/pallas_call | solution.py:175
  120.2 6.0 %narrow.14 = (bf16[2,512,1024]{2,1,0:T(8,128)(2,1)S(1)}, bf16[8,2048,1024]{2,1,0:T(8,128)(2,1)}) custom-call(s32[4]{0:T(128)S(1)} %get-tuple-element.58.place_ref, f32[8]{0:T(128)S(1)} %copy-done.45, f32[5,1024]{1,0:T(8,128)S(1)} %local_max.3.refs_0_.refs_8_, f32[5,1024]{1,0:T(8,128)S(1)} %collective-permute-done.refs_1_.refs_9_, ...), custom_call_target="tpu_custom_call", output_to_operand_aliasing={{1}: (8, {})} | custom-call | flops 6291456 | bytes 12582912 | tf_op jit(solution)/shard_map/narrow/pallas_call | solution.py:175
  126.3 17.8 %collective-permute-done.44 = bf16[1,416,1024]{2,1,0:T(8,128)(2,1)} collective-permute-done((bf16[1,416,1024]{2,1,0:T(8,128)(2,1)S(1)}, bf16[1,416,1024]{2,1,0:T(8,128)(2,1)}, u32[]{:S(2)}, u32[]{:S(2)}) %collective-permute-start.44) | collective-permute-done | bytes 852000 | tf_op jit(solution)/shard_map/ppermute | solution.py:362
  146.5 1.7 collective-permute-start.34
  148.1 18.3 %collective-permute-done.16.refs_1_ = bf16[1,512,1024]{2,1,0:T(8,128)(2,1)S(1)} collective-permute-done((bf16[1,512,1024]{2,1,0:T(8,128)(2,1)}, bf16[1,512,1024]{2,1,0:T(8,128)(2,1)S(1)}, u32[]{:S(2)}, u32[]{:S(2)}) %collective-permute-start.16) | collective-permute-done | bytes 1048608 | tf_op jit(solution)/shard_map/ppermute | solution.py:362
  169.9 63.2 %collective-permute-done.34.refs_1_ = bf16[1,512,1024]{2,1,0:T(8,128)(2,1)} collective-permute-done((bf16[1,512,1024]{2,1,0:T(8,128)(2,1)S(1)}, bf16[1,512,1024]{2,1,0:T(8,128)(2,1)}, u32[]{:S(2)}, u32[]{:S(2)}) %collective-permute-start.34) | collective-permute-done | bytes 1048608 | tf_op jit(solution)/shard_map/ppermute | solution.py:362
  234.8 1.3 collective-permute-start.40
  239.4 65.0 %collective-permute-done.13.refs_1_ = bf16[3,512,1024]{2,1,0:T(8,128)(2,1)S(1)} collective-permute-done((bf16[3,512,1024]{2,1,0:T(8,128)(2,1)}, bf16[3,512,1024]{2,1,0:T(8,128)(2,1)S(1)}, u32[]{:S(2)}, u32[]{:S(2)}) %collective-permute-start.13) | collective-permute-done | bytes 3145760 | tf_op jit(solution)/shard_map/ppermute | solution.py:362
  304.3 67.4 %collective-permute-done.40.refs_1_ = bf16[3,512,1024]{2,1,0:T(8,128)(2,1)S(1)} collective-permute-done((bf16[3,512,1024]{2,1,0:T(8,128)(2,1)S(1)}, bf16[3,512,1024]{2,1,0:T(8,128)(2,1)S(1)}, u32[]{:S(2)}, u32[]{:S(2)}) %collective-permute-start.40) | collective-permute-done | bytes 3145760 | tf_op jit(solution)/shard_map/ppermute | solution.py:362
  372.3 65.3 %collective-permute-done.37.refs_1_ = bf16[3,512,1024]{2,1,0:T(8,128)(2,1)} collective-permute-done((bf16[3,512,1024]{2,1,0:T(8,128)(2,1)}, bf16[3,512,1024]{2,1,0:T(8,128)(2,1)}, u32[]{:S(2)}, u32[]{:S(2)}) %collective-permute-start.37) | collective-permute-done | bytes 3145760 | tf_op jit(solution)/shard_map/ppermute | solution.py:362
  437.6 1.7 copy-done
  439.8 1.3 copy-done.4
  441.1 5.4 collective-permute-done.11.refs_2_
  451.7 31.1 %all_gather.3 = bf16[2048,64]{0,1:T(8,128)(2,1)S(1)} all-gather(bf16[2048,8]{0,1:T(8,128)(2,1)S(1)} %constant_dynamic-update-slice_fusion), channel_id=1, replica_groups=mesh['ep'=8,'fsdp'=4] {'ep'}, dimensions={1}, use_global_device_ids=true | all-gather | bytes 294912 | tf_op jit(solution)/shard_map/all_gather | solution.py:418
  485.4 1.6 put.17.refs_1_
  487.0 2.1 finish.1.refs_4_
  489.1 1.5 put.18.refs_3_
  490.7 2.1 put.11.refs_3_
  492.8 2.2 put.12.refs_3_
  495.1 2.5 put.13.refs_3_
  497.6 2.5 put.14.refs_3_
  500.1 7.8 %put.15.refs_3_ = bf16[8,2048,1024]{2,1,0:T(8,128)(2,1)} custom-call(s32[4]{0:T(128)S(1)} %get-tuple-element.58.place_ref, bf16[3,512,1024]{2,1,0:T(8,128)(2,1)S(1)} %collective-permute-done.12.refs_0_, bf16[3,512,1024]{2,1,0:T(8,128)(2,1)} %copy-done.49, bf16[3,512,1024]{2,1,0:T(8,128)(2,1)} %copy-done.51, ...), custom_call_target="tpu_custom_call", output_to_operand_aliasing={{}: (4, {})} | custom-call | flops 4718592 | bytes 18874368 | tf_op jit(solution)/shard_map/put/pallas_call | solution.py:266
  507.9 5.1 put.16
  513.0 7.3 %put.19.refs_3_ = bf16[8,2048,1024]{2,1,0:T(8,128)(2,1)} custom-call(s32[4]{0:T(128)S(1)} %get-tuple-element.58.place_ref, bf16[3,512,1024]{2,1,0:T(8,128)(2,1)S(1)} %copy-done.1, bf16[3,512,1024]{2,1,0:T(8,128)(2,1)} %copy-done.48, bf16[3,512,1024]{2,1,0:T(8,128)(2,1)} %copy-done.50, bf16[8,2048,1024]{2,1,0:T(8,128)(2,1)} %put.18.refs_3_), custom_call_target="tpu_custom_call", output_to_operand_aliasing={{}: (4, {})} | custom-call | flops 4718592 | bytes 18874368 | tf_op jit(solution)/shard_map/put/pallas_call | solution.py:266
  520.4 7.7 %put.20.refs_3_ = bf16[8,2048,1024]{2,1,0:T(8,128)(2,1)} custom-call(s32[4]{0:T(128)S(1)} %get-tuple-element.58.place_ref, bf16[3,512,1024]{2,1,0:T(8,128)(2,1)} %collective-permute-done.36.refs_0_, bf16[3,512,1024]{2,1,0:T(8,128)(2,1)} %collective-permute-done.37.refs_1_, ...), custom_call_target="tpu_custom_call", output_to_operand_aliasing={{}: (4, {})} | custom-call | flops 4718592 | bytes 18874368 | tf_op jit(solution)/shard_map/put/pallas_call | solution.py:266
  528.2 3.5 put.21
  531.6 2.1 constant_dynamic-update-slice_fusion.7
  533.8 2.1 constant_dynamic-update-slice_fusion.6
  (209 shorter events, 34.0 us)
Async XLA Ops:
  14.0 12.4 %collective-permute-start.31 = (f32[8,1024]{1,0:T(8,128)S(1)}, f32[8,1024]{1,0:T(8,128)S(1)}, u32[]{:S(2)}, u32[]{:S(2)}) collective-permute-start(f32[8,1024]{1,0:T(8,128)S(1)} %local_max.5.refs_0_.refs_12_), channel_id=1, source_target_pairs={{0,2},{1,3},{2,0},{3,1},{4,6},{5,7},{6,4},{7,5},{8,10},{9,11},{10,... | collective-permute-start | bytes 98312 | tf_op jit(solution)/shard_map/ppermute | solution.py:362
  17.0 15.3 %collective-permute-start.30 = (f32[8,1024]{1,0:T(8,128)S(1)}, f32[8,1024]{1,0:T(8,128)S(1)}, u32[]{:S(2)}, u32[]{:S(2)}) collective-permute-start(f32[8,1024]{1,0:T(8,128)S(1)} %local_max.5.refs_0_.refs_12_), channel_id=1, source_target_pairs={{0,1},{1,0},{2,3},{3,2},{4,5},{5,4},{6,7},{7,6},{8,9},{9,8},{10,11... | collective-permute-start | bytes 98312 | tf_op jit(solution)/shard_map/ppermute | solution.py:360
  19.4 7.0 %collective-permute-start.7 = (f32[1,1024]{1,0:T(1,128)S(1)}, f32[1,1024]{1,0:T(1,128)S(1)}, u32[]{:S(2)}, u32[]{:S(2)}) collective-permute-start(f32[1,1024]{1,0:T(1,128)S(1)} %get-tuple-element.30.refs_0_), channel_id=1, source_target_pairs={{0,2},{1,3},{2,0},{3,1},{4,6},{5,7},{6,4},{7,5},{8,10},{9,11},{10,... | collective-permute-start | bytes 12296 | tf_op jit(solution)/shard_map/ppermute | solution.py:362
  19.5 8.7 %collective-permute-start.6 = (f32[1,1024]{1,0:T(1,128)S(1)}, f32[1,1024]{1,0:T(1,128)S(1)}, u32[]{:S(2)}, u32[]{:S(2)}) collective-permute-start(f32[1,1024]{1,0:T(1,128)S(1)} %get-tuple-element.30.refs_0_), channel_id=1, source_target_pairs={{0,1},{1,0},{2,3},{3,2},{4,5},{5,4},{6,7},{7,6},{8,9},{9,8},{10,11... | collective-permute-start | bytes 12296 | tf_op jit(solution)/shard_map/ppermute | solution.py:360
  24.0 44.6 %collective-permute-start.4 = (f32[2,1024]{1,0:T(2,128)S(1)}, f32[2,1024]{1,0:T(2,128)S(1)}, u32[]{:S(2)}, u32[]{:S(2)}) collective-permute-start(f32[2,1024]{1,0:T(2,128)S(1)} %local_max.4.refs_0_.refs_4_), channel_id=1, source_target_pairs={{0,2},{1,3},{2,0},{3,1},{4,6},{5,7},{6,4},{7,5},{8,10},{9,11},{10,... | collective-permute-start | bytes 24584 | tf_op jit(solution)/shard_map/ppermute | solution.py:362
  26.4 2.0 collective-permute-start.8
  26.4 5.9 %collective-permute-start.32 = (f32[8,1024]{1,0:T(8,128)S(1)}, f32[8,1024]{1,0:T(8,128)S(1)}, u32[]{:S(2)}, u32[]{:S(2)}) collective-permute-start(f32[8,1024]{1,0:T(8,128)S(1)} %collective-permute-done.31.refs_2_.refs_14_), channel_id=1, source_target_pairs={{0,1},{1,0},{2,3},{3,2},{4,5},{5,4},{6,7},{7,6},{8,9},{9,8},{10,11... | collective-permute-start | bytes 98312 | tf_op jit(solution)/shard_map/ppermute | solution.py:364
  28.2 40.5 %collective-permute-start.3 = (f32[2,1024]{1,0:T(2,128)S(1)}, f32[2,1024]{1,0:T(2,128)S(1)}, u32[]{:S(2)}, u32[]{:S(2)}) collective-permute-start(f32[2,1024]{1,0:T(2,128)S(1)} %local_max.4.refs_0_.refs_4_), channel_id=1, source_target_pairs={{0,1},{1,0},{2,3},{3,2},{4,5},{5,4},{6,7},{7,6},{8,9},{9,8},{10,11... | collective-permute-start | bytes 24584 | tf_op jit(solution)/shard_map/ppermute | solution.py:360
  31.9 61.3 %collective-permute-start.22 = (bf16[1,192,1024]{2,1,0:T(8,128)(2,1)S(1)}, bf16[1,192,1024]{2,1,0:T(8,128)(2,1)S(1)}, u32[]{:S(2)}, u32[]{:S(2)}) collective-permute-start(bf16[1,192,1024]{2,1,0:T(8,128)(2,1)S(1)} %get-tuple-element.39), channel_id=1, source_target_pairs={{0,2},{1,3},{2,0},{3,1},{4,6},{5,7},{6,4},{7,5},{8,10},{9,11},{10,... | collective-permute-start | bytes 1179656 | tf_op jit(solution)/shard_map/ppermute | solution.py:362
  66.7 16.8 %collective-permute-start.42 = (bf16[1,96,1024]{2,1,0:T(8,128)(2,1)S(1)}, bf16[1,96,1024]{2,1,0:T(8,128)(2,1)S(1)}, u32[]{:S(2)}, u32[]{:S(2)}) collective-permute-start(bf16[1,96,1024]{2,1,0:T(8,128)(2,1)S(1)} %get-tuple-element.50), channel_id=1, source_target_pairs={{0,1},{1,0},{2,3},{3,2},{4,5},{5,4},{6,7},{7,6},{8,9},{9,8},{10,11... | collective-permute-start | bytes 589832 | tf_op jit(solution)/shard_map/ppermute | solution.py:360
  66.9 18.8 %collective-permute-start.46 = (bf16[1,96,1024]{2,1,0:T(8,128)(2,1)S(1)}, bf16[1,96,1024]{2,1,0:T(8,128)(2,1)S(1)}, u32[]{:S(2)}, u32[]{:S(2)}) collective-permute-start(bf16[1,96,1024]{2,1,0:T(8,128)(2,1)S(1)} %get-tuple-element.50), channel_id=1, source_target_pairs={{0,2},{1,3},{2,0},{3,1},{4,6},{5,7},{6,4},{7,5},{8,10},{9,11},{10,... | collective-permute-start | bytes 589832 | tf_op jit(solution)/shard_map/ppermute | solution.py:362
  68.6 8.9 %collective-permute-start.48 = (bf16[512,8]{0,1:T(8,128)(2,1)S(1)}, bf16[512,8]{0,1:T(8,128)(2,1)S(1)}, u32[]{:S(2)}, u32[]{:S(2)}) collective-permute-start(bf16[512,8]{0,1:T(8,128)(2,1)S(1)} %get-tuple-element.56), channel_id=1, source_target_pairs={{0,1},{1,0},{2,3},{3,2},{4,5},{5,4},{6,7},{7,6},{8,9},{9,8},{10,11... | collective-permute-start | bytes 24584 | tf_op jit(solution)/shard_map/ppermute | solution.py:360
  68.7 10.5 %collective-permute-start.49 = (bf16[512,8]{0,1:T(8,128)(2,1)S(1)}, bf16[512,8]{0,1:T(8,128)(2,1)S(1)}, u32[]{:S(2)}, u32[]{:S(2)}) collective-permute-start(bf16[512,8]{0,1:T(8,128)(2,1)S(1)} %get-tuple-element.56), channel_id=1, source_target_pairs={{0,2},{1,3},{2,0},{3,1},{4,6},{5,7},{6,4},{7,5},{8,10},{9,11},{10,... | collective-permute-start | bytes 24584 | tf_op jit(solution)/shard_map/ppermute | solution.py:362
  77.5 4.3 collective-permute-start.1
  81.8 1.4 collective-permute-start.2
  82.8 9.2 %collective-permute-start.28 = (f32[64,1024]{1,0:T(8,128)S(1)}, f32[64,1024]{1,0:T(8,128)S(1)}, u32[]{:S(2)}, u32[]{:S(2)}) collective-permute-start(f32[64,1024]{1,0:T(8,128)S(1)} %get-tuple-element.41.refs_4_), channel_id=1, source_target_pairs={{0,2},{1,3},{2,0},{3,1},{4,6},{5,7},{6,4},{7,5},{8,10},{9,11},{10,... | collective-permute-start | bytes 786440 | tf_op jit(solution)/shard_map/ppermute | solution.py:362
  83.2 8.8 %collective-permute-start.27 = (f32[64,1024]{1,0:T(8,128)S(1)}, f32[64,1024]{1,0:T(8,128)S(1)}, u32[]{:S(2)}, u32[]{:S(2)}) collective-permute-start(f32[64,1024]{1,0:T(8,128)S(1)} %get-tuple-element.41.refs_4_), channel_id=1, source_target_pairs={{0,1},{1,0},{2,3},{3,2},{4,5},{5,4},{6,7},{7,6},{8,9},{9,8},{10,11... | collective-permute-start | bytes 786440 | tf_op jit(solution)/shard_map/ppermute | solution.py:360
  84.3 19.0 %collective-permute-start.25 = (bf16[1,256,1024]{2,1,0:T(8,128)(2,1)S(1)}, bf16[1,256,1024]{2,1,0:T(8,128)(2,1)S(1)}, u32[]{:S(2)}, u32[]{:S(2)}) collective-permute-start(bf16[1,256,1024]{2,1,0:T(8,128)(2,1)S(1)} %first_narrow.1.refs_0_), channel_id=1, source_target_pairs={{0,2},{1,3},{2,0},{3,1},{4,6},{5,7},{6,4},{7,5},{8,10},{9,11},{10,... | collective-permute-start | bytes 1572872 | tf_op jit(solution)/shard_map/ppermute | solution.py:362
  85.7 7.6 %collective-permute-start.21 = (bf16[1,192,1024]{2,1,0:T(8,128)(2,1)S(1)}, bf16[1,192,1024]{2,1,0:T(8,128)(2,1)S(1)}, u32[]{:S(2)}, u32[]{:S(2)}) collective-permute-start(bf16[1,192,1024]{2,1,0:T(8,128)(2,1)S(1)} %get-tuple-element.39), channel_id=1, source_target_pairs={{0,1},{1,0},{2,3},{3,2},{4,5},{5,4},{6,7},{7,6},{8,9},{9,8},{10,11... | collective-permute-start | bytes 1179656 | tf_op jit(solution)/shard_map/ppermute | solution.py:360
  92.0 11.2 %collective-permute-start.24 = (bf16[1,256,1024]{2,1,0:T(8,128)(2,1)S(1)}, bf16[1,256,1024]{2,1,0:T(8,128)(2,1)S(1)}, u32[]{:S(2)}, u32[]{:S(2)}) collective-permute-start(bf16[1,256,1024]{2,1,0:T(8,128)(2,1)S(1)} %first_narrow.1.refs_0_), channel_id=1, source_target_pairs={{0,1},{1,0},{2,3},{3,2},{4,5},{5,4},{6,7},{7,6},{8,9},{9,8},{10,11... | collective-permute-start | bytes 1572872 | tf_op jit(solution)/shard_map/ppermute | solution.py:360
  92.7 17.3 %collective-permute-start.43 = (bf16[1,416,1024]{2,1,0:T(8,128)(2,1)S(1)}, bf16[1,416,1024]{2,1,0:T(8,128)(2,1)S(1)}, u32[]{:S(2)}, u32[]{:S(2)}) collective-permute-start(bf16[1,416,1024]{2,1,0:T(8,128)(2,1)S(1)} %get-tuple-element.51), channel_id=1, source_target_pairs={{0,1},{1,0},{2,3},{3,2},{4,5},{5,4},{6,7},{7,6},{8,9},{9,8},{10,11... | collective-permute-start | bytes 2555912 | tf_op jit(solution)/shard_map/ppermute | solution.py:360
  93.2 4.5 collective-permute-start.29
  93.3 14.3 %collective-permute-start.23 = (bf16[1,192,1024]{2,1,0:T(8,128)(2,1)S(1)}, bf16[1,192,1024]{2,1,0:T(8,128)(2,1)S(1)}, u32[]{:S(2)}, u32[]{:S(2)}) collective-permute-start(bf16[1,192,1024]{2,1,0:T(8,128)(2,1)S(1)} %collective-permute-done.22.refs_1_), channel_id=1, source_target_pairs={{0,1},{1,0},{2,3},{3,2},{4,5},{5,4},{6,7},{7,6},{8,9},{9,8},{10,11... | collective-permute-start | bytes 1179656 | tf_op jit(solution)/shard_map/ppermute | solution.py:364
  97.7 47.5 %collective-permute-start.19 = (bf16[1,512,1024]{2,1,0:T(8,128)(2,1)}, bf16[1,512,1024]{2,1,0:T(8,128)(2,1)S(1)}, u32[]{:S(2)}, u32[]{:S(2)}) collective-permute-start(bf16[1,512,1024]{2,1,0:T(8,128)(2,1)} %get-tuple-element.38), channel_id=1, source_target_pairs={{0,2},{1,3},{2,0},{3,1},{4,6},{5,7},{6,4},{7,5},{8,10},{9,11},{10,... | collective-permute-start | bytes 3145736 | tf_op jit(solution)/shard_map/ppermute | solution.py:362
  103.2 42.3 %collective-permute-start.18 = (bf16[1,512,1024]{2,1,0:T(8,128)(2,1)}, bf16[1,512,1024]{2,1,0:T(8,128)(2,1)S(1)}, u32[]{:S(2)}, u32[]{:S(2)}) collective-permute-start(bf16[1,512,1024]{2,1,0:T(8,128)(2,1)} %get-tuple-element.38), channel_id=1, source_target_pairs={{0,1},{1,0},{2,3},{3,2},{4,5},{5,4},{6,7},{7,6},{8,9},{9,8},{10,11... | collective-permute-start | bytes 3145736 | tf_op jit(solution)/shard_map/ppermute | solution.py:360
  103.2 40.8 %collective-permute-start.44 = (bf16[1,416,1024]{2,1,0:T(8,128)(2,1)S(1)}, bf16[1,416,1024]{2,1,0:T(8,128)(2,1)}, u32[]{:S(2)}, u32[]{:S(2)}) collective-permute-start(bf16[1,416,1024]{2,1,0:T(8,128)(2,1)S(1)} %get-tuple-element.51), channel_id=1, source_target_pairs={{0,2},{1,3},{2,0},{3,1},{4,6},{5,7},{6,4},{7,5},{8,10},{9,11},{10,... | collective-permute-start | bytes 2555912 | tf_op jit(solution)/shard_map/ppermute | solution.py:362
  108.4 58.0 %collective-permute-start.16 = (bf16[1,512,1024]{2,1,0:T(8,128)(2,1)}, bf16[1,512,1024]{2,1,0:T(8,128)(2,1)S(1)}, u32[]{:S(2)}, u32[]{:S(2)}) collective-permute-start(bf16[1,512,1024]{2,1,0:T(8,128)(2,1)} %get-tuple-element.37), channel_id=1, source_target_pairs={{0,2},{1,3},{2,0},{3,1},{4,6},{5,7},{6,4},{7,5},{8,10},{9,11},{10,... | collective-permute-start | bytes 3145736 | tf_op jit(solution)/shard_map/ppermute | solution.py:362
  111.0 33.1 %collective-permute-start.26 = (bf16[1,256,1024]{2,1,0:T(8,128)(2,1)S(1)}, bf16[1,256,1024]{2,1,0:T(8,128)(2,1)S(1)}, u32[]{:S(2)}, u32[]{:S(2)}) collective-permute-start(bf16[1,256,1024]{2,1,0:T(8,128)(2,1)S(1)} %collective-permute-done.25.refs_2_), channel_id=1, source_target_pairs={{0,1},{1,0},{2,3},{3,2},{4,5},{5,4},{6,7},{7,6},{8,9},{9,8},{10,11... | collective-permute-start | bytes 1572872 | tf_op jit(solution)/shard_map/ppermute | solution.py:364
  144.1 23.4 %collective-permute-start.15 = (bf16[1,512,1024]{2,1,0:T(8,128)(2,1)}, bf16[1,512,1024]{2,1,0:T(8,128)(2,1)S(1)}, u32[]{:S(2)}, u32[]{:S(2)}) collective-permute-start(bf16[1,512,1024]{2,1,0:T(8,128)(2,1)} %get-tuple-element.37), channel_id=1, source_target_pairs={{0,1},{1,0},{2,3},{3,2},{4,5},{5,4},{6,7},{7,6},{8,9},{9,8},{10,11... | collective-permute-start | bytes 3145736 | tf_op jit(solution)/shard_map/ppermute | solution.py:360
  144.9 92.2 %collective-permute-start.10 = (bf16[2,512,1024]{2,1,0:T(8,128)(2,1)S(1)}, bf16[2,512,1024]{2,1,0:T(8,128)(2,1)S(1)}, u32[]{:S(2)}, u32[]{:S(2)}) collective-permute-start(bf16[2,512,1024]{2,1,0:T(8,128)(2,1)S(1)} %get-tuple-element.35), channel_id=1, source_target_pairs={{0,2},{1,3},{2,0},{3,1},{4,6},{5,7},{6,4},{7,5},{8,10},{9,11},{10,... | collective-permute-start | bytes 6291464 | tf_op jit(solution)/shard_map/ppermute | solution.py:362
  145.3 92.6 %collective-permute-start.9 = (bf16[2,512,1024]{2,1,0:T(8,128)(2,1)S(1)}, bf16[2,512,1024]{2,1,0:T(8,128)(2,1)S(1)}, u32[]{:S(2)}, u32[]{:S(2)}) collective-permute-start(bf16[2,512,1024]{2,1,0:T(8,128)(2,1)S(1)} %get-tuple-element.35), channel_id=1, source_target_pairs={{0,1},{1,0},{2,3},{3,2},{4,5},{5,4},{6,7},{7,6},{8,9},{9,8},{10,11... | collective-permute-start | bytes 6291464 | tf_op jit(solution)/shard_map/ppermute | solution.py:360
  146.5 86.7 %collective-permute-start.34 = (bf16[1,512,1024]{2,1,0:T(8,128)(2,1)S(1)}, bf16[1,512,1024]{2,1,0:T(8,128)(2,1)}, u32[]{:S(2)}, u32[]{:S(2)}) collective-permute-start(bf16[1,512,1024]{2,1,0:T(8,128)(2,1)S(1)} %copy-done.47), channel_id=1, source_target_pairs={{0,2},{1,3},{2,0},{3,1},{4,6},{5,7},{6,4},{7,5},{8,10},{9,11},{10,... | collective-permute-start | bytes 3145736 | tf_op jit(solution)/shard_map/ppermute | solution.py:362
  166.4 67.4 %collective-permute-start.20 = (bf16[1,512,1024]{2,1,0:T(8,128)(2,1)S(1)}, bf16[1,512,1024]{2,1,0:T(8,128)(2,1)S(1)}, u32[]{:S(2)}, u32[]{:S(2)}) collective-permute-start(bf16[1,512,1024]{2,1,0:T(8,128)(2,1)S(1)} %collective-permute-done.19.refs_1_), channel_id=1, source_target_pairs={{0,1},{1,0},{2,3},{3,2},{4,5},{5,4},{6,7},{7,6},{8,9},{9,8},{10,11... | collective-permute-start | bytes 3145736 | tf_op jit(solution)/shard_map/ppermute | solution.py:364
  168.4 67.8 %collective-permute-start.17 = (bf16[1,512,1024]{2,1,0:T(8,128)(2,1)S(1)}, bf16[1,512,1024]{2,1,0:T(8,128)(2,1)S(1)}, u32[]{:S(2)}, u32[]{:S(2)}) collective-permute-start(bf16[1,512,1024]{2,1,0:T(8,128)(2,1)S(1)} %collective-permute-done.16.refs_1_), channel_id=1, source_target_pairs={{0,1},{1,0},{2,3},{3,2},{4,5},{5,4},{6,7},{7,6},{8,9},{9,8},{10,11... | collective-permute-start | bytes 3145736 | tf_op jit(solution)/shard_map/ppermute | solution.py:364
  233.1 71.2 %collective-permute-start.13 = (bf16[3,512,1024]{2,1,0:T(8,128)(2,1)}, bf16[3,512,1024]{2,1,0:T(8,128)(2,1)S(1)}, u32[]{:S(2)}, u32[]{:S(2)}) collective-permute-start(bf16[3,512,1024]{2,1,0:T(8,128)(2,1)} %get-tuple-element.36), channel_id=1, source_target_pairs={{0,2},{1,3},{2,0},{3,1},{4,6},{5,7},{6,4},{7,5},{8,10},{9,11},{10,... | collective-permute-start | bytes 9437192 | tf_op jit(solution)/shard_map/ppermute | solution.py:362
  234.8 136.9 %collective-permute-start.40 = (bf16[3,512,1024]{2,1,0:T(8,128)(2,1)S(1)}, bf16[3,512,1024]{2,1,0:T(8,128)(2,1)S(1)}, u32[]{:S(2)}, u32[]{:S(2)}) collective-permute-start(bf16[3,512,1024]{2,1,0:T(8,128)(2,1)S(1)} %get-tuple-element.47), channel_id=1, source_target_pairs={{0,2},{1,3},{2,0},{3,1},{4,6},{5,7},{6,4},{7,5},{8,10},{9,11},{10,... | collective-permute-start | bytes 9437192 | tf_op jit(solution)/shard_map/ppermute | solution.py:362
  237.1 134.6 %collective-permute-start.12 = (bf16[3,512,1024]{2,1,0:T(8,128)(2,1)}, bf16[3,512,1024]{2,1,0:T(8,128)(2,1)S(1)}, u32[]{:S(2)}, u32[]{:S(2)}) collective-permute-start(bf16[3,512,1024]{2,1,0:T(8,128)(2,1)} %get-tuple-element.36), channel_id=1, source_target_pairs={{0,1},{1,0},{2,3},{3,2},{4,5},{5,4},{6,7},{7,6},{8,9},{9,8},{10,11... | collective-permute-start | bytes 9437192 | tf_op jit(solution)/shard_map/ppermute | solution.py:360
  237.1 200.5 %collective-permute-start.37 = (bf16[3,512,1024]{2,1,0:T(8,128)(2,1)}, bf16[3,512,1024]{2,1,0:T(8,128)(2,1)}, u32[]{:S(2)}, u32[]{:S(2)}) collective-permute-start(bf16[3,512,1024]{2,1,0:T(8,128)(2,1)} %get-tuple-element.46), channel_id=1, source_target_pairs={{0,2},{1,3},{2,0},{3,1},{4,6},{5,7},{6,4},{7,5},{8,10},{9,11},{10,... | collective-permute-start | bytes 9437192 | tf_op jit(solution)/shard_map/ppermute | solution.py:362
  239.1 198.5 %collective-permute-start.39 = (bf16[3,512,1024]{2,1,0:T(8,128)(2,1)S(1)}, bf16[3,512,1024]{2,1,0:T(8,128)(2,1)S(1)}, u32[]{:S(2)}, u32[]{:S(2)}) collective-permute-start(bf16[3,512,1024]{2,1,0:T(8,128)(2,1)S(1)} %get-tuple-element.47), channel_id=1, source_target_pairs={{0,1},{1,0},{2,3},{3,2},{4,5},{5,4},{6,7},{7,6},{8,9},{9,8},{10,11... | collective-permute-start | bytes 9437192 | tf_op jit(solution)/shard_map/ppermute | solution.py:360
  304.3 142.3 %collective-permute-start.14 = (bf16[3,512,1024]{2,1,0:T(8,128)(2,1)S(1)}, bf16[3,512,1024]{2,1,0:T(8,128)(2,1)S(1)}, u32[]{:S(2)}, u32[]{:S(2)}) collective-permute-start(bf16[3,512,1024]{2,1,0:T(8,128)(2,1)S(1)} %collective-permute-done.13.refs_1_), channel_id=1, source_target_pairs={{0,1},{1,0},{2,3},{3,2},{4,5},{5,4},{6,7},{7,6},{8,9},{9,8},{10,11... | collective-permute-start | bytes 9437192 | tf_op jit(solution)/shard_map/ppermute | solution.py:364
  371.7 75.3 %collective-permute-start.41 = (bf16[3,512,1024]{2,1,0:T(8,128)(2,1)S(1)}, bf16[3,512,1024]{2,1,0:T(8,128)(2,1)S(1)}, u32[]{:S(2)}, u32[]{:S(2)}) collective-permute-start(bf16[3,512,1024]{2,1,0:T(8,128)(2,1)S(1)} %collective-permute-done.40.refs_1_), channel_id=1, source_target_pairs={{0,1},{1,0},{2,3},{3,2},{4,5},{5,4},{6,7},{7,6},{8,9},{9,8},{10,11... | collective-permute-start | bytes 9437192 | tf_op jit(solution)/shard_map/ppermute | solution.py:364
  371.7 148.6 %collective-permute-start.36 = (bf16[3,512,1024]{2,1,0:T(8,128)(2,1)}, bf16[3,512,1024]{2,1,0:T(8,128)(2,1)}, u32[]{:S(2)}, u32[]{:S(2)}) collective-permute-start(bf16[3,512,1024]{2,1,0:T(8,128)(2,1)} %get-tuple-element.46), channel_id=1, source_target_pairs={{0,1},{1,0},{2,3},{3,2},{4,5},{5,4},{6,7},{7,6},{8,9},{9,8},{10,11... | collective-permute-start | bytes 9437192 | tf_op jit(solution)/shard_map/ppermute | solution.py:360
  437.6 82.8 %collective-permute-start.38 = (bf16[3,512,1024]{2,1,0:T(8,128)(2,1)}, bf16[3,512,1024]{2,1,0:T(8,128)(2,1)}, u32[]{:S(2)}, u32[]{:S(2)}) collective-permute-start(bf16[3,512,1024]{2,1,0:T(8,128)(2,1)} %collective-permute-done.37.refs_1_), channel_id=1, source_target_pairs={{0,1},{1,0},{2,3},{3,2},{4,5},{5,4},{6,7},{7,6},{8,9},{9,8},{10,11... | collective-permute-start | bytes 9437192 | tf_op jit(solution)/shard_map/ppermute | solution.py:364
  439.3 7.2 %collective-permute-start.11 = (bf16[2,512,1024]{2,1,0:T(8,128)(2,1)S(1)}, bf16[2,512,1024]{2,1,0:T(8,128)(2,1)S(1)}, u32[]{:S(2)}, u32[]{:S(2)}) collective-permute-start(bf16[2,512,1024]{2,1,0:T(8,128)(2,1)S(1)} %collective-permute-done.10.refs_1_), channel_id=1, source_target_pairs={{0,1},{1,0},{2,3},{3,2},{4,5},{5,4},{6,7},{7,6},{8,9},{9,8},{10,11... | collective-permute-start | bytes 6291464 | tf_op jit(solution)/shard_map/ppermute | solution.py:364
  446.5 81.7 %collective-permute-start.33 = (bf16[1,512,1024]{2,1,0:T(8,128)(2,1)}, bf16[1,512,1024]{2,1,0:T(8,128)(2,1)}, u32[]{:S(2)}, u32[]{:S(2)}) collective-permute-start(bf16[1,512,1024]{2,1,0:T(8,128)(2,1)} %copy-done.46), channel_id=1, source_target_pairs={{0,1},{1,0},{2,3},{3,2},{4,5},{5,4},{6,7},{7,6},{8,9},{9,8},{10,11... | collective-permute-start | bytes 3145736 | tf_op jit(solution)/shard_map/ppermute | solution.py:360
  446.6 81.5 %collective-permute-start.35 = (bf16[1,512,1024]{2,1,0:T(8,128)(2,1)}, bf16[1,512,1024]{2,1,0:T(8,128)(2,1)}, u32[]{:S(2)}, u32[]{:S(2)}) collective-permute-start(bf16[1,512,1024]{2,1,0:T(8,128)(2,1)} %collective-permute-done.34.refs_1_), channel_id=1, source_target_pairs={{0,1},{1,0},{2,3},{3,2},{4,5},{5,4},{6,7},{7,6},{8,9},{9,8},{10,11... | collective-permute-start | bytes 3145736 | tf_op jit(solution)/shard_map/ppermute | solution.py:364
  447.0 86.8 %collective-permute-start.45 = (bf16[1,416,1024]{2,1,0:T(8,128)(2,1)}, bf16[1,416,1024]{2,1,0:T(8,128)(2,1)}, u32[]{:S(2)}, u32[]{:S(2)}) collective-permute-start(bf16[1,416,1024]{2,1,0:T(8,128)(2,1)} %collective-permute-done.44), channel_id=1, source_target_pairs={{0,1},{1,0},{2,3},{3,2},{4,5},{5,4},{6,7},{7,6},{8,9},{9,8},{10,11... | collective-permute-start | bytes 2555912 | tf_op jit(solution)/shard_map/ppermute | solution.py:364
  520.4 16.2 %collective-permute-start.47 = (bf16[1,96,1024]{2,1,0:T(8,128)(2,1)S(1)}, bf16[1,96,1024]{2,1,0:T(8,128)(2,1)S(1)}, u32[]{:S(2)}, u32[]{:S(2)}) collective-permute-start(bf16[1,96,1024]{2,1,0:T(8,128)(2,1)S(1)} %copy-done.54), channel_id=1, source_target_pairs={{0,1},{1,0},{2,3},{3,2},{4,5},{5,4},{6,7},{7,6},{8,9},{9,8},{10,11... | collective-permute-start | bytes 589832 | tf_op jit(solution)/shard_map/ppermute | solution.py:364
  (60 other events, 483.9 us)
